TPU v7x, 32 devices: a whole 2x2x4 slice. The times are simulated.
32 devices in a mesh: cp: 4 (over z), fsdp: 8 (over y, x, core).
Axes of the slice: x: 2, y: 2, z: 4, core: 2. Of those that a mesh axis runs over, the one named last changes fastest.
Arguments:
- tokens: int32 [256, 256], P('fsdp', 'cp')
- lengths: int32 [256], P('fsdp')
- embed_table: bfloat16 [33, 320], replicated
- layer_vecs: float32 [9, 320], P(None, 'fsdp')
- w_qkv: bfloat16 [320, 3, 20, 16], P('fsdp')
- w_out: bfloat16 [320, 320], P('fsdp')
- w_up: bfloat16 [320, 1280], P('fsdp')
- b_up: float32 [1280], P('fsdp')
- w_down: bfloat16 [1280, 320], P('fsdp')
- grad_out: bfloat16 [256, 256, 320], P('fsdp', 'cp')
Outputs:
- output 1: bfloat16 [256, 256, 320], P('fsdp', 'cp')
- output 2: float32 [33, 320], replicated
- output 3: float32 [9, 320], P(None, 'fsdp')
- output 4: float32 [320, 3, 20, 16], P('fsdp')
- output 5: float32 [320, 320], P('fsdp')
- output 6: float32 [320, 1280], P('fsdp')
- output 7: float32 [1280], P('fsdp')
- output 8: float32 [1280, 320], P('fsdp')
All inputs are finite; a program needn't handle non-finite values.
Results may differ from a plain program's by a relative error of at most 0.0103739.
Values are sent between devices in bfloat16 or wider.
A program may use at most 1 GiB of HBM per device.

v0:
```python
import jax
import jax.numpy as jnp
from jax import lax
from jax.sharding import PartitionSpec as P

MASK_ID = 32
LN_EPS = 1e-5
ROPE_BASE = 10000.0
TRAIN_RATIO = 0.15 * 0.8
NEG_BIG = -1e30


def layer_norm(z_in, ln_gain, ln_bias):
    row_mean = jnp.mean(z_in, axis=-1, keepdims=True)
    centered = z_in - row_mean
    row_var = jnp.mean(centered * centered, axis=-1, keepdims=True)
    return centered * lax.rsqrt(row_var + LN_EPS) * ln_gain + ln_bias


def gelu_exact(z_in):
    return jax.nn.gelu(z_in, approximate=False)


def rope_tables(positions, head_dim):
    inv_freq = 1.0 / (ROPE_BASE ** (jnp.arange(0, head_dim, 2, dtype=jnp.float32) / head_dim))
    angles = positions.astype(jnp.float32)[:, None] * inv_freq[None, :]
    return jnp.cos(angles)[:, None, :], jnp.sin(angles)[:, None, :]


def rotate(z_in, cos_t, sin_t):
    lower_half, upper_half = jnp.split(z_in, 2, axis=-1)
    return jnp.concatenate([lower_half * cos_t - upper_half * sin_t, upper_half * cos_t + lower_half * sin_t], axis=-1)


def reduce_grad(full_grad, axis_dim):
    return lax.psum(lax.psum_scatter(full_grad, 'fsdp', scatter_dimension=axis_dim, tiled=True), 'cp')


def solution(mesh):
    cp_size = mesh.shape['cp']
    send_pairs = [(dev_index, (dev_index + 1) % cp_size) for dev_index in range(cp_size)]

    def local_step(tokens, lengths, embed_table, layer_vecs, w_qkv, w_out, w_up, b_up, w_down, grad_out):
        vecs_all = lax.all_gather(layer_vecs, 'fsdp', axis=1, tiled=True)
        qkv_w = lax.all_gather(w_qkv, 'fsdp', axis=0, tiled=True)
        out_w = lax.all_gather(w_out, 'fsdp', axis=0, tiled=True)
        up_w = lax.all_gather(w_up, 'fsdp', axis=0, tiled=True)
        up_b = lax.all_gather(b_up, 'fsdp', axis=0, tiled=True)
        down_w = lax.all_gather(w_down, 'fsdp', axis=0, tiled=True)
        n_seq, seq_loc = tokens.shape
        vocab_size, model_dim = embed_table.shape
        n_heads, head_dim = qkv_w.shape[2], qkv_w.shape[3]
        cp_index = lax.axis_index('cp')
        positions = cp_index * seq_loc + jnp.arange(seq_loc)
        len_col = lengths[:, None]
        is_mask = tokens == MASK_ID
        tok_valid = positions[None, :] < len_col
        mask_count = lax.psum(jnp.sum(is_mask.astype(jnp.int32), axis=1), 'cp')
        drop_scale = (1.0 - TRAIN_RATIO) / (1.0 - mask_count.astype(jnp.float32) / lengths.astype(jnp.float32))
        keep_scale = jnp.where(is_mask | jnp.logical_not(tok_valid), 0.0, drop_scale[:, None])[:, :, None]
        one_hot = (tokens[:, :, None] == jnp.arange(vocab_size)).astype(jnp.bfloat16)
        embedded = jnp.einsum('bsv,vd->bsd', one_hot, embed_table, preferred_element_type=jnp.float32) * keep_scale
        norm_in32, ln1_pull = jax.vjp(layer_norm, embedded, vecs_all[0], vecs_all[1])
        norm_in = norm_in32.astype(jnp.bfloat16)
        qkv_lin = jnp.einsum('bsd,dthe->bsthe', norm_in, qkv_w, preferred_element_type=jnp.float32) + vecs_all[2:5].reshape(3, n_heads, head_dim)
        cos_t, sin_t = rope_tables(positions, head_dim)
        q_rot = rotate(qkv_lin[:, :, 0] * head_dim ** -0.5, cos_t, sin_t).astype(jnp.bfloat16)
        k_rot = rotate(qkv_lin[:, :, 1], cos_t, sin_t).astype(jnp.bfloat16)
        v_val = qkv_lin[:, :, 2].astype(jnp.bfloat16)

        def block_scores(k_blk, step):
            src_index = (cp_index - step) % cp_size
            key_pos = src_index * seq_loc + jnp.arange(seq_loc)
            key_ok = key_pos[None, :] < len_col
            raw_scores = jnp.einsum('bqhd,bkhd->bhqk', q_rot, k_blk, preferred_element_type=jnp.float32)
            return jnp.where(key_ok[:, None, None, :], raw_scores, NEG_BIG)

        def fwd_block(step, k_blk, v_blk, run_max, run_sum, acc_out):
            scores = block_scores(k_blk, step)
            new_max = jnp.maximum(run_max, jnp.max(scores, axis=-1))
            weights = jnp.exp(scores - new_max[..., None])
            rescale = jnp.exp(run_max - new_max)
            run_sum = run_sum * rescale + jnp.sum(weights, axis=-1)
            acc_out = acc_out * jnp.swapaxes(rescale, 1, 2)[..., None] + jnp.einsum('bhqk,bkhd->bqhd', weights.astype(jnp.bfloat16), v_blk, preferred_element_type=jnp.float32)
            return new_max, run_sum, acc_out

        def fwd_body(step, carry):
            k_blk, v_blk, run_max, run_sum, acc_out = carry
            run_max, run_sum, acc_out = fwd_block(step, k_blk, v_blk, run_max, run_sum, acc_out)
            return (lax.ppermute(k_blk, 'cp', send_pairs), lax.ppermute(v_blk, 'cp', send_pairs), run_max, run_sum, acc_out)

        stat_shape = (n_seq, n_heads, seq_loc)
        carry = (k_rot, v_val, jnp.full(stat_shape, NEG_BIG, jnp.float32), jnp.zeros(stat_shape, jnp.float32), jnp.zeros(q_rot.shape, jnp.float32))
        carry = lax.fori_loop(0, cp_size - 1, fwd_body, carry)
        run_max, run_sum, acc_out = fwd_block(cp_size - 1, carry[0], carry[1], carry[2], carry[3], carry[4])
        log_sum = run_max + jnp.log(run_sum)
        attn32 = acc_out / jnp.swapaxes(run_sum, 1, 2)[..., None]
        attn_out = attn32.astype(jnp.bfloat16).reshape(n_seq, seq_loc, model_dim)
        resid_mid = embedded + jnp.einsum('bsd,de->bse', attn_out, out_w, preferred_element_type=jnp.float32) + vecs_all[5]
        norm_mid32, ln2_pull = jax.vjp(layer_norm, resid_mid, vecs_all[6], vecs_all[7])
        norm_mid = norm_mid32.astype(jnp.bfloat16)
        up_lin = jnp.einsum('bsd,df->bsf', norm_mid, up_w, preferred_element_type=jnp.float32) + up_b
        gelu32, gelu_pull = jax.vjp(gelu_exact, up_lin)
        gelu_out = gelu32.astype(jnp.bfloat16)
        layer_out = (resid_mid + jnp.einsum('bsf,fd->bsd', gelu_out, down_w, preferred_element_type=jnp.float32) + vecs_all[8]).astype(jnp.bfloat16)

        grad32 = grad_out.astype(jnp.float32)
        d_down = jnp.einsum('bsf,bsd->fd', gelu_out, grad_out, preferred_element_type=jnp.float32)
        d_gelu = jnp.einsum('bsd,fd->bsf', grad_out, down_w, preferred_element_type=jnp.float32)
        d_up_lin = gelu_pull(d_gelu)[0]
        d_up_b = d_up_lin.astype(jnp.bfloat16)
        d_up = jnp.einsum('bsd,bsf->df', norm_mid, d_up_b, preferred_element_type=jnp.float32)
        d_norm_mid = jnp.einsum('bsf,df->bsd', d_up_b, up_w, preferred_element_type=jnp.float32)
        d_resid_ln, d_gain2, d_bias2 = ln2_pull(d_norm_mid)
        d_resid = grad32 + d_resid_ln
        d_resid_b = d_resid.astype(jnp.bfloat16)
        d_outw = jnp.einsum('bsd,bse->de', attn_out, d_resid_b, preferred_element_type=jnp.float32)
        d_attn = jnp.einsum('bse,de->bsd', d_resid_b, out_w, preferred_element_type=jnp.float32).reshape(n_seq, seq_loc, n_heads, head_dim)
        d_attn_b = d_attn.astype(jnp.bfloat16)
        delta = jnp.swapaxes(jnp.sum(d_attn * attn32, axis=-1), 1, 2)

        def bwd_block(step, k_blk, v_blk, d_query):
            scores = block_scores(k_blk, step)
            weights = jnp.exp(scores - log_sum[..., None])
            d_weights = jnp.einsum('bqhd,bkhd->bhqk', d_attn_b, v_blk, preferred_element_type=jnp.float32)
            d_scores = (weights * (d_weights - delta[..., None])).astype(jnp.bfloat16)
            d_query = d_query + jnp.einsum('bhqk,bkhd->bqhd', d_scores, k_blk, preferred_element_type=jnp.float32)
            d_key = jnp.einsum('bhqk,bqhd->bkhd', d_scores, q_rot, preferred_element_type=jnp.float32)
            d_value = jnp.einsum('bhqk,bqhd->bkhd', weights.astype(jnp.bfloat16), d_attn_b, preferred_element_type=jnp.float32)
            return d_query, d_key, d_value

        def bwd_body(step, carry):
            k_blk, v_blk, dk_blk, dv_blk, d_query = carry
            d_query, d_key, d_value = bwd_block(step, k_blk, v_blk, d_query)
            return (lax.ppermute(k_blk, 'cp', send_pairs), lax.ppermute(v_blk, 'cp', send_pairs), lax.ppermute(dk_blk + d_key, 'cp', send_pairs), lax.ppermute(dv_blk + d_value, 'cp', send_pairs), d_query)

        kv_zero = jnp.zeros(q_rot.shape, jnp.float32)
        carry = (k_rot, v_val, kv_zero, kv_zero, kv_zero)
        carry = lax.fori_loop(0, cp_size - 1, bwd_body, carry)
        d_query, d_key, d_value = bwd_block(cp_size - 1, carry[0], carry[1], carry[4])
        d_key = lax.ppermute(carry[2] + d_key, 'cp', send_pairs)
        d_value = lax.ppermute(carry[3] + d_value, 'cp', send_pairs)

        d_q_lin = rotate(d_query, cos_t, -sin_t) * head_dim ** -0.5
        d_k_lin = rotate(d_key, cos_t, -sin_t)
        d_qkv_lin = jnp.stack([d_q_lin, d_k_lin, d_value], axis=2)
        d_qkv_b = d_qkv_lin.astype(jnp.bfloat16)
        d_qkvw = jnp.einsum('bsd,bsthe->dthe', norm_in, d_qkv_b, preferred_element_type=jnp.float32)
        d_norm_in = jnp.einsum('bsthe,dthe->bsd', d_qkv_b, qkv_w, preferred_element_type=jnp.float32)
        d_embedded, d_gain1, d_bias1 = ln1_pull(d_norm_in)
        d_embedded = d_embedded + d_resid
        d_table = jnp.einsum('bsv,bsd->vd', one_hot, (d_embedded * keep_scale).astype(jnp.bfloat16), preferred_element_type=jnp.float32)
        d_bqkv = jnp.sum(d_qkv_lin, axis=(0, 1)).reshape(3, model_dim)
        d_tail = jnp.stack([jnp.sum(d_resid, axis=(0, 1)), d_gain2, d_bias2, jnp.sum(grad32, axis=(0, 1))])
        d_vecs_full = jnp.concatenate([jnp.stack([d_gain1, d_bias1]), d_bqkv, d_tail], axis=0)
        return (layer_out, lax.psum(d_table, ('cp', 'fsdp')), reduce_grad(d_vecs_full, 1), reduce_grad(d_qkvw, 0), reduce_grad(d_outw, 0), reduce_grad(d_up, 0), reduce_grad(jnp.sum(d_up_lin, axis=(0, 1)), 0), reduce_grad(d_down, 0))

    in_specs = (P('fsdp', 'cp'), P('fsdp'), P(), P(None, 'fsdp'), P('fsdp', None, None, None), P('fsdp', None), P('fsdp', None), P('fsdp'), P('fsdp', None), P('fsdp', 'cp', None))
    out_specs = (P('fsdp', 'cp', None), P(), P(None, 'fsdp'), P('fsdp', None, None, None), P('fsdp', None), P('fsdp', None), P('fsdp'), P('fsdp', None))
    return jax.shard_map(local_step, mesh=mesh, in_specs=in_specs, out_specs=out_specs, check_vma=False)
```

profile of v0, /device:TPU:0, one launch (start us, length us, event | category | flops | bytes accessed | tf_op | source)
XLA Modules:
  0.0 2243.1 jit_solution(14187286872934897314)
XLA Ops:
  7.3 10.8 all-gather
  35.7 21.2 all_gather.19
  78.5 10.7 fusion.42
  91.6 14.0 all-reduce
  156.1 359.9 %while.48 = (s32[]{:T(128)}, bf16[32,64,20,16]{1,3,2,0:T(8,128)(2,1)}, bf16[32,64,20,16]{1,3,2,0:T(8,128)(2,1)}, f32[32,20,64]{2,1,0:T(8,128)S(1)}, f32[32,20,64...) while((s32[]{:T(128)}, ...), condition=%wide.region_7.8_spmd.clone, body=%wide.region_4.7_spmd.clone.sunk | while | flops 190957648 | bytes 85206064 | solution.py:94
  165.1 11.5 select_reduce_fusion.3
  176.7 11.8 fusion.158
  198.9 22.4 collective-permute-done
  221.3 56.0 %collective-permute-done.1 = bf16[32,64,20,16]{1,3,2,0:T(8,128)(2,1)} collective-permute-done((bf16[32,64,20,16]{1,3,2,0:T(8,128)(2,1)}, bf16[32,64,20,16]{1,3,2,0:T(8,128)(2,1)}, u32[]{:S(2)}, u32[]{:S(2)}) %collective-permute-start.1) | collective-permute-done | bytes 1310752 | tf_op jit(solution)/shard_map/while/body/eval_jaxpr/ppermute | solution.py:90
  284.7 11.5 select_reduce_fusion.3
  296.4 11.8 fusion.158
  318.5 23.9 %collective-permute-done = bf16[32,64,20,16]{1,3,2,0:T(8,128)(2,1)} collective-permute-done((bf16[32,64,20,16]{1,3,2,0:T(8,128)(2,1)}, bf16[32,64,20,16]{1,3,2,0:T(8,128)(2,1)}, u32[]{:S(2)}, u32[]{:S(2)}) %collective-permute-start) | collective-permute-done | bytes 1310752 | tf_op jit(solution)/shard_map/while/body/eval_jaxpr/ppermute | solution.py:90
  342.5 54.8 %collective-permute-done.1 = bf16[32,64,20,16]{1,3,2,0:T(8,128)(2,1)} collective-permute-done((bf16[32,64,20,16]{1,3,2,0:T(8,128)(2,1)}, bf16[32,64,20,16]{1,3,2,0:T(8,128)(2,1)}, u32[]{:S(2)}, u32[]{:S(2)}) %collective-permute-start.1) | collective-permute-done | bytes 1310752 | tf_op jit(solution)/shard_map/while/body/eval_jaxpr/ppermute | solution.py:90
  404.7 11.5 select_reduce_fusion.3
  416.3 11.8 fusion.158
  438.5 24.0 %collective-permute-done = bf16[32,64,20,16]{1,3,2,0:T(8,128)(2,1)} collective-permute-done((bf16[32,64,20,16]{1,3,2,0:T(8,128)(2,1)}, bf16[32,64,20,16]{1,3,2,0:T(8,128)(2,1)}, u32[]{:S(2)}, u32[]{:S(2)}) %collective-permute-start) | collective-permute-done | bytes 1310752 | tf_op jit(solution)/shard_map/while/body/eval_jaxpr/ppermute | solution.py:90
  462.4 53.6 %collective-permute-done.1 = bf16[32,64,20,16]{1,3,2,0:T(8,128)(2,1)} collective-permute-done((bf16[32,64,20,16]{1,3,2,0:T(8,128)(2,1)}, bf16[32,64,20,16]{1,3,2,0:T(8,128)(2,1)}, u32[]{:S(2)}, u32[]{:S(2)}) %collective-permute-start.1) | collective-permute-done | bytes 1310752 | tf_op jit(solution)/shard_map/while/body/eval_jaxpr/ppermute | solution.py:90
  516.0 11.7 select_reduce_fusion.1
  527.8 11.6 fusion.21
  539.7 15.4 fusion.95
  565.3 25.0 %multiply_convert_fusion.2 = (bf16[32,64,1280]{2,1,0:T(8,128)(2,1)}, f32[32,64,1280]{2,1,0:T(8,128)}) fusion(f32[32,64,1280]{2,1,0:T(8,128)S(1)} %get-tuple-element.801, f32[1280]{0:T(1024)S(1)} %copy-done.46, u32[64,1280]{1,0:T(8,128)S(1)} %get-tuple-element.691, u32[64,1280]{1,0:T(8,128)S(1)} %get-tuple-element.690), kind=kLoop, calls=%fused_computation.52 | loop fusion | flops 180879360 | bytes 26874880 | tf_op jit(solution)/shard_map/convert_element_type | solution.py:104
  590.2 11.0 fusion.97
  627.6 1139.5 %while.49 = (s32[]{:T(128)}, bf16[32,64,20,16]{1,3,2,0:T(8,128)(2,1)}, bf16[32,64,20,16]{1,3,2,0:T(8,128)(2,1)}, f32[32,64,20,16]{1,3,2,0:T(8,128)}, f32[32,64,2...) while((s32[]{:T(128)}, ...), condition=%wide.region_16.17_spmd.clone, body=%wide.region_15.16_spmd.clone.sunk | while | flops 443025472 | bytes 125017240 | solution.py:139
  641.2 17.3 multiply_convert_fusion.8
  658.5 11.6 bitcast_add_fusion.13
  685.4 12.7 bitcast_add_fusion.15
  698.1 258.2 %collective-permute-done.3 = bf16[32,64,20,16]{1,3,2,0:T(8,128)(2,1)} collective-permute-done((bf16[32,64,20,16]{1,3,2,0:T(8,128)(2,1)}, bf16[32,64,20,16]{1,3,2,0:T(8,128)(2,1)}, u32[]{:S(2)}, u32[]{:S(2)}) %collective-permute-start.3) | collective-permute-done | bytes 1310752 | tf_op jit(solution)/shard_map/while/body/eval_jaxpr/ppermute | solution.py:135
  956.3 52.4 %collective-permute-done.2 = bf16[32,64,20,16]{1,3,2,0:T(8,128)(2,1)} collective-permute-done((bf16[32,64,20,16]{1,3,2,0:T(8,128)(2,1)}, bf16[32,64,20,16]{1,3,2,0:T(8,128)(2,1)}, u32[]{:S(2)}, u32[]{:S(2)}) %collective-permute-start.2) | collective-permute-done | bytes 1310752 | tf_op jit(solution)/shard_map/while/body/eval_jaxpr/ppermute | solution.py:135
  1022.2 17.3 multiply_convert_fusion.8
  1039.5 11.6 bitcast_add_fusion.13
  1066.4 14.2 bitcast_add_fusion.15
  1080.6 256.7 %collective-permute-done.3 = bf16[32,64,20,16]{1,3,2,0:T(8,128)(2,1)} collective-permute-done((bf16[32,64,20,16]{1,3,2,0:T(8,128)(2,1)}, bf16[32,64,20,16]{1,3,2,0:T(8,128)(2,1)}, u32[]{:S(2)}, u32[]{:S(2)}) %collective-permute-start.3) | collective-permute-done | bytes 1310752 | tf_op jit(solution)/shard_map/while/body/eval_jaxpr/ppermute | solution.py:135
  1337.3 51.2 %collective-permute-done.2 = bf16[32,64,20,16]{1,3,2,0:T(8,128)(2,1)} collective-permute-done((bf16[32,64,20,16]{1,3,2,0:T(8,128)(2,1)}, bf16[32,64,20,16]{1,3,2,0:T(8,128)(2,1)}, u32[]{:S(2)}, u32[]{:S(2)}) %collective-permute-start.2) | collective-permute-done | bytes 1310752 | tf_op jit(solution)/shard_map/while/body/eval_jaxpr/ppermute | solution.py:135
  1401.9 17.3 multiply_convert_fusion.8
  1419.2 11.6 bitcast_add_fusion.13
  1446.1 14.2 bitcast_add_fusion.15
  1460.4 256.7 %collective-permute-done.3 = bf16[32,64,20,16]{1,3,2,0:T(8,128)(2,1)} collective-permute-done((bf16[32,64,20,16]{1,3,2,0:T(8,128)(2,1)}, bf16[32,64,20,16]{1,3,2,0:T(8,128)(2,1)}, u32[]{:S(2)}, u32[]{:S(2)}) %collective-permute-start.3) | collective-permute-done | bytes 1310752 | tf_op jit(solution)/shard_map/while/body/eval_jaxpr/ppermute | solution.py:135
  1717.0 50.0 %collective-permute-done.2 = bf16[32,64,20,16]{1,3,2,0:T(8,128)(2,1)} collective-permute-done((bf16[32,64,20,16]{1,3,2,0:T(8,128)(2,1)}, bf16[32,64,20,16]{1,3,2,0:T(8,128)(2,1)}, u32[]{:S(2)}, u32[]{:S(2)}) %collective-permute-start.2) | collective-permute-done | bytes 1310752 | tf_op jit(solution)/shard_map/while/body/eval_jaxpr/ppermute | solution.py:135
  1777.0 16.2 multiply_convert_fusion.1
  1793.2 10.4 bitcast_add_fusion.6
  1803.6 14.1 bitcast_add_fusion.5
  1831.4 89.9 %collective-permute-done.6 = f32[32,64,20,16]{1,3,2,0:T(8,128)S(1)} collective-permute-done((f32[32,64,20,16]{1,3,2,0:T(8,128)}, f32[32,64,20,16]{1,3,2,0:T(8,128)S(1)}, u32[]{:S(2)}, u32[]{:S(2)}) %collective-permute-start.6) | collective-permute-done | bytes 2621472 | tf_op jit(solution)/shard_map/ppermute | solution.py:141
  1932.3 94.0 %collective-permute-done.7 = f32[32,64,20,16]{1,3,2,0:T(8,128)} collective-permute-done((f32[32,64,20,16]{1,3,2,0:T(8,128)}, f32[32,64,20,16]{1,3,2,0:T(8,128)}, u32[]{:S(2)}, u32[]{:S(2)}) %collective-permute-start.7) | collective-permute-done | bytes 2621472 | tf_op jit(solution)/shard_map/ppermute | solution.py:142
  2080.1 17.1 bitcast_reduce_fusion
  2109.9 22.7 %all-reduce.4 = (f32[9,320]{1,0:T(8,128)S(1)}, f32[1280]{0:T(1024)S(1)}) all-reduce(f32[9,320]{1,0:T(8,128)S(1)} %concatenate.34, f32[1280]{0:T(1024)S(1)} %copy-done.54), channel_id=2, replica_groups=mesh['cp'=4,'fsdp'=8] {'fsdp'}, use_global_device_ids=true, to_apply=%region_27.28.clone | all-reduce | flops 4160 | bytes 33280
  2132.7 18.0 all-reduce.5
  2155.7 20.3 reduce-scatter.10.cloned.1.call-done
  2181.1 41.1 %psum.57 = f32[33,320]{1,0:T(8,128)} all-reduce(f32[33,320]{1,0:T(8,128)S(1)} %fusion.64), channel_id=1, replica_groups=mesh['cp'=4,'fsdp'=8] {'cp','fsdp'}, use_global_device_ids=true, to_apply=%region_19.20 | all-reduce | flops 10560 | bytes 84480 | tf_op jit(solution)/shard_map/psum | solution.py:156
  (344 shorter events, 392.5 us)
Async XLA Ops:
  7.2 2125.6 %reduce-scatter.16.cloned.1.call-start = ((), (), s32[]{:S(2)}) async-start(), calls=%async_computation.7 | async-start | bytes 552960
  78.5 47.2 %copy-start.32 = (bf16[160,320]{1,0:T(8,128)(2,1)S(1)}, bf16[160,320]{1,0:T(8,128)(2,1)}, u32[]{:S(2)}) copy-start(bf16[160,320]{1,0:T(8,128)(2,1)} %param.22) | copy-start | bytes 307204
  156.1 359.9 %copy-start.34 = (pred[32,64]{1,0:T(8,128)(4,1)S(1)}, pred[32,64]{1,0:T(8,128)(4,1)}, u32[]{:S(2)}) copy-start(pred[32,64]{1,0:T(8,128)(4,1)} %broadcast_compare_fusion.2) | copy-start | bytes 6148
  159.7 61.5 %collective-permute-start = (bf16[32,64,20,16]{1,3,2,0:T(8,128)(2,1)}, bf16[32,64,20,16]{1,3,2,0:T(8,128)(2,1)}, u32[]{:S(2)}, u32[]{:S(2)}) collective-permute-start(bf16[32,64,20,16]{1,3,2,0:T(8,128)(2,1)} %copy.169), channel_id=1, source_target_pairs={{0,8},{8,16},{16,24},{24,0},{1,9},{9,17},{17,25},{25,1},{2,10},{10... | collective-permute-start | bytes 3932168 | tf_op jit(solution)/shard_map/while/body/eval_jaxpr/ppermute | solution.py:90
  165.0 112.2 %collective-permute-start.1 = (bf16[32,64,20,16]{1,3,2,0:T(8,128)(2,1)}, bf16[32,64,20,16]{1,3,2,0:T(8,128)(2,1)}, u32[]{:S(2)}, u32[]{:S(2)}) collective-permute-start(bf16[32,64,20,16]{1,3,2,0:T(8,128)(2,1)} %copy.170), channel_id=1, source_target_pairs={{0,8},{8,16},{16,24},{24,0},{1,9},{9,17},{17,25},{25,1},{2,10},{10... | collective-permute-start | bytes 3932168 | tf_op jit(solution)/shard_map/while/body/eval_jaxpr/ppermute | solution.py:90
  198.9 78.4 %copy-start.5 = (f32[32,64,20,16]{1,3,2,0:T(8,128)}, f32[32,64,20,16]{1,3,2,0:T(8,128)S(1)}, u32[]{:S(2)}) copy-start(f32[32,64,20,16]{1,3,2,0:T(8,128)S(1)} %bitcast_add_fusion.12) | copy-start | bytes 7864324 | tf_op jit(solution)/shard_map/while
  280.9 61.5 %collective-permute-start = (bf16[32,64,20,16]{1,3,2,0:T(8,128)(2,1)}, bf16[32,64,20,16]{1,3,2,0:T(8,128)(2,1)}, u32[]{:S(2)}, u32[]{:S(2)}) collective-permute-start(bf16[32,64,20,16]{1,3,2,0:T(8,128)(2,1)} %copy.169), channel_id=1, source_target_pairs={{0,8},{8,16},{16,24},{24,0},{1,9},{9,17},{17,25},{25,1},{2,10},{10... | collective-permute-start | bytes 3932168 | tf_op jit(solution)/shard_map/while/body/eval_jaxpr/ppermute | solution.py:90
  284.6 112.6 %collective-permute-start.1 = (bf16[32,64,20,16]{1,3,2,0:T(8,128)(2,1)}, bf16[32,64,20,16]{1,3,2,0:T(8,128)(2,1)}, u32[]{:S(2)}, u32[]{:S(2)}) collective-permute-start(bf16[32,64,20,16]{1,3,2,0:T(8,128)(2,1)} %copy.170), channel_id=1, source_target_pairs={{0,8},{8,16},{16,24},{24,0},{1,9},{9,17},{17,25},{25,1},{2,10},{10... | collective-permute-start | bytes 3932168 | tf_op jit(solution)/shard_map/while/body/eval_jaxpr/ppermute | solution.py:90
  318.5 78.7 %copy-start.5 = (f32[32,64,20,16]{1,3,2,0:T(8,128)}, f32[32,64,20,16]{1,3,2,0:T(8,128)S(1)}, u32[]{:S(2)}) copy-start(f32[32,64,20,16]{1,3,2,0:T(8,128)S(1)} %bitcast_add_fusion.12) | copy-start | bytes 7864324 | tf_op jit(solution)/shard_map/while
  400.9 61.5 %collective-permute-start = (bf16[32,64,20,16]{1,3,2,0:T(8,128)(2,1)}, bf16[32,64,20,16]{1,3,2,0:T(8,128)(2,1)}, u32[]{:S(2)}, u32[]{:S(2)}) collective-permute-start(bf16[32,64,20,16]{1,3,2,0:T(8,128)(2,1)} %copy.169), channel_id=1, source_target_pairs={{0,8},{8,16},{16,24},{24,0},{1,9},{9,17},{17,25},{25,1},{2,10},{10... | collective-permute-start | bytes 3932168 | tf_op jit(solution)/shard_map/while/body/eval_jaxpr/ppermute | solution.py:90
  404.6 111.4 %collective-permute-start.1 = (bf16[32,64,20,16]{1,3,2,0:T(8,128)(2,1)}, bf16[32,64,20,16]{1,3,2,0:T(8,128)(2,1)}, u32[]{:S(2)}, u32[]{:S(2)}) collective-permute-start(bf16[32,64,20,16]{1,3,2,0:T(8,128)(2,1)} %copy.170), channel_id=1, source_target_pairs={{0,8},{8,16},{16,24},{24,0},{1,9},{9,17},{17,25},{25,1},{2,10},{10... | collective-permute-start | bytes 3932168 | tf_op jit(solution)/shard_map/while/body/eval_jaxpr/ppermute | solution.py:90
  438.5 77.5 %copy-start.5 = (f32[32,64,20,16]{1,3,2,0:T(8,128)}, f32[32,64,20,16]{1,3,2,0:T(8,128)S(1)}, u32[]{:S(2)}) copy-start(f32[32,64,20,16]{1,3,2,0:T(8,128)S(1)} %bitcast_add_fusion.12) | copy-start | bytes 7864324 | tf_op jit(solution)/shard_map/while
  558.7 48.8 %copy-start.9 = (f32[32,64,320]{2,1,0:T(8,128)}, f32[32,64,320]{2,1,0:T(8,128)S(1)}, u32[]{:S(2)}) copy-start(f32[32,64,320]{2,1,0:T(8,128)S(1)} %get-tuple-element.800) | copy-start | bytes 7864324
  558.7 48.8 %copy-start.28 = (f32[32,64]{1,0:T(8,128)}, f32[32,64]{1,0:T(8,128)S(1)}, u32[]{:S(2)}) copy-start(f32[32,64]{1,0:T(8,128)S(1)} %broadcast_multiply_fusion) | copy-start | bytes 24580
  559.5 48.1 %copy-start.42 = (f32[32,64]{1,0:T(8,128)}, f32[32,64]{1,0:T(8,128)S(1)}, u32[]{:S(2)}) copy-start(f32[32,64]{1,0:T(8,128)S(1)} %fusion.83) | copy-start | bytes 24580
  614.7 1536.1 %reduce-scatter.14.cloned.1.call-start = ((), (), s32[]{:S(2)}) async-start(), calls=%async_computation.6 | async-start | bytes 1474560
  670.1 338.6 %collective-permute-start.4 = (f32[32,64,20,16]{1,3,2,0:T(8,128)}, f32[32,64,20,16]{1,3,2,0:T(8,128)}, u32[]{:S(2)}, u32[]{:S(2)}) collective-permute-start(f32[32,64,20,16]{1,3,2,0:T(8,128)} %bitcast_add_fusion.13), channel_id=1, source_target_pairs={{0,8},{8,16},{16,24},{24,0},{1,9},{9,17},{17,25},{25,1},{2,10},{10... | collective-permute-start | bytes 7864328 | tf_op jit(solution)/shard_map/while/body/eval_jaxpr/ppermute | solution.py:135
  680.5 328.2 %collective-permute-start.5 = (f32[32,64,20,16]{1,3,2,0:T(8,128)}, f32[32,64,20,16]{1,3,2,0:T(8,128)}, u32[]{:S(2)}, u32[]{:S(2)}) collective-permute-start(f32[32,64,20,16]{1,3,2,0:T(8,128)} %bitcast_add_fusion.14), channel_id=1, source_target_pairs={{0,8},{8,16},{16,24},{24,0},{1,9},{9,17},{17,25},{25,1},{2,10},{10... | collective-permute-start | bytes 7864328 | tf_op jit(solution)/shard_map/while/body/eval_jaxpr/ppermute | solution.py:135
  680.5 275.9 %collective-permute-start.3 = (bf16[32,64,20,16]{1,3,2,0:T(8,128)(2,1)}, bf16[32,64,20,16]{1,3,2,0:T(8,128)(2,1)}, u32[]{:S(2)}, u32[]{:S(2)}) collective-permute-start(bf16[32,64,20,16]{1,3,2,0:T(8,128)(2,1)} %copy.189), channel_id=1, source_target_pairs={{0,8},{8,16},{16,24},{24,0},{1,9},{9,17},{17,25},{25,1},{2,10},{10... | collective-permute-start | bytes 3932168 | tf_op jit(solution)/shard_map/while/body/eval_jaxpr/ppermute | solution.py:135
  681.1 327.6 %collective-permute-start.2 = (bf16[32,64,20,16]{1,3,2,0:T(8,128)(2,1)}, bf16[32,64,20,16]{1,3,2,0:T(8,128)(2,1)}, u32[]{:S(2)}, u32[]{:S(2)}) collective-permute-start(bf16[32,64,20,16]{1,3,2,0:T(8,128)(2,1)} %copy.188), channel_id=1, source_target_pairs={{0,8},{8,16},{16,24},{24,0},{1,9},{9,17},{17,25},{25,1},{2,10},{10... | collective-permute-start | bytes 3932168 | tf_op jit(solution)/shard_map/while/body/eval_jaxpr/ppermute | solution.py:135
  685.4 323.3 %copy-start.3 = (bf16[32,64,20,16]{1,3,2,0:T(8,128)(2,1)S(1)}, bf16[32,64,20,16]{1,3,2,0:T(8,128)(2,1)}, u32[]{:S(2)}) copy-start(bf16[32,64,20,16]{1,3,2,0:T(8,128)(2,1)} %copy-done.2) | copy-start | bytes 3932164 | tf_op jit(solution)/shard_map/while
  1051.0 337.4 %collective-permute-start.4 = (f32[32,64,20,16]{1,3,2,0:T(8,128)}, f32[32,64,20,16]{1,3,2,0:T(8,128)}, u32[]{:S(2)}, u32[]{:S(2)}) collective-permute-start(f32[32,64,20,16]{1,3,2,0:T(8,128)} %bitcast_add_fusion.13), channel_id=1, source_target_pairs={{0,8},{8,16},{16,24},{24,0},{1,9},{9,17},{17,25},{25,1},{2,10},{10... | collective-permute-start | bytes 7864328 | tf_op jit(solution)/shard_map/while/body/eval_jaxpr/ppermute | solution.py:135
  1061.4 327.0 %collective-permute-start.5 = (f32[32,64,20,16]{1,3,2,0:T(8,128)}, f32[32,64,20,16]{1,3,2,0:T(8,128)}, u32[]{:S(2)}, u32[]{:S(2)}) collective-permute-start(f32[32,64,20,16]{1,3,2,0:T(8,128)} %bitcast_add_fusion.14), channel_id=1, source_target_pairs={{0,8},{8,16},{16,24},{24,0},{1,9},{9,17},{17,25},{25,1},{2,10},{10... | collective-permute-start | bytes 7864328 | tf_op jit(solution)/shard_map/while/body/eval_jaxpr/ppermute | solution.py:135
  1061.4 275.9 %collective-permute-start.3 = (bf16[32,64,20,16]{1,3,2,0:T(8,128)(2,1)}, bf16[32,64,20,16]{1,3,2,0:T(8,128)(2,1)}, u32[]{:S(2)}, u32[]{:S(2)}) collective-permute-start(bf16[32,64,20,16]{1,3,2,0:T(8,128)(2,1)} %copy.189), channel_id=1, source_target_pairs={{0,8},{8,16},{16,24},{24,0},{1,9},{9,17},{17,25},{25,1},{2,10},{10... | collective-permute-start | bytes 3932168 | tf_op jit(solution)/shard_map/while/body/eval_jaxpr/ppermute | solution.py:135
  1062.1 326.4 %collective-permute-start.2 = (bf16[32,64,20,16]{1,3,2,0:T(8,128)(2,1)}, bf16[32,64,20,16]{1,3,2,0:T(8,128)(2,1)}, u32[]{:S(2)}, u32[]{:S(2)}) collective-permute-start(bf16[32,64,20,16]{1,3,2,0:T(8,128)(2,1)} %copy.188), channel_id=1, source_target_pairs={{0,8},{8,16},{16,24},{24,0},{1,9},{9,17},{17,25},{25,1},{2,10},{10... | collective-permute-start | bytes 3932168 | tf_op jit(solution)/shard_map/while/body/eval_jaxpr/ppermute | solution.py:135
  1066.4 322.1 %copy-start.3 = (bf16[32,64,20,16]{1,3,2,0:T(8,128)(2,1)S(1)}, bf16[32,64,20,16]{1,3,2,0:T(8,128)(2,1)}, u32[]{:S(2)}) copy-start(bf16[32,64,20,16]{1,3,2,0:T(8,128)(2,1)} %copy-done.2) | copy-start | bytes 3932164 | tf_op jit(solution)/shard_map/while
  1430.8 336.2 %collective-permute-start.4 = (f32[32,64,20,16]{1,3,2,0:T(8,128)}, f32[32,64,20,16]{1,3,2,0:T(8,128)}, u32[]{:S(2)}, u32[]{:S(2)}) collective-permute-start(f32[32,64,20,16]{1,3,2,0:T(8,128)} %bitcast_add_fusion.13), channel_id=1, source_target_pairs={{0,8},{8,16},{16,24},{24,0},{1,9},{9,17},{17,25},{25,1},{2,10},{10... | collective-permute-start | bytes 7864328 | tf_op jit(solution)/shard_map/while/body/eval_jaxpr/ppermute | solution.py:135
  1441.2 325.8 %collective-permute-start.5 = (f32[32,64,20,16]{1,3,2,0:T(8,128)}, f32[32,64,20,16]{1,3,2,0:T(8,128)}, u32[]{:S(2)}, u32[]{:S(2)}) collective-permute-start(f32[32,64,20,16]{1,3,2,0:T(8,128)} %bitcast_add_fusion.14), channel_id=1, source_target_pairs={{0,8},{8,16},{16,24},{24,0},{1,9},{9,17},{17,25},{25,1},{2,10},{10... | collective-permute-start | bytes 7864328 | tf_op jit(solution)/shard_map/while/body/eval_jaxpr/ppermute | solution.py:135
  1441.2 275.9 %collective-permute-start.3 = (bf16[32,64,20,16]{1,3,2,0:T(8,128)(2,1)}, bf16[32,64,20,16]{1,3,2,0:T(8,128)(2,1)}, u32[]{:S(2)}, u32[]{:S(2)}) collective-permute-start(bf16[32,64,20,16]{1,3,2,0:T(8,128)(2,1)} %copy.189), channel_id=1, source_target_pairs={{0,8},{8,16},{16,24},{24,0},{1,9},{9,17},{17,25},{25,1},{2,10},{10... | collective-permute-start | bytes 3932168 | tf_op jit(solution)/shard_map/while/body/eval_jaxpr/ppermute | solution.py:135
  1441.8 325.2 %collective-permute-start.2 = (bf16[32,64,20,16]{1,3,2,0:T(8,128)(2,1)}, bf16[32,64,20,16]{1,3,2,0:T(8,128)(2,1)}, u32[]{:S(2)}, u32[]{:S(2)}) collective-permute-start(bf16[32,64,20,16]{1,3,2,0:T(8,128)(2,1)} %copy.188), channel_id=1, source_target_pairs={{0,8},{8,16},{16,24},{24,0},{1,9},{9,17},{17,25},{25,1},{2,10},{10... | collective-permute-start | bytes 3932168 | tf_op jit(solution)/shard_map/while/body/eval_jaxpr/ppermute | solution.py:135
  1446.1 320.9 %copy-start.3 = (bf16[32,64,20,16]{1,3,2,0:T(8,128)(2,1)S(1)}, bf16[32,64,20,16]{1,3,2,0:T(8,128)(2,1)}, u32[]{:S(2)}) copy-start(bf16[32,64,20,16]{1,3,2,0:T(8,128)(2,1)} %copy-done.2) | copy-start | bytes 3932164 | tf_op jit(solution)/shard_map/while
  1803.6 117.7 %collective-permute-start.6 = (f32[32,64,20,16]{1,3,2,0:T(8,128)}, f32[32,64,20,16]{1,3,2,0:T(8,128)S(1)}, u32[]{:S(2)}, u32[]{:S(2)}) collective-permute-start(f32[32,64,20,16]{1,3,2,0:T(8,128)} %bitcast_add_fusion.6), channel_id=1, source_target_pairs={{0,8},{8,16},{16,24},{24,0},{1,9},{9,17},{17,25},{25,1},{2,10},{10... | collective-permute-start | bytes 7864328 | tf_op jit(solution)/shard_map/ppermute | solution.py:141
  1817.7 208.5 %collective-permute-start.7 = (f32[32,64,20,16]{1,3,2,0:T(8,128)}, f32[32,64,20,16]{1,3,2,0:T(8,128)}, u32[]{:S(2)}, u32[]{:S(2)}) collective-permute-start(f32[32,64,20,16]{1,3,2,0:T(8,128)} %bitcast_add_fusion.5), channel_id=1, source_target_pairs={{0,8},{8,16},{16,24},{24,0},{1,9},{9,17},{17,25},{25,1},{2,10},{10... | collective-permute-start | bytes 7864328 | tf_op jit(solution)/shard_map/ppermute | solution.py:142
  1831.4 90.6 %copy-start.45 = (f32[64,8]{0,1:T(8,128)S(1)}, f32[64,8]{0,1:T(8,128)}, u32[]{:S(2)}) copy-start(f32[64,8]{0,1:T(8,128)} %copy-done.44) | copy-start | bytes 6148
  1831.4 90.6 %copy-start.48 = (f32[64,8]{0,1:T(8,128)S(1)}, f32[64,8]{0,1:T(8,128)}, u32[]{:S(2)}) copy-start(f32[64,8]{0,1:T(8,128)} %get-tuple-element.788) | copy-start | bytes 6148
  1928.7 104.8 %copy-start.10 = (f32[32,64,1,20,16]{1,3,4,0,2:T(8,128)}, f32[32,64,1,20,16]{1,3,4,0,2:T(8,128)S(1)}, u32[]{:S(2)}) copy-start(f32[32,64,1,20,16]{1,3,4,0,2:T(8,128)S(1)} %maximum_multiply_fusion) | copy-start | bytes 7864324
  1932.2 101.2 %copy-start.8 = (f32[32,64,320]{2,1,0:T(8,128)S(1)}, f32[32,64,320]{2,1,0:T(8,128)}, u32[]{:S(2)}) copy-start(f32[32,64,320]{2,1,0:T(8,128)} %copy-done.6) | copy-start | bytes 7864324
  1932.3 101.2 %copy-start.25 = (f32[32,64]{1,0:T(8,128)S(1)}, f32[32,64]{1,0:T(8,128)}, u32[]{:S(2)}) copy-start(f32[32,64]{1,0:T(8,128)} %copy-done.23) | copy-start | bytes 24580
  1932.3 101.2 %copy-start.27 = (f32[32,64]{1,0:T(8,128)S(1)}, f32[32,64]{1,0:T(8,128)}, u32[]{:S(2)}) copy-start(f32[32,64]{1,0:T(8,128)} %copy-done.26) | copy-start | bytes 24580
  1932.3 101.2 %copy-start.39 = (f32[32,64]{1,0:T(8,128)S(1)}, f32[32,64]{1,0:T(8,128)}, u32[]{:S(2)}) copy-start(f32[32,64]{1,0:T(8,128)} %copy-done.38) | copy-start | bytes 24580
  1932.3 101.3 %copy-start.52 = (f32[320]{0:T(512)S(1)}, f32[320]{0:T(512)}, u32[]{:S(2)}) copy-start(f32[320]{0:T(512)} %copy-done.51) | copy-start | bytes 3844
  1932.3 101.3 %copy-start.64 = (f32[320]{0:T(512)S(1)}, f32[320]{0:T(512)}, u32[]{:S(2)}) copy-start(f32[320]{0:T(512)} %copy-done.63) | copy-start | bytes 3844
  2056.3 99.3 %reduce-scatter.12.cloned.1.call-start = ((), (), s32[]{:S(2)}) async-start(), calls=%async_computation.5 | async-start | bytes 2211840 | tf_op jit(solution)/shard_map/reduce_scatter | solution.py:36
  2063.6 112.4 %reduce-scatter.10.cloned.1.call-start = ((), (), s32[]{:S(2)}) async-start(), calls=%async_computation.4 | async-start | bytes 1843200 | tf_op jit(solution)/shard_map/reduce_scatter | solution.py:36
  2070.8 160.1 %all-reduce.9.cloned.1.call-start = ((), (), s32[]{:S(2)}) async-start(), calls=%async_computation.8 | async-start | bytes 2080768 | tf_op jit(solution)/shard_map/psum | solution.py:36
  2100.9 75.1 %copy-start.37 = (s32[32,64]{1,0:T(8,128)S(1)}, s32[32,64]{1,0:T(8,128)}, u32[]{:S(2)}) copy-start(s32[32,64]{1,0:T(8,128)} %param.14) | copy-start | bytes 24580
  2100.9 75.1 %copy-start.41 = (f32[32,64]{1,0:T(8,128)S(1)}, f32[32,64]{1,0:T(8,128)}, u32[]{:S(2)}) copy-start(f32[32,64]{1,0:T(8,128)} %copy-done.40) | copy-start | bytes 24580
  2176.0 60.0 %copy-start.1 = (bf16[33,320]{1,0:T(8,128)(2,1)S(1)}, bf16[33,320]{1,0:T(8,128)(2,1)}, u32[]{:S(2)}) copy-start(bf16[33,320]{1,0:T(8,128)(2,1)} %param.16) | copy-start | bytes 63364
  (59 other events, 783.0 us)
Sparse Core Ops, SparseCore 0:
  614.8 30.1 reduce-scatter.15
  2056.4 34.2 reduce-scatter.13
  2094.1 40.1 reduce-scatter.11
  2137.5 38.4 reduce-scatter.9
  2178.4 52.3 all-reduce.8
where the time goes:
time: 2250 us; the launch traced here: 2240 us
  waiting for transfers between devices  1370 us (61%)
  matrix products  416 us (18%)
  blocking collectives  167 us (7%)
  other arithmetic  130 us (6%)
  local copies, waits for them, and re-layouts  123 us (5%)
    ppermute x3, waiting for transfers between devices, bwd_body(): lax.ppermute(v_blk, 'cp', send_pairs)  772 us
    ppermute x3, waiting for transfers between devices, fwd_body(): lax.ppermute(v_blk, 'cp', send_pairs)  164 us
    ppermute x3, waiting for transfers between devices, bwd_body(): lax.ppermute(k_blk, 'cp', send_pairs)  153 us
    ppermute x1, waiting for transfers between devices, local_step(): d_value = lax.ppermute(carry[3] + d_value, 'cp', send_pairs)  94 us
    ppermute x1, waiting for transfers between devices, local_step(): d_key = lax.ppermute(carry[2] + d_key, 'cp', send_pairs)  89.9 us
    dot_general x8, matrix products, block_scores(): jnp.einsum('bqhd,bkhd->bhqk', q_rot, k_blk, preferred_element_type=jnp.fl...  71.5 us
    ppermute x3, waiting for transfers between devices, fwd_body(): lax.ppermute(k_blk, 'cp', send_pairs)  70.3 us
    dot_general x4, matrix products, bwd_block(): jnp.einsum('bqhd,bkhd->bhqk', d_attn_b, v_blk, preferred_element_type=jnp...  68 us
  transfers between devices with their start and end apart: 25, of which 16 were waited for; matrix products, arithmetic and copies ran while one was open for 22% of the time, Pallas kernels for 0%

commit v1 on v0

v1 whole, which is shorter than its diff:
```python
import functools

import jax
import jax.numpy as jnp
from jax import lax
from jax.experimental import pallas as pl
from jax.experimental.pallas import tpu as pltpu
from jax.sharding import PartitionSpec as P

MASK_ID = 32
LN_EPS = 1e-5
ROPE_BASE = 10000.0
TRAIN_RATIO = 0.15 * 0.8
NEG_BIG = -1e30
VOCAB_PAD = 128
HEAD_DIM = 16
N_HEADS = 20
D = 320
F = 1280
SEQ = 256
LANES = 128
HEADS_PER_TILE = LANES // HEAD_DIM
N_TILES = -(-D // LANES)
HEAD_UNROLL = 4
QKV_HALF = 512
UO_PAD = 1664
SM_ROWS = 16
BF = jnp.bfloat16
F32 = jnp.float32
SQRT_HALF = 0.7071067811865476
INV_SQRT_2PI = 0.3989422804014327

NN = (((1,), (0,)), ((), ()))
NT = (((1,), (1,)), ((), ()))


def dot(a, b, dims=NN):
    return lax.dot_general(a, b, dims, preferred_element_type=F32)


def col(vecs_t, j):
    return vecs_t[:, j:j + 1]


def rope(z, cos_t, sin_t):
    z4 = z.reshape(N_HEADS, 2, HEAD_DIM // 2, SEQ)
    lower, upper = z4[:, 0], z4[:, 1]
    new_l = lower * cos_t - upper * sin_t
    new_u = upper * cos_t + lower * sin_t
    return jnp.stack([new_l, new_u], axis=1).reshape(D, SEQ)


def key_bias(shift_base, cp_size, seq_loc, length):
    row = lax.broadcasted_iota(jnp.int32, (SEQ, SEQ), 0)
    src = (shift_base - row // seq_loc + cp_size) % cp_size
    pos = src * seq_loc + row % seq_loc
    return jnp.where(pos < length, 0.0, NEG_BIG).astype(F32)


def store_token_major(dst_ref, z_t):
    for t in range(N_TILES):
        lo = t * LANES
        hi = min(lo + LANES, D)
        part = z_t[lo:hi]
        if hi - lo < LANES:
            part = jnp.concatenate([part, jnp.zeros((LANES - (hi - lo), z_t.shape[1]), F32)], axis=0)
        dst_ref[t] = part.T.astype(BF)


def head_rows(tile, slot):
    row = lax.broadcasted_iota(jnp.int32, tile.shape, 0)
    return jnp.where(row // HEAD_DIM == slot, tile, jnp.zeros_like(tile))


def token_scale(tok, length, seq_loc, cp_size, me):
    lane = lax.broadcasted_iota(jnp.int32, (1, SEQ), 1)
    src = (me - lane // seq_loc + cp_size) % cp_size
    pos = src * seq_loc + lane % seq_loc
    is_mask = tok == MASK_ID
    n_mask = jnp.sum(is_mask.astype(F32), axis=1, keepdims=True)
    drop = (1.0 - TRAIN_RATIO) / (1.0 - n_mask / length.astype(F32))
    return jnp.where(is_mask | (pos >= length), 0.0, drop)


def one_hot_rows(tok):
    row = lax.broadcasted_iota(jnp.int32, (VOCAB_PAD, SEQ), 0)
    return jnp.where(row == tok, 1.0, 0.0).astype(BF)


def join_rows(ref):
    return jnp.concatenate([ref[i].astype(F32) for i in range(ref.shape[0])], axis=0).astype(BF)


def wide(z):
    return jnp.concatenate([z, z], axis=1)


def fwd_kernel(cp_size, seq_loc, len_ref, me_ref, tok_ref, emb_ref, sm_ref, wqkv_ref, wout_ref, wup_ref, wdown_ref, cos_ref, sin_ref,
               o0_ref, o1_ref, o2_ref, o3_ref, h_ref, xhat1_ref, stat_ref, qkv_ref, lse_ref, attn_ref, xhat2_ref, a_ref, gelu_ref, dgelu_ref, gain_ref, wqkv_n, wout_n, wup_n,
               wqkv_t, wout_t, wup_t, wdown_t, k_tm, q_pad, bias, vec_b, bup_b):
    step = pl.program_id(0)

    @pl.when(step == 0)
    def _():
        for src, nat, tr in ((wqkv_ref, wqkv_n, wqkv_t), (wout_ref, wout_n, wout_t), (wup_ref, wup_n, wup_t)):
            joined = join_rows(src)
            nat[...] = joined
            tr[...] = joined.T
        wdown_t[...] = wdown_ref[...].T
        q_pad[...] = jnp.zeros_like(q_pad)
        pieces = sm_ref.shape[0]
        rows = D // pieces
        for i in range(pieces):
            sm_t = sm_ref[i].T
            gain_ref[i * rows:(i + 1) * rows] = sm_t[:rows]
            for j in range(9):
                vec_b[j, i * rows:(i + 1) * rows] = jnp.broadcast_to(sm_t[:rows, j:j + 1], (rows, LANES))
            for r in range(F // D):
                lo = i * (F // pieces) + r * rows
                bup_b[lo:lo + rows] = jnp.broadcast_to(sm_t[:rows, 9 + r:10 + r], (rows, LANES))

    length = len_ref[step]
    me = me_ref[0]
    tok = tok_ref[0]
    keep = token_scale(tok, length, seq_loc, cp_size, me)
    e = dot(emb_ref[...], one_hot_rows(tok)) * keep
    mean = jnp.mean(e, axis=0, keepdims=True)
    cent = e - mean
    var = jnp.mean(cent * cent, axis=0, keepdims=True)
    rstd1 = lax.rsqrt(var + LN_EPS)
    xhat1 = cent * rstd1
    xhat1_ref[0] = xhat1
    h = (xhat1 * wide(vec_b[0]) + wide(vec_b[1])).astype(BF)
    h_ref[0] = h
    cos_t, sin_t = cos_ref[...], sin_ref[...]
    q = (dot(wqkv_t[0:D], h) + wide(vec_b[2])) * HEAD_DIM ** -0.5
    q = rope(q, cos_t, sin_t).astype(BF)
    qkv_ref[0, 0:D] = q
    q_pad[0:D] = q
    k = rope(dot(wqkv_t[D:2 * D], h) + wide(vec_b[3]), cos_t, sin_t)
    qkv_ref[0, D:2 * D] = k.astype(BF)
    store_token_major(k_tm, k)
    qkv_ref[0, 2 * D:3 * D] = (dot(wqkv_t[2 * D:3 * D], h) + wide(vec_b[4])).astype(BF)
    bias[...] = key_bias(me, cp_size, seq_loc, length)

    def head_body(it, _):
        for u in range(HEAD_UNROLL):
            hd = it * HEAD_UNROLL + u
            tile = hd // HEADS_PER_TILE
            slot = hd % HEADS_PER_TILE
            q_t = q_pad[pl.ds(pl.multiple_of(tile * LANES, LANES), LANES), :]
            s = dot(k_tm[tile], head_rows(q_t, slot)) + bias[...]
            m = jnp.max(s, axis=0, keepdims=True)
            p = jnp.exp(s - m)
            l = jnp.sum(p, axis=0, keepdims=True)
            r0 = pl.multiple_of(hd * HEAD_DIM, HEAD_DIM)
            v_h = qkv_ref[0, pl.ds(pl.multiple_of(2 * D + hd * HEAD_DIM, HEAD_DIM), HEAD_DIM), :]
            attn_ref[0, pl.ds(r0, HEAD_DIM), :] = dot(v_h, p.astype(BF)) / l
            lse_ref[0, hd] = m + jnp.log(l)
        return 0

    lax.fori_loop(0, N_HEADS // HEAD_UNROLL, head_body, 0)

    o = attn_ref[0].astype(BF)
    x1 = e + dot(wout_t[...], o) + wide(vec_b[5])
    mean2 = jnp.mean(x1, axis=0, keepdims=True)
    cent2 = x1 - mean2
    var2 = jnp.mean(cent2 * cent2, axis=0, keepdims=True)
    rstd2 = lax.rsqrt(var2 + LN_EPS)
    xhat2 = cent2 * rstd2
    xhat2_ref[0] = xhat2
    a = (xhat2 * wide(vec_b[6]) + wide(vec_b[7])).astype(BF)
    a_ref[0] = a
    stat_ref[0] = jnp.concatenate([rstd1, rstd2, keep, jnp.zeros((5, SEQ), F32)], axis=0)
    out = x1 + wide(vec_b[8])
    for c in range(F // D):
        rows = slice(c * D, (c + 1) * D)
        u = dot(wup_t[rows], a) + wide(bup_b[rows])
        cdf = 0.5 * (1.0 + lax.erf(u * SQRT_HALF))
        g = (u * cdf).astype(BF)
        gelu_ref[0, rows] = g
        dgelu_ref[0, rows] = cdf + u * (INV_SQRT_2PI * jnp.exp(-0.5 * u * u))
    out = out + dot(wdown_t[...], gelu_ref[0])
    out_tm = to_token_major(out)
    for k_i, o_ref in enumerate((o0_ref, o1_ref, o2_ref, o3_ref)):
        o_ref[0] = out_tm[k_i * seq_loc:(k_i + 1) * seq_loc]


def to_token_major(z_t):
    parts = []
    for t in range(N_TILES):
        lo, hi = t * LANES, min((t + 1) * LANES, D)
        part = z_t[lo:hi]
        if hi - lo < LANES:
            part = jnp.concatenate([part, jnp.zeros((LANES - (hi - lo), SEQ), F32)], axis=0)
        parts.append(part.T.astype(BF))
    return jnp.concatenate(parts, axis=1)[:, :D]


def to_feature_major(z):
    z32 = z.astype(F32)
    pad = jnp.concatenate([z32, jnp.zeros((SEQ, N_TILES * LANES - D), F32)], axis=1)
    return jnp.concatenate([pad[:, t * LANES:(t + 1) * LANES].T for t in range(N_TILES)], axis=0)[:D]


def lane_part(z):
    return z[:, :LANES] + z[:, LANES:]


def ln_grad(dn, xhat, rstd, gain):
    dxh = dn * gain
    m1 = jnp.mean(dxh, axis=0, keepdims=True)
    m2 = jnp.mean(dxh * xhat, axis=0, keepdims=True)
    return rstd * (dxh - m1 - xhat * m2)


def row_sum(acc):
    return jnp.sum(acc.T, axis=0, keepdims=True)


def ffn_bwd_kernel(n_steps, seq_loc, g0_ref, g1_ref, g2_ref, g3_ref, vec_ref, wdown_ref, wup_ref, wout_ref, gelu_ref, dgelu_ref, a_ref, xhat2_ref, stat_ref, attn_ref,
                   dres_ref, dattn_ref, dwdown_ref, dwuo_ref, dbup_ref, dvec_ref,
                   acc_bup, acc_vec):
    step = pl.program_id(0)

    @pl.when(step == 0)
    def _():
        dwdown_ref[...] = jnp.zeros_like(dwdown_ref)
        dwuo_ref[...] = jnp.zeros_like(dwuo_ref)
        acc_bup[...] = jnp.zeros_like(acc_bup)
        acc_vec[...] = jnp.zeros_like(acc_vec)

    vecs = vec_ref[...]
    g = jnp.concatenate([g0_ref[0], g1_ref[0], g2_ref[0], g3_ref[0]], axis=0)
    g_t = to_feature_major(g)
    a = a_ref[0]
    dn2 = jnp.zeros((D, SEQ), F32)
    dup_parts = []
    for c in range(F // D):
        rows = slice(c * D, (c + 1) * D)
        dup = dot(wdown_ref[rows], g, NT) * dgelu_ref[0, rows]
        acc_bup[rows] += lane_part(dup)
        dup_parts.append(dup.astype(BF))
        dwdown_ref[rows] += dot(gelu_ref[0, rows], g)
    dup_b = jnp.concatenate(dup_parts, axis=0)
    dwuo_ref[:, 0:F] += dot(a, dup_b, NT)
    dn2 = dot(wup_ref[...], dup_b)
    xhat2 = xhat2_ref[0]
    rstd2 = stat_ref[0, 1:2]
    dres = g_t + ln_grad(dn2, xhat2, rstd2, col(vecs, 6))
    acc_vec[0] += lane_part(dres)
    acc_vec[1] += lane_part(dn2 * xhat2)
    acc_vec[2] += lane_part(dn2)
    acc_vec[3] += lane_part(g_t)
    dres_ref[0] = dres
    dres_b = dres.astype(BF)
    dwuo_ref[:, F:F + D] += dot(attn_ref[0].astype(BF), dres_b, NT)
    dattn_ref[0] = dot(wout_ref[...], dres_b)

    @pl.when(step == n_steps - 1)
    def _():
        dbup_ref[...] = row_sum(acc_bup[...])
        dvec_ref[...] = jnp.concatenate([row_sum(pad_rows(acc_vec[j])) for j in range(4)] + [jnp.zeros((4, N_TILES * LANES), F32)], axis=0)


def pad_rows(z):
    return jnp.concatenate([z, jnp.zeros((N_TILES * LANES - D, LANES), F32)], axis=0)


def attn_bwd_kernel(n_steps, cp_size, seq_loc, len_ref, me_ref, tok_ref, vec_ref, wqkv_ref, cos_ref, sin_ref, qkv_ref, lse_ref, attn_ref, dattn_ref, dres_ref, xhat1_ref, h_ref, stat_ref,
                    dwqa_ref, dwqb_ref, demb_ref, dvec_ref,
                    k_tm, v_tm, q_pad, do_pad, bias, dq_s, dk_s, dv_s, acc_b, acc_vec):
    step = pl.program_id(0)

    @pl.when(step == 0)
    def _():
        dwqa_ref[...] = jnp.zeros_like(dwqa_ref)
        dwqb_ref[...] = jnp.zeros_like(dwqb_ref)
        demb_ref[...] = jnp.zeros_like(demb_ref)
        acc_b[...] = jnp.zeros_like(acc_b)
        acc_vec[...] = jnp.zeros_like(acc_vec)
        q_pad[...] = jnp.zeros_like(q_pad)
        do_pad[...] = jnp.zeros_like(do_pad)

    length = len_ref[step]
    me = me_ref[0]
    vecs = vec_ref[...]
    q_pad[0:D] = qkv_ref[0, 0:D]
    do_pad[0:D] = dattn_ref[0].astype(BF)
    store_token_major(k_tm, qkv_ref[0, D:2 * D].astype(F32))
    store_token_major(v_tm, qkv_ref[0, 2 * D:3 * D].astype(F32))
    bias[...] = key_bias(me, cp_size, seq_loc, length)

    def head_body(it, _):
        for u in range(HEAD_UNROLL):
            hd = it * HEAD_UNROLL + u
            tile = hd // HEADS_PER_TILE
            slot = hd % HEADS_PER_TILE
            t0 = pl.ds(pl.multiple_of(tile * LANES, LANES), LANES)
            rows = pl.ds(pl.multiple_of(hd * HEAD_DIM, HEAD_DIM), HEAD_DIM)
            q_h = q_pad[rows, :]
            do_h = do_pad[rows, :]
            k_h = qkv_ref[0, pl.ds(pl.multiple_of(D + hd * HEAD_DIM, HEAD_DIM), HEAD_DIM), :]
            delta = jnp.sum(dattn_ref[0, rows, :] * attn_ref[0, rows, :], axis=0, keepdims=True)
            s = dot(k_tm[tile], head_rows(q_pad[t0, :], slot)) + bias[...]
            p = jnp.exp(s - lse_ref[0, hd])
            dp = dot(v_tm[tile], head_rows(do_pad[t0, :], slot))
            ds = (p * (dp - delta)).astype(BF)
            dq_s[rows, :] = dot(k_h, ds)
            dk_s[rows, :] = dot(q_h, ds, NT)
            dv_s[rows, :] = dot(do_h, p.astype(BF), NT)
        return 0

    lax.fori_loop(0, N_HEADS // HEAD_UNROLL, head_body, 0)

    cos_t, sin_t = cos_ref[...], sin_ref[...]
    h = h_ref[0]
    dq = rope(dq_s[...], cos_t, -sin_t) * HEAD_DIM ** -0.5
    dk = rope(dk_s[...], cos_t, -sin_t)
    dv = dv_s[...]
    dn1 = jnp.zeros((D, SEQ), F32)
    parts = []
    for j, dz in enumerate((dq, dk, dv)):
        acc_b[j] += lane_part(dz)
        parts.append(dz.astype(BF))
    dz_b = jnp.concatenate(parts, axis=0)
    dwqa_ref[...] += dot(h, dz_b[:QKV_HALF], NT)
    dwqb_ref[:, :3 * D - QKV_HALF] += dot(h, dz_b[QKV_HALF:], NT)
    dn1 = dot(wqkv_ref[...], dz_b)
    xhat1 = xhat1_ref[0]
    acc_vec[0] += lane_part(dn1 * xhat1)
    acc_vec[1] += lane_part(dn1)
    de = dres_ref[0] + ln_grad(dn1, xhat1, stat_ref[0, 0:1], col(vecs, 0))
    de = (de * stat_ref[0, 2:3]).astype(BF)
    demb_ref[...] += dot(one_hot_rows(tok_ref[0]), de, NT)

    @pl.when(step == n_steps - 1)
    def _():
        rows = [row_sum(pad_rows(acc_vec[j])) for j in range(2)] + [row_sum(pad_rows(acc_b[j])) for j in range(3)]
        dvec_ref[...] = jnp.concatenate(rows + [jnp.zeros((3, N_TILES * LANES), F32)], axis=0)


def per_seq(*shape):
    return pl.BlockSpec((1,) + shape, lambda b: (b,) + (0,) * len(shape))


def whole(*shape):
    return pl.BlockSpec(shape, lambda b: (0,) * len(shape))


SMEM = pl.BlockSpec(memory_space=pltpu.SMEM)


def sds(shape, dtype):
    return jax.ShapeDtypeStruct(shape, dtype)


def call(kernel, grid, in_specs, out_specs, out_shape, scratch, flops, name):
    return pl.pallas_call(
        kernel, grid=(grid,), in_specs=in_specs, out_specs=out_specs, out_shape=out_shape, scratch_shapes=scratch, name=name,
        cost_estimate=pl.CostEstimate(flops=flops, bytes_accessed=50_000_000, transcendentals=10_000_000),
        compiler_params=pltpu.CompilerParams(dimension_semantics=('arbitrary',), vmem_limit_bytes=58 * 1024 * 1024))


MESH = pl.DeviceIdType.MESH


def place(fs):
    return fs // 4, (fs // 2) % 2, fs % 2


def device(cp, fs):
    return {'cp': cp, 'fsdp': fs}


def enter(peers):
    barrier = pltpu.get_barrier_semaphore()
    for peer in peers:
        pl.semaphore_signal(barrier, inc=1, device_id=peer, device_id_type=MESH)
    pl.semaphore_wait(barrier, len(peers))


def remote(src, dst, send_sem, recv_sem, peer):
    return pltpu.make_async_remote_copy(src_ref=src, dst_ref=dst, send_sem=send_sem, recv_sem=recv_sem, device_id=peer, device_id_type=MESH)


def gather_kernel(cp_size, n_arr, *refs):
    ins, tok_in = refs[:n_arr], refs[n_arr]
    outs, tok_out = refs[n_arr + 1:2 * n_arr + 1], refs[2 * n_arr + 1]
    send, recv, tok_send, tok_recv = refs[2 * n_arr + 2:]
    me = lax.axis_index('cp')
    fs = lax.axis_index('fsdp')
    y, x, c = place(fs)
    near, xn, yn = fs + 1 - 2 * c, fs + 2 - 4 * x, fs + 4 - 8 * y
    dg = xn + 4 - 8 * y
    first = xn * (1 - c) + yn * c
    other = yn * (1 - c) + xn * c
    cps = [lax.rem(me + k, cp_size) for k in range(1, cp_size)]
    enter([device(me, near), device(me, xn), device(me, yn)] + [device(z, fs) for z in cps])

    sent = []

    def push(a, src, slot, peer, lane):
        copy = remote(src, outs[a].at[slot], send.at[a, lane], recv.at[a, slot], device(me, peer))
        copy.start()
        sent.append(copy)

    def arrived(a, slot):
        remote(ins[a], outs[a].at[slot], send.at[a, 0], recv.at[a, slot], device(me, near)).wait_recv()

    for k in range(1, cp_size):
        copy = remote(tok_in.at[cps[k - 1]], tok_out.at[k], tok_send.at[k], tok_recv.at[k], device(cps[k - 1], fs))
        copy.start()
        sent.append(copy)
    for a in range(n_arr):
        push(a, ins[a], fs, xn, 0)
        push(a, ins[a], fs, yn, 1)
        push(a, ins[a], fs, near, 2)
    for a in range(n_arr):
        outs[a][fs] = ins[a][...]
    tok_out[0] = tok_in[me]
    for a in range(n_arr):
        arrived(a, first)
        push(a, outs[a].at[first], first, other, 3)
        push(a, outs[a].at[first], first, near, 4)
    for a in range(n_arr):
        arrived(a, other)
        push(a, outs[a].at[other], other, near, 5)
    for a in range(n_arr):
        arrived(a, dg)
        push(a, outs[a].at[dg], dg, near, 6)
    for a in range(n_arr):
        arrived(a, near)
        for slot in (xn, yn, dg):
            arrived(a, slot + 1 - 2 * c)
    for k in range(1, cp_size):
        remote(tok_in.at[0], tok_out.at[k], tok_send.at[k], tok_recv.at[k], device(me, near)).wait_recv()
    for copy in sent:
        copy.wait_send()


def gather_call(cp_size, arrays, tok):
    n_arr = len(arrays)
    pieces = 8
    vmem = pl.BlockSpec(memory_space=pltpu.VMEM)
    dma = pltpu.SemaphoreType.DMA
    return pl.pallas_call(
        functools.partial(gather_kernel, cp_size, n_arr),
        out_shape=[sds((pieces,) + arr.shape, arr.dtype) for arr in arrays] + [sds(tok.shape, tok.dtype)],
        in_specs=[vmem] * (n_arr + 1), out_specs=[vmem] * (n_arr + 1),
        scratch_shapes=[dma((n_arr, 7)), dma((n_arr, pieces)), dma((cp_size,)), dma((cp_size,))],
        compiler_params=pltpu.CompilerParams(collective_id=0, has_side_effects=True, vmem_limit_bytes=48 * 1024 * 1024),
        name='gather',
    )(*arrays, tok)


def piece_of(ref, spec, p):
    axis, size, stride = spec
    start = pl.multiple_of(p * stride, stride)
    return ref.at[pl.ds(start, size), :] if axis == 0 else ref.at[:, pl.ds(start, size)]


def reduce_kernel(cp_size, specs, *refs):
    n = len(specs)
    big, small = refs[:n], refs[n]
    outs, small_out = refs[n + 1:2 * n + 1], refs[2 * n + 1]
    rest = refs[2 * n + 2:]
    r0, acc, r1, r2, rz, rg = (rest[i * n:(i + 1) * n] for i in range(6))
    es, er, ez, s0, v0, s1, v1, s2, v2, sz, vz, sg, vg, se, ve, sez, vez = rest[6 * n:]
    me = lax.axis_index('cp')
    fs = lax.axis_index('fsdp')
    y, x, c = place(fs)
    near, xn, yn = fs + 1 - 2 * c, fs + 2 - 4 * x, fs + 4 - 8 * y
    cps = [lax.rem(me + k, cp_size) for k in range(1, cp_size)]
    hops = (device(me, near), device(me, xn), device(me, yn))
    enter(list(hops) + [device(z, fs) for z in cps])

    def start(copies):
        for copy in copies:
            copy.start()

    def finish(copies):
        for copy in copies:
            copy.wait()

    def small_hop(i, src):
        copy = remote(src, er.at[i], se.at[i], ve.at[i], hops[i])
        copy.start()
        return copy

    first = [[remote(b.at[2 * j + 1 - c], r0[i].at[j], s0.at[i, j], v0.at[i, j], hops[0]) for j in range(4)] for i, b in enumerate(big)]
    for group in first:
        start(group)
    hop = small_hop(0, small)
    second = []
    for i, (path, _) in enumerate(specs):
        finish(first[i])
        for j in range(4):
            acc[i][j] = big[i][2 * j + c] + r0[i][j]
        group = []
        for k in range(2):
            give = 2 * k + 1 - x if path == 'xy' else 2 * (1 - y) + k
            group.append(remote(acc[i].at[give], r1[i].at[k], s1.at[i, k], v1.at[i, k], hops[1] if path == 'xy' else hops[2]))
        start(group)
        second.append(group)
    hop.wait()
    es[0] = small[...] + er[0]
    hop = small_hop(1, es.at[0])
    third = []
    for i, (path, _) in enumerate(specs):
        finish(second[i])
        for k in range(2):
            keep = 2 * k + x if path == 'xy' else 2 * y + k
            r1[i][k] = acc[i][keep] + r1[i][k]
        give = 1 - y if path == 'xy' else 1 - x
        copy = remote(r1[i].at[give], r2[i], s2.at[i], v2.at[i], hops[2] if path == 'xy' else hops[1])
        copy.start()
        third.append(copy)
    hop.wait()
    es[1] = es[0] + er[1]
    hop = small_hop(2, es.at[1])
    fourth = []
    for i, (path, spec) in enumerate(specs):
        third[i].wait()
        keep = y if path == 'xy' else x
        outs[i][...] = r1[i][keep] + r2[i][...]
        group = [remote(piece_of(outs[i], spec, cps[k]), rz[i].at[k], sz.at[i, k], vz.at[i, k], device(cps[k], fs)) for k in range(cp_size - 1)]
        start(group)
        fourth.append(group)
    hop.wait()
    ez[me] = es[1] + er[2]
    last = [remote(ez.at[me], ez.at[me], sez.at[k], vez.at[k], device(cps[k], fs)) for k in range(cp_size - 1)]
    start(last)
    fifth = []
    for i, (path, spec) in enumerate(specs):
        finish(fourth[i])
        rg[i][me] = ((piece_of(outs[i], spec, me)[...] + rz[i][0]) + rz[i][1]) + rz[i][2]
        group = [remote(rg[i].at[me], rg[i].at[me], sg.at[i, k], vg.at[i, k], device(cps[k], fs)) for k in range(cp_size - 1)]
        start(group)
        fifth.append(group)
    finish(last)
    small_out[...] = ((ez[0] + ez[1]) + ez[2]) + ez[3]
    for i, (path, spec) in enumerate(specs):
        finish(fifth[i])
        for p in range(cp_size):
            axis, size, stride = spec
            lo = p * stride
            if axis == 0:
                outs[i][lo:lo + size, :] = rg[i][p]
            else:
                outs[i][:, lo:lo + size] = rg[i][p]


def reduce_call(cp_size, arrays, small):
    vmem = pl.BlockSpec(memory_space=pltpu.VMEM)
    dma = pltpu.SemaphoreType.DMA
    n = len(arrays)
    specs = tuple((path, spec) for _, path, spec in arrays)
    shapes = [arr.shape[1:] for arr, _, _ in arrays]
    cut = [((size, sh[1]) if axis == 0 else (sh[0], size)) for sh, (_, (axis, size, _)) in zip(shapes, specs)]
    scratch = [pltpu.VMEM((4,) + sh, F32) for sh in shapes] * 2 + [pltpu.VMEM((2,) + sh, F32) for sh in shapes] + [pltpu.VMEM(sh, F32) for sh in shapes]
    scratch += [pltpu.VMEM((cp_size - 1,) + sh, F32) for sh in cut] + [pltpu.VMEM((cp_size,) + sh, F32) for sh in cut]
    scratch += [pltpu.VMEM((2,) + small.shape, F32), pltpu.VMEM((3,) + small.shape, F32), pltpu.VMEM((cp_size,) + small.shape, F32)]
    for shape in ((n, 4), (n, 2), (n,), (n, cp_size - 1), (n, cp_size - 1), (3,), (cp_size - 1,)):
        scratch += [dma(shape), dma(shape)]
    return pl.pallas_call(
        functools.partial(reduce_kernel, cp_size, specs),
        out_shape=[sds(sh, F32) for sh in shapes] + [sds(small.shape, F32)],
        in_specs=[vmem] * (n + 1), out_specs=[vmem] * (n + 1), scratch_shapes=scratch,
        compiler_params=pltpu.CompilerParams(collective_id=1, has_side_effects=True, vmem_limit_bytes=48 * 1024 * 1024),
        name='reduce',
    )(*[arr for arr, _, _ in arrays], small)


def solution(mesh):
    cp_size = mesh.shape['cp']
    fs_size = mesh.shape['fsdp']

    def shift(k):
        return [(i, (i + k) % cp_size) for i in range(cp_size)]

    def local_step(tokens, lengths, embed_table, layer_vecs, w_qkv, w_out, w_up, b_up, w_down, grad_out):
        n_loc, seq_loc = tokens.shape
        n_seq = n_loc // cp_size
        me = lax.axis_index('cp')
        fs = lax.axis_index('fsdp')

        def to_whole(arr):
            blocks = []
            for k in range(cp_size):
                dest = (me + k) % cp_size
                blk = lax.dynamic_slice_in_dim(arr, dest * n_seq, n_seq, 0)
                blocks.append(lax.ppermute(blk, 'cp', shift(k)) if k else blk)
            return blocks

        g_blocks = to_whole(grad_out)
        len_w = lax.dynamic_slice_in_dim(lengths, me * n_seq, n_seq, 0)
        small = jnp.concatenate([layer_vecs, b_up.reshape(F // D, D // fs_size)], axis=0)
        small = jnp.pad(small, ((0, SM_ROWS - small.shape[0]), (0, LANES - small.shape[1])))
        qkv_p, out_p, up_p, down_p, small_p, tok_p = gather_call(cp_size, [w_qkv.reshape(-1, 3 * D), w_out, w_up, w_down, small], tokens.reshape(cp_size, n_seq, seq_loc))
        down_w = down_p.reshape(F, D)
        tok_w = tok_p.transpose(1, 0, 2).reshape(n_seq, 1, SEQ)
        emb_t = jnp.pad(embed_table, ((0, VOCAB_PAD - embed_table.shape[0]), (0, 0))).T

        lane = jnp.arange(SEQ)
        positions = ((me - lane // seq_loc + cp_size) % cp_size) * seq_loc + lane % seq_loc
        inv_freq = 1.0 / (ROPE_BASE ** (jnp.arange(0, HEAD_DIM, 2, dtype=F32) / HEAD_DIM))
        angles = inv_freq[:, None] * positions.astype(F32)[None, :]
        cos_t, sin_t = jnp.cos(angles), jnp.sin(angles)
        me_arr = me.reshape(1).astype(jnp.int32)

        S = SEQ
        blk_spec = per_seq(seq_loc, D)
        outs = call(
            functools.partial(fwd_kernel, cp_size, seq_loc), n_seq,
            [SMEM, SMEM, per_seq(1, S), whole(D, VOCAB_PAD), whole(*small_p.shape), whole(*qkv_p.shape), whole(*out_p.shape), whole(*up_p.shape), whole(F, D), whole(8, S), whole(8, S)],
            [blk_spec] * 4 + [per_seq(D, S), per_seq(D, S), per_seq(8, S), per_seq(3 * D, S), per_seq(N_HEADS, 1, S), per_seq(D, S), per_seq(D, S), per_seq(D, S), per_seq(F, S), per_seq(F, S), whole(D, SM_ROWS), whole(D, 3 * D), whole(D, D), whole(D, F)],
            [sds((n_seq, seq_loc, D), BF)] * 4 + [sds((n_seq, D, S), BF), sds((n_seq, D, S), F32), sds((n_seq, 8, S), F32), sds((n_seq, 3 * D, S), BF), sds((n_seq, N_HEADS, 1, S), F32), sds((n_seq, D, S), F32), sds((n_seq, D, S), F32), sds((n_seq, D, S), BF), sds((n_seq, F, S), BF), sds((n_seq, F, S), F32), sds((D, SM_ROWS), F32), sds((D, 3 * D), BF), sds((D, D), BF), sds((D, F), BF)],
            [pltpu.VMEM((3 * D, D), BF), pltpu.VMEM((D, D), BF), pltpu.VMEM((F, D), BF), pltpu.VMEM((D, F), BF), pltpu.VMEM((N_TILES, S, LANES), BF), pltpu.VMEM((N_TILES * LANES, S), BF), pltpu.VMEM((S, S), F32), pltpu.VMEM((9, D, LANES), F32), pltpu.VMEM((F, LANES), F32)],
            9_000_000_000, 'fwd',
        )(len_w, me_arr, tok_w, emb_t, small_p, qkv_p, out_p, up_p, down_w, cos_t, sin_t)
        out_blocks = outs[:4]
        h, xhat1, stat, qkv, lse, attn, xhat2, a, gelu, dgelu, vecs_t, qkv_w, out_w, up_w = outs[4:]

        dres, dattn, dw_down, dw_uo, db_up, dvec2 = call(
            functools.partial(ffn_bwd_kernel, n_seq, seq_loc), n_seq,
            [blk_spec] * 4 + [whole(D, SM_ROWS), whole(F, D), whole(D, F), whole(D, D), per_seq(F, S), per_seq(F, S), per_seq(D, S), per_seq(D, S), per_seq(8, S), per_seq(D, S)],
            [per_seq(D, S), per_seq(D, S), whole(F, D), whole(D, UO_PAD), whole(1, F), whole(8, N_TILES * LANES)],
            [sds((n_seq, D, S), F32), sds((n_seq, D, S), F32), sds((F, D), F32), sds((D, UO_PAD), F32), sds((1, F), F32), sds((8, N_TILES * LANES), F32)],
            [pltpu.VMEM((F, LANES), F32), pltpu.VMEM((4, D, LANES), F32)],
            9_000_000_000, 'ffn_bwd',
        )(*g_blocks, vecs_t, down_w, up_w, out_w, gelu, dgelu, a, xhat2, stat, attn)

        dw_qa, dw_qb, d_emb, dvec1 = call(
            functools.partial(attn_bwd_kernel, n_seq, cp_size, seq_loc), n_seq,
            [SMEM, SMEM, per_seq(1, S), whole(D, SM_ROWS), whole(D, 3 * D), whole(8, S), whole(8, S), per_seq(3 * D, S), per_seq(N_HEADS, 1, S), per_seq(D, S), per_seq(D, S), per_seq(D, S), per_seq(D, S), per_seq(D, S), per_seq(8, S)],
            [whole(D, QKV_HALF), whole(D, QKV_HALF), whole(VOCAB_PAD, D), whole(8, N_TILES * LANES)],
            [sds((D, QKV_HALF), F32), sds((D, QKV_HALF), F32), sds((VOCAB_PAD, D), F32), sds((8, N_TILES * LANES), F32)],
            [pltpu.VMEM((N_TILES, S, LANES), BF), pltpu.VMEM((N_TILES, S, LANES), BF), pltpu.VMEM((N_TILES * LANES, S), BF), pltpu.VMEM((N_TILES * LANES, S), BF), pltpu.VMEM((S, S), F32),
             pltpu.VMEM((D, S), F32), pltpu.VMEM((D, S), F32), pltpu.VMEM((D, S), F32), pltpu.VMEM((3, D, LANES), F32), pltpu.VMEM((2, D, LANES), F32)],
            9_000_000_000, 'attn_bwd',
        )(len_w, me_arr, tok_w, vecs_t, qkv_w, cos_t, sin_t, qkv, lse, attn, dattn, dres, xhat1, h, stat)

        layer_out = jnp.zeros((n_loc, seq_loc, D), BF)
        for k in range(cp_size):
            back = lax.ppermute(out_blocks[k], 'cp', shift(-k)) if k else out_blocks[0]
            layer_out = lax.dynamic_update_slice_in_dim(layer_out, back, ((me + k) % cp_size) * n_seq, 0)

        vocab = embed_table.shape[0]
        packed = jnp.concatenate([d_emb[:vocab], dvec1[:5, :D], dvec2[:4, :D], db_up.reshape(F // D, D)], axis=0)
        packed = jnp.pad(packed, ((0, 48 - packed.shape[0]), (0, N_TILES * LANES - D)))

        def pieces(arr):
            return arr.reshape(fs_size, arr.shape[0] // fs_size, arr.shape[1])

        r_down, r_uo, r_qa, r_qb, packed = reduce_call(cp_size, [(pieces(dw_down), 'xy', (0, 40, 40)), (pieces(dw_uo), 'yx', (1, 512, 384)), (pieces(dw_qa), 'xy', (1, 128, 128)), (pieces(dw_qb), 'yx', (1, 128, 128))], packed)
        packed = packed[:, :D]
        d_vecs = lax.dynamic_slice_in_dim(packed[vocab:vocab + 9], fs * (D // fs_size), D // fs_size, 1)
        d_bup = lax.dynamic_slice_in_dim(packed[vocab + 9:vocab + 13].reshape(F), fs * (F // fs_size), F // fs_size, 0)
        d_qkv = jnp.concatenate([r_qa, r_qb], axis=1)[:, :3 * D].reshape(w_qkv.shape)
        return (layer_out, packed[:vocab], d_vecs, d_qkv, r_uo[:, F:F + D], r_uo[:, :F], d_bup, r_down)

    in_specs = (P('fsdp', 'cp'), P('fsdp'), P(), P(None, 'fsdp'), P('fsdp', None, None, None), P('fsdp', None), P('fsdp', None), P('fsdp'), P('fsdp', None), P('fsdp', 'cp', None))
    out_specs = (P('fsdp', 'cp', None), P(), P(None, 'fsdp'), P('fsdp', None, None, None), P('fsdp', None), P('fsdp', None), P('fsdp'), P('fsdp', None))
    return jax.shard_map(local_step, mesh=mesh, in_specs=in_specs, out_specs=out_specs, check_vma=False)
```

time: 2250 us -> 297 us (0.13)
  waiting for transfers between devices: 1370 us -> 0.02 us
  matrix products: 416 us -> 0 us
  Pallas kernels: 0 us -> 264 us
  blocking collectives: 167 us -> 0 us
  other arithmetic: 130 us -> 2.2 us
  local copies, waits for them, and re-layouts: 123 us -> 18.8 us
    ppermute x20 -> x6, waiting for transfers between devices: 1340 us -> 0.02 us  [the longest x3 0.01 us: local_step(): back = lax.ppermute(out_blocks[k], 'cp', shift(-k)) if k else out_blocks[0]]
    dot_general x42 -> x0, matrix products: 416 us -> none  [the longest x8 71.5 us: block_scores(): jnp.einsum('bqhd,bkhd->bhqk', q_rot, k_blk, preferred_element_type=jnp.fl...]
    pallas_call x0 -> x5, Pallas kernels: none -> 264 us  [the longest x1 72.5 us: local_step(): call(functools.partial(fwd_kernel, cp_size, seq_loc), n_seq, [SMEM, SMEM,...]
    psum x3 -> x0, blocking collectives: 67.5 us -> none  [the longest x1 41.1 us: local_step(): lax.psum(d_table, ('cp', 'fsdp'))]
    reduce_sum x12 -> x0, other arithmetic: 64.9 us -> none  [the longest x4 47 us: fwd_block(): run_sum = run_sum * rescale + jnp.sum(weights, axis=-1)]
    all_gather x5 -> x0, blocking collectives: 62.6 us -> none  [the longest x1 21.2 us: local_step(): qkv_w = lax.all_gather(w_qkv, 'fsdp', axis=0, tiled=True)]
    while x51 -> x0, local copies, waits for them, and re-layouts: 47.1 us -> none
    unnamed x147 -> x40, local copies, waits for them, and re-layouts: 53.1 us -> 7.53 us
  transfers between devices with their start and end apart: 25 -> 6, of which waited for: 16 -> 0; matrix products, arithmetic and copies ran while one was open for 22% -> 4% of each run, Pallas kernels for 0% -> 89%
where the time goes in v1:
time: 297 us
  Pallas kernels  264 us (89%)
  local copies, waits for them, and re-layouts  18.8 us (6%)
  starting transfers between devices  10.3 us (3%)
    pallas_call x1, Pallas kernels, local_step(): call(functools.partial(fwd_kernel, cp_size, seq_loc), n_seq, [SMEM, SMEM,...  72.5 us
    pallas_call x1, Pallas kernels, reduce_call(): pl.pallas_call(functools.partial(reduce_kernel, cp_size, specs), out_shap...  71.8 us
    pallas_call x1, Pallas kernels, local_step(): call(functools.partial(attn_bwd_kernel, n_seq, cp_size, seq_loc), n_seq,...  63.4 us
    pallas_call x1, Pallas kernels, gather_call(): pl.pallas_call(functools.partial(gather_kernel, cp_size, n_arr), out_shap...  33.1 us
    pallas_call x1, Pallas kernels, local_step(): call(functools.partial(ffn_bwd_kernel, n_seq, seq_loc), n_seq, [blk_spec]...  23.6 us
    unnamed x40, local copies, waits for them, and re-layouts  7.53 us
    ppermute x3, starting transfers between devices, to_whole(): blocks.append(lax.ppermute(blk, 'cp', shift(k)) if k else blk)  7.02 us
  transfers between devices with their start and end apart: 6, of which 0 were waited for; matrix products, arithmetic and copies ran while one was open for 4% of the time, Pallas kernels for 89%

profile of v1, /device:TPU:0, one launch (start us, length us, event | category | flops | bytes accessed | tf_op | source)
XLA Modules:
  0.0 296.8 jit_solution(6905301053451102109)
XLA Ops:
  0.8 2.7 constant_dynamic-slice_fusion.1
  3.4 3.1 %collective-permute-start.3 = (bf16[8,64,320]{2,1,0:T(8,128)(2,1)}, bf16[8,64,320]{2,1,0:T(8,128)(2,1)}, u32[]{:S(2)}, u32[]{:S(2)}) collective-permute-start(bf16[8,64,320]{2,1,0:T(8,128)(2,1)} %get-tuple-element.95), channel_id=1, source_target_pairs={{0,8},{8,16},{16,24},{24,0},{1,9},{9,17},{17,25},{25,1},{2,10},{10... | collective-permute-start | bytes 983048 | tf_op jit(solution)/shard_map/ppermute | solution.py:593
  6.5 2.6 collective-permute-start.4
  9.1 1.3 collective-permute-start.5
  10.5 0.1 copy.22.refs_0_
  10.6 0.1 reshape.99
  10.8 33.1 %gather.1 = (bf16[8,40,960]{2,1,0:T(8,128)(2,1)S(1)}, bf16[8,40,320]{2,1,0:T(8,128)(2,1)S(1)}, bf16[8,40,1280]{2,1,0:T(8,128)(2,1)S(1)}, bf16[8,160,320]{2,1,0:T...) custom-call(bf16[40,960]{1,0:T(8,128)(2,1)S(1)} %copy.22.refs_0_, bf16[40,320]{1,0:T(8,128)(2,1)S(1)} %copy-done.5, ...), custom_call_target="tpu_custom_call" | custom-call | tf_op jit(solution)/shard_map/gather/pallas_call | solution.py:447
  43.9 0.9 copy-done.7
  44.8 0.9 copy-done.8
  45.7 0.8 copy-done.9
  46.6 0.7 copy-done.10
  47.3 0.6 copy-done.11
  47.9 0.7 reshape.101.tok_ref
  48.6 0.1 copy.24
  48.7 0.7 pad_bitcast_fusion.emb_ref
  49.4 0.6 dynamic_slice.21.len_ref
  50.0 0.7 multiply_sine_fusion
  50.7 72.5 %fwd.1 = (bf16[8,64,320]{2,1,0:T(8,128)(2,1)}, bf16[8,64,320]{2,1,0:T(8,128)(2,1)}, bf16[8,64,320]{2,1,0:T(8,128)(2,1)}, bf16[8,64,320]{2,1,0:T(8,128)(2,1)}, bf...) custom-call(s32[8]{0:T(128)} %dynamic_slice.21.len_ref, ...), custom_call_target="tpu_custom_call" | custom-call | flops 8999999488 | bytes 50000000 | tf_op jit(solution)/shard_map/fwd/pallas_call | solution.py:614
  123.2 0.0 copy-start.13
  123.2 2.0 collective-permute-start
  125.2 0.1 collective-permute-start.1
  125.4 0.2 broadcast_in_dim.2
  125.6 0.1 constant_dynamic-update-slice_fusion.3
  125.7 1.2 collective-permute-start.2
  126.9 23.6 %ffn_bwd.1 = (f32[8,320,256]{2,1,0:T(8,128)}, f32[8,320,256]{2,1,0:T(8,128)}, f32[1280,320]{1,0:T(8,128)}, f32[320,1664]{1,0:T(8,128)}, f32[1,1280]{1,0:T(1,128)}, /*index=5*/f32[8,384]{1,0:T(8,128)}) custom-call(bf16[8,64,320]{2,1,0:T(8,128)(2,1)} %get-tuple-element.96.g0_ref, bf16[8,64,320]{2,1,0:T(8,128)(2,1)} %collective-permute-done.3.g1_ref, ...), custom_call_target="tpu_custom_call" | custom-call | flops 8999999488 | bytes 50000000 | tf_op jit(solution)/shard_map/ffn_bwd/pallas_call | solution.py:625
  150.5 0.7 reduce.1
  151.2 0.1 reshape.107
  151.3 0.7 slice.33
  152.0 63.4 %attn_bwd.1 = (f32[320,512]{1,0:T(8,128)}, f32[320,512]{1,0:T(8,128)}, f32[128,320]{1,0:T(8,128)}, f32[8,384]{1,0:T(8,128)}) custom-call(s32[8]{0:T(128)} %dynamic_slice.21.len_ref, s32[1]{0:T(128)} %bitcast.me_ref, s32[8,1,256]{2,1,0:T(1,128)} %reshape.101.tok_ref, f32[320,16]{1,0:T(8,128)} %get-tuple-element.57.vec_ref, ...), custom_call_target="tpu_custom_call" | custom-call | flops 8999999488 | bytes 50000000 | tf_op jit(solution)/shard_map/attn_bwd/pallas_call | solution.py:634
  215.4 0.8 slice.31
  216.2 0.7 select_maximum_fusion.refs_4_
  217.0 1.1 copy-done.1
  218.1 1.1 copy-done.2
  219.1 71.8 %reduce.2 = (f32[160,320]{1,0:T(8,128)S(1)}, f32[40,1664]{1,0:T(8,128)S(1)}, f32[40,512]{1,0:T(8,128)S(1)}, f32[40,512]{1,0:T(8,128)S(1)}, f32[48,384]{1,0:T(8,128)S(1)}) custom-call(f32[8,160,320]{2,1,0:T(8,128)S(1)} %bitcast.13, f32[8,40,1664]{2,1,0:T(8,128)} %bitcast.20, f32[8,40,512]{2,1,0:T(8,128)S(1)} %bitcast.14, f32[8,40,512]{2,1,0:T(8,128)S(1)} %bitcast.15, ...), custom_call_target="tpu_custom_call" | custom-call | tf_op jit(solution)/shard_map/reduce/pallas_call | solution.py:566
  291.0 0.6 slice.34
  291.6 0.6 slice.37
  292.2 0.7 slice.38
  293.0 1.0 copy.25
  293.9 0.1 reshape.109
  294.0 0.6 dynamic_slice.27
  294.7 0.7 constant_dynamic-slice_fusion
  295.3 0.0 collective-permute-done
  295.3 0.1 constant_dynamic-update-slice_fusion.2
  295.4 0.1 constant_dynamic-update-slice_fusion.1
  295.5 0.1 constant_dynamic-update-slice_fusion
  295.6 0.0 copy-start.12
  295.6 0.7 copy.31
  296.3 0.5 copy-done.12
  (40 shorter events, 0.1 us)
Async XLA Ops:
  0.7 9.8 %copy-start.14 = (bf16[40,3,20,16]{0,3,2,1:T(8,128)(2,1)S(1)}, bf16[40,3,20,16]{0,3,2,1:T(8,128)(2,1)}, u32[]{:S(2)}) copy-start(bf16[40,3,20,16]{0,3,2,1:T(8,128)(2,1)} %param.14) | copy-start | bytes 230404
  0.7 9.9 %copy-start.17 = (f32[160]{0:T(256)S(1)}, f32[160]{0:T(256)}, u32[]{:S(2)}) copy-start(f32[160]{0:T(256)} %param.17) | copy-start | bytes 1924
  0.7 10.0 %copy-start.16 = (f32[9,40]{1,0:T(8,128)S(1)}, f32[9,40]{1,0:T(8,128)}, u32[]{:S(2)}) copy-start(f32[9,40]{1,0:T(8,128)} %param.13) | copy-start | bytes 4324
  0.7 10.0 %copy-start.3 = (bf16[160,320]{1,0:T(8,128)(2,1)S(1)}, bf16[160,320]{1,0:T(8,128)(2,1)}, u32[]{:S(2)}) copy-start(bf16[160,320]{1,0:T(8,128)(2,1)} %refs_3_.1) | copy-start | bytes 307204
  0.7 10.0 %copy-start.4 = (bf16[40,1280]{1,0:T(8,128)(2,1)S(1)}, bf16[40,1280]{1,0:T(8,128)(2,1)}, u32[]{:S(2)}) copy-start(bf16[40,1280]{1,0:T(8,128)(2,1)} %refs_2_.1) | copy-start | bytes 307204
  0.7 10.0 %copy-start.5 = (bf16[40,320]{1,0:T(8,128)(2,1)S(1)}, bf16[40,320]{1,0:T(8,128)(2,1)}, u32[]{:S(2)}) copy-start(bf16[40,320]{1,0:T(8,128)(2,1)} %refs_1_.1) | copy-start | bytes 76804
  0.8 10.0 %copy-start.6 = (s32[32,64]{1,0:T(8,128)S(1)}, s32[32,64]{1,0:T(8,128)}, u32[]{:S(2)}) copy-start(s32[32,64]{1,0:T(8,128)} %param.10) | copy-start | bytes 24580
  0.8 47.8 %copy-start.15 = (bf16[33,320]{1,0:T(8,128)(2,1)S(1)}, bf16[33,320]{1,0:T(8,128)(2,1)}, u32[]{:S(2)}) copy-start(bf16[33,320]{1,0:T(8,128)(2,1)} %param.12) | copy-start | bytes 63364
  0.8 48.6 %copy-start.18 = (s32[32]{0:T(128)S(1)}, s32[32]{0:T(128)}, u32[]{:S(2)}) copy-start(s32[32]{0:T(128)} %param.11) | copy-start | bytes 388
  3.4 122.2 %collective-permute-start.3 = (bf16[8,64,320]{2,1,0:T(8,128)(2,1)}, bf16[8,64,320]{2,1,0:T(8,128)(2,1)}, u32[]{:S(2)}, u32[]{:S(2)}) collective-permute-start(bf16[8,64,320]{2,1,0:T(8,128)(2,1)} %get-tuple-element.95), channel_id=1, source_target_pairs={{0,8},{8,16},{16,24},{24,0},{1,9},{9,17},{17,25},{25,1},{2,10},{10... | collective-permute-start | bytes 983048 | tf_op jit(solution)/shard_map/ppermute | solution.py:593
  6.5 120.3 %collective-permute-start.4 = (bf16[8,64,320]{2,1,0:T(8,128)(2,1)}, bf16[8,64,320]{2,1,0:T(8,128)(2,1)}, u32[]{:S(2)}, u32[]{:S(2)}) collective-permute-start(bf16[8,64,320]{2,1,0:T(8,128)(2,1)} %get-tuple-element.97), channel_id=1, source_target_pairs={{0,16},{8,24},{16,0},{24,8},{1,17},{9,25},{17,1},{25,9},{2,18},{10... | collective-permute-start | bytes 983048 | tf_op jit(solution)/shard_map/ppermute | solution.py:593
  9.1 117.8 %collective-permute-start.5 = (bf16[8,64,320]{2,1,0:T(8,128)(2,1)S(1)}, bf16[8,64,320]{2,1,0:T(8,128)(2,1)}, u32[]{:S(2)}, u32[]{:S(2)}) collective-permute-start(bf16[8,64,320]{2,1,0:T(8,128)(2,1)S(1)} %get-tuple-element.94), channel_id=1, source_target_pairs={{0,24},{8,0},{16,8},{24,16},{1,25},{9,1},{17,9},{25,17},{2,26},{10... | collective-permute-start | bytes 983048 | tf_op jit(solution)/shard_map/ppermute | solution.py:593
  43.9 0.9 copy-start.7
  44.8 0.9 copy-start.8
  45.7 0.8 copy-start.9
  46.6 0.7 copy-start.10
  47.3 0.6 copy-start.11
  123.2 2.4 copy-start.13
  123.2 172.1 %collective-permute-start = (bf16[8,64,320]{2,1,0:T(8,128)(2,1)}, bf16[8,64,320]{2,1,0:T(8,128)(2,1)S(1)}, u32[]{:S(2)}, u32[]{:S(2)}) collective-permute-start(bf16[8,64,320]{2,1,0:T(8,128)(2,1)} %get-tuple-element.54), channel_id=1, source_target_pairs={{0,24},{8,0},{16,8},{24,16},{1,25},{9,1},{17,9},{25,17},{2,26},{10... | collective-permute-start | bytes 983048 | tf_op jit(solution)/shard_map/ppermute | solution.py:646
  125.2 170.2 %collective-permute-start.1 = (bf16[8,64,320]{2,1,0:T(8,128)(2,1)}, bf16[8,64,320]{2,1,0:T(8,128)(2,1)S(1)}, u32[]{:S(2)}, u32[]{:S(2)}) collective-permute-start(bf16[8,64,320]{2,1,0:T(8,128)(2,1)} %get-tuple-element.55), channel_id=1, source_target_pairs={{0,16},{8,24},{16,0},{24,8},{1,17},{9,25},{17,1},{25,9},{2,18},{10... | collective-permute-start | bytes 983048 | tf_op jit(solution)/shard_map/ppermute | solution.py:646
  125.7 169.8 %collective-permute-start.2 = (bf16[8,64,320]{2,1,0:T(8,128)(2,1)}, bf16[8,64,320]{2,1,0:T(8,128)(2,1)S(1)}, u32[]{:S(2)}, u32[]{:S(2)}) collective-permute-start(bf16[8,64,320]{2,1,0:T(8,128)(2,1)} %get-tuple-element.56), channel_id=1, source_target_pairs={{0,8},{8,16},{16,24},{24,0},{1,9},{9,17},{17,25},{25,1},{2,10},{10... | collective-permute-start | bytes 983048 | tf_op jit(solution)/shard_map/ppermute | solution.py:646
  152.0 64.9 %copy-start = (f32[1280,320]{1,0:T(8,128)S(1)}, f32[1280,320]{1,0:T(8,128)}, u32[]{:S(2)}) copy-start(f32[1280,320]{1,0:T(8,128)} %get-tuple-element.66) | copy-start | bytes 4915204
  217.0 1.1 copy-start.1
  218.1 1.1 copy-start.2
  295.6 1.2 copy-start.12

commit v2 on v1

--- a/solution.py
+++ b/solution.py
@@ -219,7 +219,7 @@
 
 
 def ffn_bwd_kernel(n_steps, seq_loc, g0_ref, g1_ref, g2_ref, g3_ref, vec_ref, wdown_ref, wup_ref, wout_ref, gelu_ref, dgelu_ref, a_ref, xhat2_ref, stat_ref, attn_ref,
-                   dres_ref, dattn_ref, dwdown_ref, dwuo_ref, dbup_ref, dvec_ref,
+                   dres_ref, dattn_ref, dwdown_ref, dwuo_ref, dvec_ref,
                    acc_bup, acc_vec):
     step = pl.program_id(0)
 
@@ -259,28 +259,39 @@
 
     @pl.when(step == n_steps - 1)
     def _():
-        dbup_ref[...] = row_sum(acc_bup[...])
-        dvec_ref[...] = jnp.concatenate([row_sum(pad_rows(acc_vec[j])) for j in range(4)] + [jnp.zeros((4, N_TILES * LANES), F32)], axis=0)
+        rows = [row_sum(pad_rows(acc_vec[j])) for j in range(4)] + [row_sum(pad_rows(acc_bup[j * D:(j + 1) * D])) for j in range(F // D)]
+        dvec_ref[...] = jnp.concatenate(rows, axis=0)
 
 
 def pad_rows(z):
     return jnp.concatenate([z, jnp.zeros((N_TILES * LANES - D, LANES), F32)], axis=0)
 
 
-def attn_bwd_kernel(n_steps, cp_size, seq_loc, len_ref, me_ref, tok_ref, vec_ref, wqkv_ref, cos_ref, sin_ref, qkv_ref, lse_ref, attn_ref, dattn_ref, dres_ref, xhat1_ref, h_ref, stat_ref,
-                    dwqa_ref, dwqb_ref, demb_ref, dvec_ref,
-                    k_tm, v_tm, q_pad, do_pad, bias, dq_s, dk_s, dv_s, acc_b, acc_vec):
+def attn_bwd_kernel(n_steps, cp_size, seq_loc, len_ref, me_ref, tok_ref, vec_ref, wqkv_ref, cos_ref, sin_ref, qkv_ref, lse_ref, attn_ref, dattn_ref, dres_ref, xhat1_ref, h_ref, stat_ref, dwdown_ref, dwuo_ref, dvec2_ref,
+                    rdown_ref, ruo_ref, rqa_ref, rqb_ref, rsmall_ref,
+                    k_tm, v_tm, q_pad, do_pad, bias, dq_s, dk_s, dv_s, acc_b, acc_vec, acc_qa, acc_qb, acc_emb, *red):
     step = pl.program_id(0)
+    summer = GradSum(cp_size, (dwdown_ref, dwuo_ref, acc_qa, acc_qb), (rdown_ref, ruo_ref, rqa_ref, rqb_ref), rsmall_ref, red)
 
     @pl.when(step == 0)
     def _():
-        dwqa_ref[...] = jnp.zeros_like(dwqa_ref)
-        dwqb_ref[...] = jnp.zeros_like(dwqb_ref)
-        demb_ref[...] = jnp.zeros_like(demb_ref)
+        summer.enter()
+        for i in (0, 1):
+            summer.start(0, i)
+        acc_qa[...] = jnp.zeros_like(acc_qa)
+        acc_qb[...] = jnp.zeros_like(acc_qb)
+        acc_emb[...] = jnp.zeros_like(acc_emb)
         acc_b[...] = jnp.zeros_like(acc_b)
         acc_vec[...] = jnp.zeros_like(acc_vec)
         q_pad[...] = jnp.zeros_like(q_pad)
         do_pad[...] = jnp.zeros_like(do_pad)
+
+    for phase, at in enumerate(PHASE_STEPS):
+        @pl.when(step == at)
+        def _(phase=phase):
+            for i in (0, 1):
+                summer.finish(phase, i)
+                summer.start(phase + 1, i)
 
     length = len_ref[step]
     me = me_ref[0]
@@ -324,45 +335,46 @@
         acc_b[j] += lane_part(dz)
         parts.append(dz.astype(BF))
     dz_b = jnp.concatenate(parts, axis=0)
-    dwqa_ref[...] += dot(h, dz_b[:QKV_HALF], NT)
-    dwqb_ref[:, :3 * D - QKV_HALF] += dot(h, dz_b[QKV_HALF:], NT)
+    acc_qa[...] += dot(h, dz_b[:QKV_HALF], NT).reshape(acc_qa.shape)
+    acc_qb[:, :, :3 * D - QKV_HALF] += dot(h, dz_b[QKV_HALF:], NT).reshape(acc_qb.shape[0], acc_qb.shape[1], 3 * D - QKV_HALF)
     dn1 = dot(wqkv_ref[...], dz_b)
     xhat1 = xhat1_ref[0]
     acc_vec[0] += lane_part(dn1 * xhat1)
     acc_vec[1] += lane_part(dn1)
     de = dres_ref[0] + ln_grad(dn1, xhat1, stat_ref[0, 0:1], col(vecs, 0))
     de = (de * stat_ref[0, 2:3]).astype(BF)
-    demb_ref[...] += dot(one_hot_rows(tok_ref[0]), de, NT)
+    acc_emb[...] += dot(one_hot_rows(tok_ref[0]), de, NT)
 
     @pl.when(step == n_steps - 1)
     def _():
+        for i in (2, 3):
+            summer.start(0, i)
         rows = [row_sum(pad_rows(acc_vec[j])) for j in range(2)] + [row_sum(pad_rows(acc_b[j])) for j in range(3)]
-        dvec_ref[...] = jnp.concatenate(rows + [jnp.zeros((3, N_TILES * LANES), F32)], axis=0)
-
-
-def per_seq(*shape):
-    return pl.BlockSpec((1,) + shape, lambda b: (b,) + (0,) * len(shape))
-
-
-def whole(*shape):
-    return pl.BlockSpec(shape, lambda b: (0,) * len(shape))
-
-
-SMEM = pl.BlockSpec(memory_space=pltpu.SMEM)
-
-
-def sds(shape, dtype):
-    return jax.ShapeDtypeStruct(shape, dtype)
-
-
-def call(kernel, grid, in_specs, out_specs, out_shape, scratch, flops, name):
-    return pl.pallas_call(
-        kernel, grid=(grid,), in_specs=in_specs, out_specs=out_specs, out_shape=out_shape, scratch_shapes=scratch, name=name,
-        cost_estimate=pl.CostEstimate(flops=flops, bytes_accessed=50_000_000, transcendentals=10_000_000),
-        compiler_params=pltpu.CompilerParams(dimension_semantics=('arbitrary',), vmem_limit_bytes=58 * 1024 * 1024))
+        small = summer.small
+        small[0:EMB_ROWS, 0:D] = acc_emb[0:EMB_ROWS]
+        small[0:EMB_ROWS, D:] = jnp.zeros((EMB_ROWS, N_TILES * LANES - D), F32)
+        small[EMB_ROWS:EMB_ROWS + 8] = jnp.concatenate(rows + [jnp.zeros((3, N_TILES * LANES), F32)], axis=0)
+        small[EMB_ROWS + 8:EMB_ROWS + 16] = dvec2_ref[...]
+        small[EMB_ROWS + 16:SMALL_ROWS] = jnp.zeros((SMALL_ROWS - EMB_ROWS - 16, N_TILES * LANES), F32)
+        summer.start_small(0)
+        for phase in range(5):
+            for i in (2, 3):
+                summer.finish(phase, i)
+                if phase < 4:
+                    summer.start(phase + 1, i)
+            summer.finish_small(phase)
+            if phase < 4:
+                summer.start_small(phase + 1)
+        for i in (0, 1):
+            summer.finish(4, i)
 
 
 MESH = pl.DeviceIdType.MESH
+EMB_ROWS = 40
+SMALL_ROWS = 64
+PHASE_STEPS = (1, 3, 4, 6)
+STREAMS = (('xy', (0, 40, 40)), ('yx', (1, 512, 384)), ('xy', (1, 128, 128)), ('yx', (1, 128, 128)))
+SMALL_SPEC = (0, SMALL_ROWS // 4, SMALL_ROWS // 4)
 
 
 def place(fs):
@@ -382,6 +394,137 @@
 
 def remote(src, dst, send_sem, recv_sem, peer):
     return pltpu.make_async_remote_copy(src_ref=src, dst_ref=dst, send_sem=send_sem, recv_sem=recv_sem, device_id=peer, device_id_type=MESH)
+
+
+def piece_of(ref, spec, p):
+    axis, size, stride = spec
+    start = pl.multiple_of(p * stride, stride)
+    return ref.at[pl.ds(start, size), :] if axis == 0 else ref.at[:, pl.ds(start, size)]
+
+
+class GradSum:
+    def __init__(self, cp_size, big, outs, small_out, refs):
+        n = len(STREAMS)
+        self.cp_size, self.big, self.outs, self.small_out = cp_size, big, outs, small_out
+        self.r0, self.acc, self.r1, self.r2, self.rz, self.rg = (refs[i * n:(i + 1) * n] for i in range(6))
+        self.small, self.er, self.ez, self.eg = refs[6 * n:6 * n + 4]
+        sems = refs[6 * n + 4:]
+        self.sends, self.recvs = sems[0:5], sems[5:10]
+        self.small_send, self.small_recv = sems[10], sems[11]
+        self.me = lax.axis_index('cp')
+        self.fs = lax.axis_index('fsdp')
+        self.y, self.x, self.c = place(self.fs)
+        fs, y, x, c = self.fs, self.y, self.x, self.c
+        self.cps = [lax.rem(self.me + k, cp_size) for k in range(1, cp_size)]
+        self.hops = [device(self.me, f) for f in (fs + 1 - 2 * c, fs + 2 - 4 * x, fs + 4 - 8 * y)]
+        self.peers = [device(z, fs) for z in self.cps]
+
+    def enter(self):
+        enter(self.hops + self.peers)
+
+    def copies(self, phase, i):
+        path, spec = STREAMS[i]
+        xy = path == 'xy'
+        s, v = self.sends[phase], self.recvs[phase]
+        x, y, c, me = self.x, self.y, self.c, self.me
+        if phase == 0:
+            return [remote(self.big[i].at[2 * j + 1 - c], self.r0[i].at[j], s.at[i, j], v.at[i, j], self.hops[0]) for j in range(4)]
+        if phase == 1:
+            give = [2 * k + 1 - x if xy else 2 * (1 - y) + k for k in range(2)]
+            return [remote(self.acc[i].at[give[k]], self.r1[i].at[k], s.at[i, k], v.at[i, k], self.hops[1 if xy else 2]) for k in range(2)]
+        if phase == 2:
+            return [remote(self.r1[i].at[1 - y if xy else 1 - x], self.r2[i], s.at[i, 0], v.at[i, 0], self.hops[2 if xy else 1])]
+        if phase == 3:
+            return [remote(piece_of(self.outs[i], spec, self.cps[k]), self.rz[i].at[k], s.at[i, k], v.at[i, k], self.peers[k]) for k in range(self.cp_size - 1)]
+        return [remote(self.rg[i].at[me], self.rg[i].at[me], s.at[i, k], v.at[i, k], self.peers[k]) for k in range(self.cp_size - 1)]
+
+    def start(self, phase, i):
+        for copy in self.copies(phase, i):
+            copy.start()
+
+    def finish(self, phase, i):
+        for copy in self.copies(phase, i):
+            copy.wait()
+        path, spec = STREAMS[i]
+        xy = path == 'xy'
+        big, r0, acc, r1, r2, out = self.big[i], self.r0[i], self.acc[i], self.r1[i], self.r2[i], self.outs[i]
+        rz, rg = self.rz[i], self.rg[i]
+        if phase == 0:
+            for j in range(4):
+                acc[j] = big[2 * j + self.c] + r0[j]
+        elif phase == 1:
+            for k in range(2):
+                r1[k] = acc[2 * k + self.x if xy else 2 * self.y + k] + r1[k]
+        elif phase == 2:
+            out[...] = r1[self.y if xy else self.x] + r2[...]
+        elif phase == 3:
+            rg[self.me] = ((piece_of(out, spec, self.me)[...] + rz[0]) + rz[1]) + rz[2]
+        else:
+            axis, size, stride = spec
+            for p in range(self.cp_size):
+                lo = p * stride
+                if axis == 0:
+                    out[lo:lo + size, :] = rg[p]
+                else:
+                    out[:, lo:lo + size] = rg[p]
+
+    def small_copies(self, phase):
+        s, v = self.small_send, self.small_recv
+        if phase < 3:
+            return [remote(self.small, self.er.at[phase], s.at[phase], v.at[phase], self.hops[phase])]
+        if phase == 3:
+            return [remote(piece_of(self.small, SMALL_SPEC, self.cps[k]), self.ez.at[k], s.at[3 + k], v.at[3 + k], self.peers[k]) for k in range(self.cp_size - 1)]
+        return [remote(self.eg.at[self.me], self.eg.at[self.me], s.at[6 + k], v.at[6 + k], self.peers[k]) for k in range(self.cp_size - 1)]
+
+    def start_small(self, phase):
+        for copy in self.small_copies(phase):
+            copy.start()
+
+    def finish_small(self, phase):
+        for copy in self.small_copies(phase):
+            copy.wait()
+        if phase < 3:
+            self.small[...] += self.er[phase]
+        elif phase == 3:
+            self.eg[self.me] = ((piece_of(self.small, SMALL_SPEC, self.me)[...] + self.ez[0]) + self.ez[1]) + self.ez[2]
+        else:
+            size = SMALL_SPEC[1]
+            for p in range(self.cp_size):
+                self.small_out[p * size:(p + 1) * size, :] = self.eg[p]
+
+
+def sum_scratch(cp_size, shapes, small_shape):
+    dma = pltpu.SemaphoreType.DMA
+    n = len(shapes)
+    cut = [((size, sh[1]) if axis == 0 else (sh[0], size)) for sh, (_, (axis, size, _)) in zip(shapes, STREAMS)]
+    lanes = small_shape[1]
+    scratch = [pltpu.VMEM((4,) + sh, F32) for sh in shapes] * 2 + [pltpu.VMEM((2,) + sh, F32) for sh in shapes] + [pltpu.VMEM(sh, F32) for sh in shapes]
+    scratch += [pltpu.VMEM((cp_size - 1,) + sh, F32) for sh in cut] + [pltpu.VMEM((cp_size,) + sh, F32) for sh in cut]
+    scratch += [pltpu.VMEM(small_shape, F32), pltpu.VMEM((3,) + small_shape, F32), pltpu.VMEM((cp_size - 1, SMALL_SPEC[1], lanes), F32), pltpu.VMEM((cp_size, SMALL_SPEC[1], lanes), F32)]
+    scratch += [dma(shape) for shape in ((n, 4), (n, 2), (n, 1), (n, cp_size - 1), (n, cp_size - 1))] * 2 + [dma((3 + 2 * (cp_size - 1),))] * 2
+    return scratch
+
+
+def per_seq(*shape):
+    return pl.BlockSpec((1,) + shape, lambda b: (b,) + (0,) * len(shape))
+
+
+def whole(*shape):
+    return pl.BlockSpec(shape, lambda b: (0,) * len(shape))
+
+
+SMEM = pl.BlockSpec(memory_space=pltpu.SMEM)
+
+
+def sds(shape, dtype):
+    return jax.ShapeDtypeStruct(shape, dtype)
+
+
+def call(kernel, grid, in_specs, out_specs, out_shape, scratch, flops, name, **params):
+    return pl.pallas_call(
+        kernel, grid=(grid,), in_specs=in_specs, out_specs=out_specs, out_shape=out_shape, scratch_shapes=scratch, name=name,
+        cost_estimate=pl.CostEstimate(flops=flops, bytes_accessed=50_000_000, transcendentals=10_000_000),
+        compiler_params=pltpu.CompilerParams(dimension_semantics=('arbitrary',), vmem_limit_bytes=58 * 1024 * 1024, **params))
 
 
 def gather_kernel(cp_size, n_arr, *refs):
@@ -454,124 +597,6 @@
     )(*arrays, tok)
 
 
-def piece_of(ref, spec, p):
-    axis, size, stride = spec
-    start = pl.multiple_of(p * stride, stride)
-    return ref.at[pl.ds(start, size), :] if axis == 0 else ref.at[:, pl.ds(start, size)]
-
-
-def reduce_kernel(cp_size, specs, *refs):
-    n = len(specs)
-    big, small = refs[:n], refs[n]
-    outs, small_out = refs[n + 1:2 * n + 1], refs[2 * n + 1]
-    rest = refs[2 * n + 2:]
-    r0, acc, r1, r2, rz, rg = (rest[i * n:(i + 1) * n] for i in range(6))
-    es, er, ez, s0, v0, s1, v1, s2, v2, sz, vz, sg, vg, se, ve, sez, vez = rest[6 * n:]
-    me = lax.axis_index('cp')
-    fs = lax.axis_index('fsdp')
-    y, x, c = place(fs)
-    near, xn, yn = fs + 1 - 2 * c, fs + 2 - 4 * x, fs + 4 - 8 * y
-    cps = [lax.rem(me + k, cp_size) for k in range(1, cp_size)]
-    hops = (device(me, near), device(me, xn), device(me, yn))
-    enter(list(hops) + [device(z, fs) for z in cps])
-
-    def start(copies):
-        for copy in copies:
-            copy.start()
-
-    def finish(copies):
-        for copy in copies:
-            copy.wait()
-
-    def small_hop(i, src):
-        copy = remote(src, er.at[i], se.at[i], ve.at[i], hops[i])
-        copy.start()
-        return copy
-
-    first = [[remote(b.at[2 * j + 1 - c], r0[i].at[j], s0.at[i, j], v0.at[i, j], hops[0]) for j in range(4)] for i, b in enumerate(big)]
-    for group in first:
-        start(group)
-    hop = small_hop(0, small)
-    second = []
-    for i, (path, _) in enumerate(specs):
-        finish(first[i])
-        for j in range(4):
-            acc[i][j] = big[i][2 * j + c] + r0[i][j]
-        group = []
-        for k in range(2):
-            give = 2 * k + 1 - x if path == 'xy' else 2 * (1 - y) + k
-            group.append(remote(acc[i].at[give], r1[i].at[k], s1.at[i, k], v1.at[i, k], hops[1] if path == 'xy' else hops[2]))
-        start(group)
-        second.append(group)
-    hop.wait()
-    es[0] = small[...] + er[0]
-    hop = small_hop(1, es.at[0])
-    third = []
-    for i, (path, _) in enumerate(specs):
-        finish(second[i])
-        for k in range(2):
-            keep = 2 * k + x if path == 'xy' else 2 * y + k
-            r1[i][k] = acc[i][keep] + r1[i][k]
-        give = 1 - y if path == 'xy' else 1 - x
-        copy = remote(r1[i].at[give], r2[i], s2.at[i], v2.at[i], hops[2] if path == 'xy' else hops[1])
-        copy.start()
-        third.append(copy)
-    hop.wait()
-    es[1] = es[0] + er[1]
-    hop = small_hop(2, es.at[1])
-    fourth = []
-    for i, (path, spec) in enumerate(specs):
-        third[i].wait()
-        keep = y if path == 'xy' else x
-        outs[i][...] = r1[i][keep] + r2[i][...]
-        group = [remote(piece_of(outs[i], spec, cps[k]), rz[i].at[k], sz.at[i, k], vz.at[i, k], device(cps[k], fs)) for k in range(cp_size - 1)]
-        start(group)
-        fourth.append(group)
-    hop.wait()
-    ez[me] = es[1] + er[2]
-    last = [remote(ez.at[me], ez.at[me], sez.at[k], vez.at[k], device(cps[k], fs)) for k in range(cp_size - 1)]
-    start(last)
-    fifth = []
-    for i, (path, spec) in enumerate(specs):
-        finish(fourth[i])
-        rg[i][me] = ((piece_of(outs[i], spec, me)[...] + rz[i][0]) + rz[i][1]) + rz[i][2]
-        group = [remote(rg[i].at[me], rg[i].at[me], sg.at[i, k], vg.at[i, k], device(cps[k], fs)) for k in range(cp_size - 1)]
-        start(group)
-        fifth.append(group)
-    finish(last)
-    small_out[...] = ((ez[0] + ez[1]) + ez[2]) + ez[3]
-    for i, (path, spec) in enumerate(specs):
-        finish(fifth[i])
-        for p in range(cp_size):
-            axis, size, stride = spec
-            lo = p * stride
-            if axis == 0:
-                outs[i][lo:lo + size, :] = rg[i][p]
-            else:
-                outs[i][:, lo:lo + size] = rg[i][p]
-
-
-def reduce_call(cp_size, arrays, small):
-    vmem = pl.BlockSpec(memory_space=pltpu.VMEM)
-    dma = pltpu.SemaphoreType.DMA
-    n = len(arrays)
-    specs = tuple((path, spec) for _, path, spec in arrays)
-    shapes = [arr.shape[1:] for arr, _, _ in arrays]
-    cut = [((size, sh[1]) if axis == 0 else (sh[0], size)) for sh, (_, (axis, size, _)) in zip(shapes, specs)]
-    scratch = [pltpu.VMEM((4,) + sh, F32) for sh in shapes] * 2 + [pltpu.VMEM((2,) + sh, F32) for sh in shapes] + [pltpu.VMEM(sh, F32) for sh in shapes]
-    scratch += [pltpu.VMEM((cp_size - 1,) + sh, F32) for sh in cut] + [pltpu.VMEM((cp_size,) + sh, F32) for sh in cut]
-    scratch += [pltpu.VMEM((2,) + small.shape, F32), pltpu.VMEM((3,) + small.shape, F32), pltpu.VMEM((cp_size,) + small.shape, F32)]
-    for shape in ((n, 4), (n, 2), (n,), (n, cp_size - 1), (n, cp_size - 1), (3,), (cp_size - 1,)):
-        scratch += [dma(shape), dma(shape)]
-    return pl.pallas_call(
-        functools.partial(reduce_kernel, cp_size, specs),
-        out_shape=[sds(sh, F32) for sh in shapes] + [sds(small.shape, F32)],
-        in_specs=[vmem] * (n + 1), out_specs=[vmem] * (n + 1), scratch_shapes=scratch,
-        compiler_params=pltpu.CompilerParams(collective_id=1, has_side_effects=True, vmem_limit_bytes=48 * 1024 * 1024),
-        name='reduce',
-    )(*[arr for arr, _, _ in arrays], small)
-
-
 def solution(mesh):
     cp_size = mesh.shape['cp']
     fs_size = mesh.shape['fsdp']
@@ -622,24 +647,29 @@
         out_blocks = outs[:4]
         h, xhat1, stat, qkv, lse, attn, xhat2, a, gelu, dgelu, vecs_t, qkv_w, out_w, up_w = outs[4:]
 
-        dres, dattn, dw_down, dw_uo, db_up, dvec2 = call(
+        dres, dattn, dw_down, dw_uo, dvec2 = call(
             functools.partial(ffn_bwd_kernel, n_seq, seq_loc), n_seq,
             [blk_spec] * 4 + [whole(D, SM_ROWS), whole(F, D), whole(D, F), whole(D, D), per_seq(F, S), per_seq(F, S), per_seq(D, S), per_seq(D, S), per_seq(8, S), per_seq(D, S)],
-            [per_seq(D, S), per_seq(D, S), whole(F, D), whole(D, UO_PAD), whole(1, F), whole(8, N_TILES * LANES)],
-            [sds((n_seq, D, S), F32), sds((n_seq, D, S), F32), sds((F, D), F32), sds((D, UO_PAD), F32), sds((1, F), F32), sds((8, N_TILES * LANES), F32)],
+            [per_seq(D, S), per_seq(D, S), whole(F, D), whole(D, UO_PAD), whole(8, N_TILES * LANES)],
+            [sds((n_seq, D, S), F32), sds((n_seq, D, S), F32), sds((F, D), F32), sds((D, UO_PAD), F32), sds((8, N_TILES * LANES), F32)],
             [pltpu.VMEM((F, LANES), F32), pltpu.VMEM((4, D, LANES), F32)],
             9_000_000_000, 'ffn_bwd',
         )(*g_blocks, vecs_t, down_w, up_w, out_w, gelu, dgelu, a, xhat2, stat, attn)
 
-        dw_qa, dw_qb, d_emb, dvec1 = call(
+        rows = D // fs_size
+        shapes = [(F // fs_size, D), (rows, UO_PAD), (rows, QKV_HALF), (rows, QKV_HALF)]
+        small_shape = (SMALL_ROWS, N_TILES * LANES)
+        acc_q = pltpu.VMEM((fs_size, rows, QKV_HALF), F32)
+        r_down, r_uo, r_qa, r_qb, packed = call(
             functools.partial(attn_bwd_kernel, n_seq, cp_size, seq_loc), n_seq,
-            [SMEM, SMEM, per_seq(1, S), whole(D, SM_ROWS), whole(D, 3 * D), whole(8, S), whole(8, S), per_seq(3 * D, S), per_seq(N_HEADS, 1, S), per_seq(D, S), per_seq(D, S), per_seq(D, S), per_seq(D, S), per_seq(D, S), per_seq(8, S)],
-            [whole(D, QKV_HALF), whole(D, QKV_HALF), whole(VOCAB_PAD, D), whole(8, N_TILES * LANES)],
-            [sds((D, QKV_HALF), F32), sds((D, QKV_HALF), F32), sds((VOCAB_PAD, D), F32), sds((8, N_TILES * LANES), F32)],
+            [SMEM, SMEM, per_seq(1, S), whole(D, SM_ROWS), whole(D, 3 * D), whole(8, S), whole(8, S), per_seq(3 * D, S), per_seq(N_HEADS, 1, S), per_seq(D, S), per_seq(D, S), per_seq(D, S), per_seq(D, S), per_seq(D, S), per_seq(8, S),
+             whole(fs_size, *shapes[0]), whole(fs_size, *shapes[1]), whole(8, N_TILES * LANES)],
+            [whole(*sh) for sh in shapes] + [whole(*small_shape)],
+            [sds(sh, F32) for sh in shapes] + [sds(small_shape, F32)],
             [pltpu.VMEM((N_TILES, S, LANES), BF), pltpu.VMEM((N_TILES, S, LANES), BF), pltpu.VMEM((N_TILES * LANES, S), BF), pltpu.VMEM((N_TILES * LANES, S), BF), pltpu.VMEM((S, S), F32),
-             pltpu.VMEM((D, S), F32), pltpu.VMEM((D, S), F32), pltpu.VMEM((D, S), F32), pltpu.VMEM((3, D, LANES), F32), pltpu.VMEM((2, D, LANES), F32)],
-            9_000_000_000, 'attn_bwd',
-        )(len_w, me_arr, tok_w, vecs_t, qkv_w, cos_t, sin_t, qkv, lse, attn, dattn, dres, xhat1, h, stat)
+             pltpu.VMEM((D, S), F32), pltpu.VMEM((D, S), F32), pltpu.VMEM((D, S), F32), pltpu.VMEM((3, D, LANES), F32), pltpu.VMEM((2, D, LANES), F32), acc_q, acc_q, pltpu.VMEM((VOCAB_PAD, D), F32)] + sum_scratch(cp_size, shapes, small_shape),
+            9_000_000_000, 'attn_bwd', collective_id=1, has_side_effects=True,
+        )(len_w, me_arr, tok_w, vecs_t, qkv_w, cos_t, sin_t, qkv, lse, attn, dattn, dres, xhat1, h, stat, dw_down.reshape(fs_size, *shapes[0]), dw_uo.reshape(fs_size, *shapes[1]), dvec2)
 
         layer_out = jnp.zeros((n_loc, seq_loc, D), BF)
         for k in range(cp_size):
@@ -647,18 +677,12 @@
             layer_out = lax.dynamic_update_slice_in_dim(layer_out, back, ((me + k) % cp_size) * n_seq, 0)
 
         vocab = embed_table.shape[0]
-        packed = jnp.concatenate([d_emb[:vocab], dvec1[:5, :D], dvec2[:4, :D], db_up.reshape(F // D, D)], axis=0)
-        packed = jnp.pad(packed, ((0, 48 - packed.shape[0]), (0, N_TILES * LANES - D)))
-
-        def pieces(arr):
-            return arr.reshape(fs_size, arr.shape[0] // fs_size, arr.shape[1])
-
-        r_down, r_uo, r_qa, r_qb, packed = reduce_call(cp_size, [(pieces(dw_down), 'xy', (0, 40, 40)), (pieces(dw_uo), 'yx', (1, 512, 384)), (pieces(dw_qa), 'xy', (1, 128, 128)), (pieces(dw_qb), 'yx', (1, 128, 128))], packed)
-        packed = packed[:, :D]
-        d_vecs = lax.dynamic_slice_in_dim(packed[vocab:vocab + 9], fs * (D // fs_size), D // fs_size, 1)
-        d_bup = lax.dynamic_slice_in_dim(packed[vocab + 9:vocab + 13].reshape(F), fs * (F // fs_size), F // fs_size, 0)
+        d_vecs = jnp.concatenate([packed[EMB_ROWS:EMB_ROWS + 5], packed[EMB_ROWS + 8:EMB_ROWS + 12]], axis=0)
+        d_vecs = lax.dynamic_slice_in_dim(d_vecs, fs * (D // fs_size), D // fs_size, 1)
+        d_bup = packed[EMB_ROWS + 12:EMB_ROWS + 16, :D].reshape(F)
+        d_bup = lax.dynamic_slice_in_dim(d_bup, fs * (F // fs_size), F // fs_size, 0)
         d_qkv = jnp.concatenate([r_qa, r_qb], axis=1)[:, :3 * D].reshape(w_qkv.shape)
-        return (layer_out, packed[:vocab], d_vecs, d_qkv, r_uo[:, F:F + D], r_uo[:, :F], d_bup, r_down)
+        return (layer_out, packed[:vocab, :D], d_vecs, d_qkv, r_uo[:, F:F + D], r_uo[:, :F], d_bup, r_down)
 
     in_specs = (P('fsdp', 'cp'), P('fsdp'), P(), P(None, 'fsdp'), P('fsdp', None, None, None), P('fsdp', None), P('fsdp', None), P('fsdp'), P('fsdp', None), P('fsdp', 'cp', None))
     out_specs = (P('fsdp', 'cp', None), P(), P(None, 'fsdp'), P('fsdp', None, None, None), P('fsdp', None), P('fsdp', None), P('fsdp'), P('fsdp', None))

time: 297 us -> 256 us (0.86)
  Pallas kernels: 264 us -> 222 us
    pallas_call x1 -> x0, Pallas kernels: 71.8 us -> none  [reduce_call(): pl.pallas_call(functools.partial(reduce_kernel, cp_size, specs), out_shap...]
    pallas_call x1, Pallas kernels: 63.4 us -> 93.2 us  [local_step(): call(functools.partial(attn_bwd_kernel, n_seq, cp_size, seq_loc), n_seq,...]
    unnamed x40 -> x36, local copies, waits for them, and re-layouts: 7.53 us -> 5.4 us
  transfers between devices with their start and end apart: 6 -> 6, of which waited for: 0 -> 0; matrix products, arithmetic and copies ran while one was open for 4% -> 5% of each run, Pallas kernels for 89% -> 87%
where the time goes in v2:
time: 256 us; the launch traced here: 255 us
  Pallas kernels  222 us (87%)
  local copies, waits for them, and re-layouts  19.1 us (7%)
  starting transfers between devices  10.3 us (4%)
    pallas_call x1, Pallas kernels, local_step(): call(functools.partial(attn_bwd_kernel, n_seq, cp_size, seq_loc), n_seq,...  93.2 us
    pallas_call x1, Pallas kernels, local_step(): call(functools.partial(fwd_kernel, cp_size, seq_loc), n_seq, [SMEM, SMEM,...  72.5 us
    pallas_call x1, Pallas kernels, gather_call(): pl.pallas_call(functools.partial(gather_kernel, cp_size, n_arr), out_shap...  33.1 us
    pallas_call x1, Pallas kernels, local_step(): call(functools.partial(ffn_bwd_kernel, n_seq, seq_loc), n_seq, [blk_spec]...  23.7 us
    ppermute x3, starting transfers between devices, to_whole(): blocks.append(lax.ppermute(blk, 'cp', shift(k)) if k else blk)  7.02 us
    unnamed x36, local copies, waits for them, and re-layouts  5.4 us
  transfers between devices with their start and end apart: 6, of which 0 were waited for; matrix products, arithmetic and copies ran while one was open for 5% of the time, Pallas kernels for 87%

profile of v2, /device:TPU:0, one launch (start us, length us, event | category | flops | bytes accessed | tf_op | source)
XLA Modules:
  0.0 255.3 jit_solution(8126734174885441923)
XLA Ops:
  0.8 2.7 %constant_dynamic-slice_fusion = (bf16[8,64,320]{2,1,0:T(8,128)(2,1)S(1)}, bf16[8,64,320]{2,1,0:T(8,128)(2,1)}, bf16[8,64,320]{2,1,0:T(8,128)(2,1)}, bf16[8,64,320]{2,1,0:T(8,128)(2,1)}) fusion(bf16[32,64,320]{2,1,0:T(8,128)(2,1)} %param.19, s32[]{:T(128)S(6)} %select_n.90, s32[]{:T(128)S(6)} %select_n.86, s32[]{:T(128)S(6)} %select_n.84, s32[]{:T(128)S(6)} %select_n.88), kind=kLoop, calls=%fused_computation.10 | loop fusion | bytes 2621456 | tf_op jit(solution)/shard_map/dynamic_slice | solution.py:617
  3.5 3.1 %collective-permute-start.3 = (bf16[8,64,320]{2,1,0:T(8,128)(2,1)}, bf16[8,64,320]{2,1,0:T(8,128)(2,1)}, u32[]{:S(2)}, u32[]{:S(2)}) collective-permute-start(bf16[8,64,320]{2,1,0:T(8,128)(2,1)} %get-tuple-element.85), channel_id=1, source_target_pairs={{0,8},{8,16},{16,24},{24,0},{1,9},{9,17},{17,25},{25,1},{2,10},{10... | collective-permute-start | bytes 983048 | tf_op jit(solution)/shard_map/ppermute | solution.py:618
  6.5 2.6 %collective-permute-start.4 = (bf16[8,64,320]{2,1,0:T(8,128)(2,1)}, bf16[8,64,320]{2,1,0:T(8,128)(2,1)}, u32[]{:S(2)}, u32[]{:S(2)}) collective-permute-start(bf16[8,64,320]{2,1,0:T(8,128)(2,1)} %get-tuple-element.87), channel_id=1, source_target_pairs={{0,16},{8,24},{16,0},{24,8},{1,17},{9,25},{17,1},{25,9},{2,18},{10... | collective-permute-start | bytes 983048 | tf_op jit(solution)/shard_map/ppermute | solution.py:618
  9.1 1.3 collective-permute-start.5
  10.5 0.1 copy.22.refs_0_
  10.7 0.1 reshape.90
  10.8 33.1 %gather.1 = (bf16[8,40,960]{2,1,0:T(8,128)(2,1)S(1)}, bf16[8,40,320]{2,1,0:T(8,128)(2,1)S(1)}, bf16[8,40,1280]{2,1,0:T(8,128)(2,1)S(1)}, bf16[8,160,320]{2,1,0:T...) custom-call(bf16[40,960]{1,0:T(8,128)(2,1)S(1)} %copy.22.refs_0_, bf16[40,320]{1,0:T(8,128)(2,1)S(1)} %copy-done.2, ...), custom_call_target="tpu_custom_call" | custom-call | tf_op jit(solution)/shard_map/gather/pallas_call | solution.py:590
  43.9 0.9 copy-done.4
  44.9 0.9 copy-done.5
  45.8 0.9 copy-done.6
  46.6 0.7 copy-done.7
  47.3 0.6 copy-done.8
  47.9 0.7 reshape.92.tok_ref
  48.6 0.1 copy.24
  48.8 0.7 pad_bitcast_fusion.emb_ref
  49.4 0.7 dynamic_slice.21.len_ref
  50.1 0.7 multiply_sine_fusion
  50.8 72.5 %fwd.1 = (bf16[8,64,320]{2,1,0:T(8,128)(2,1)}, bf16[8,64,320]{2,1,0:T(8,128)(2,1)}, bf16[8,64,320]{2,1,0:T(8,128)(2,1)}, bf16[8,64,320]{2,1,0:T(8,128)(2,1)}, bf...) custom-call(s32[8]{0:T(128)} %dynamic_slice.21.len_ref, ...), custom_call_target="tpu_custom_call" | custom-call | flops 8999999488 | bytes 50000000 | tf_op jit(solution)/shard_map/fwd/pallas_call | solution.py:639
  123.3 0.0 copy-start.10
  123.3 2.0 collective-permute-start
  125.3 0.1 collective-permute-start.1
  125.4 0.2 broadcast_in_dim.2
  125.6 0.1 constant_dynamic-update-slice_fusion.3
  125.7 0.0 collective-permute-done.3.g1_ref
  125.7 1.2 collective-permute-start.2
  126.9 0.0 collective-permute-done.4.g2_ref
  126.9 0.0 collective-permute-done.5.g3_ref
  126.9 23.7 %ffn_bwd.1 = (f32[8,320,256]{2,1,0:T(8,128)}, f32[8,320,256]{2,1,0:T(8,128)}, f32[1280,320]{1,0:T(8,128)}, f32[320,1664]{1,0:T(8,128)}, f32[8,384]{1,0:T(8,128)}) custom-call(bf16[8,64,320]{2,1,0:T(8,128)(2,1)} %get-tuple-element.86.g0_ref, bf16[8,64,320]{2,1,0:T(8,128)(2,1)} %collective-permute-done.3.g1_ref, ...), custom_call_target="tpu_custom_call" | custom-call | flops 8999999488 | bytes 50000000 | tf_op jit(solution)/shard_map/ffn_bwd/pallas_call | solution.py:650
  150.6 93.2 %attn_bwd.1 = (f32[160,320]{1,0:T(8,128)}, f32[40,1664]{1,0:T(8,128)}, f32[40,512]{1,0:T(8,128)}, f32[40,512]{1,0:T(8,128)}, f32[64,384]{1,0:T(8,128)}) custom-call(s32[8]{0:T(128)} %dynamic_slice.21.len_ref, s32[1]{0:T(128)} %bitcast.me_ref, s32[8,1,256]{2,1,0:T(1,128)} %reshape.92.tok_ref, f32[320,16]{1,0:T(8,128)} %get-tuple-element.52.vec_ref, ...), custom_call_target="tpu_custom_call" | custom-call | flops 8999999488 | bytes 50000000 | tf_op jit(solution)/shard_map/attn_bwd/pallas_call | solution.py:663
  243.8 1.5 slice.21
  245.2 0.7 slice.22
  246.0 0.7 slice.23
  246.7 1.5 slice.25
  248.1 1.6 slice.26
  249.7 0.7 slice.27
  250.5 0.9 pad_maximum_fusion
  251.4 1.0 copy.25
  252.4 0.1 reshape.97
  252.5 0.6 dynamic_slice.27
  253.1 0.7 fusion
  253.8 0.0 collective-permute-done
  253.8 0.1 constant_dynamic-update-slice_fusion.2
  253.9 0.1 constant_dynamic-update-slice_fusion.1
  253.9 0.0 collective-permute-done.2
  254.0 0.1 constant_dynamic-update-slice_fusion
  254.0 0.0 copy-start.9
  254.0 0.7 copy.31
  254.8 0.5 copy-done.9
  (31 shorter events, 0.1 us)
Async XLA Ops:
  0.7 9.8 %copy-start.11 = (bf16[40,3,20,16]{0,3,2,1:T(8,128)(2,1)S(1)}, bf16[40,3,20,16]{0,3,2,1:T(8,128)(2,1)}, u32[]{:S(2)}) copy-start(bf16[40,3,20,16]{0,3,2,1:T(8,128)(2,1)} %param.14) | copy-start | bytes 230404
  0.7 9.9 %copy-start.15 = (f32[160]{0:T(256)S(1)}, f32[160]{0:T(256)}, u32[]{:S(2)}) copy-start(f32[160]{0:T(256)} %param.17) | copy-start | bytes 1924
  0.7 10.0 %copy-start.14 = (f32[9,40]{1,0:T(8,128)S(1)}, f32[9,40]{1,0:T(8,128)}, u32[]{:S(2)}) copy-start(f32[9,40]{1,0:T(8,128)} %param.13) | copy-start | bytes 4324
  0.7 10.0 %copy-start = (bf16[160,320]{1,0:T(8,128)(2,1)S(1)}, bf16[160,320]{1,0:T(8,128)(2,1)}, u32[]{:S(2)}) copy-start(bf16[160,320]{1,0:T(8,128)(2,1)} %refs_3_.1) | copy-start | bytes 307204
  0.7 10.0 %copy-start.1 = (bf16[40,1280]{1,0:T(8,128)(2,1)S(1)}, bf16[40,1280]{1,0:T(8,128)(2,1)}, u32[]{:S(2)}) copy-start(bf16[40,1280]{1,0:T(8,128)(2,1)} %refs_2_.1) | copy-start | bytes 307204
  0.7 10.0 %copy-start.2 = (bf16[40,320]{1,0:T(8,128)(2,1)S(1)}, bf16[40,320]{1,0:T(8,128)(2,1)}, u32[]{:S(2)}) copy-start(bf16[40,320]{1,0:T(8,128)(2,1)} %refs_1_.1) | copy-start | bytes 76804
  0.8 10.0 %copy-start.3 = (s32[32,64]{1,0:T(8,128)S(1)}, s32[32,64]{1,0:T(8,128)}, u32[]{:S(2)}) copy-start(s32[32,64]{1,0:T(8,128)} %param.10) | copy-start | bytes 24580
  0.8 47.9 %copy-start.13 = (bf16[33,320]{1,0:T(8,128)(2,1)S(1)}, bf16[33,320]{1,0:T(8,128)(2,1)}, u32[]{:S(2)}) copy-start(bf16[33,320]{1,0:T(8,128)(2,1)} %param.12) | copy-start | bytes 63364
  0.8 48.6 %copy-start.16 = (s32[32]{0:T(128)S(1)}, s32[32]{0:T(128)}, u32[]{:S(2)}) copy-start(s32[32]{0:T(128)} %param.11) | copy-start | bytes 388
  3.5 122.3 %collective-permute-start.3 = (bf16[8,64,320]{2,1,0:T(8,128)(2,1)}, bf16[8,64,320]{2,1,0:T(8,128)(2,1)}, u32[]{:S(2)}, u32[]{:S(2)}) collective-permute-start(bf16[8,64,320]{2,1,0:T(8,128)(2,1)} %get-tuple-element.85), channel_id=1, source_target_pairs={{0,8},{8,16},{16,24},{24,0},{1,9},{9,17},{17,25},{25,1},{2,10},{10... | collective-permute-start | bytes 983048 | tf_op jit(solution)/shard_map/ppermute | solution.py:618
  6.5 120.4 %collective-permute-start.4 = (bf16[8,64,320]{2,1,0:T(8,128)(2,1)}, bf16[8,64,320]{2,1,0:T(8,128)(2,1)}, u32[]{:S(2)}, u32[]{:S(2)}) collective-permute-start(bf16[8,64,320]{2,1,0:T(8,128)(2,1)} %get-tuple-element.87), channel_id=1, source_target_pairs={{0,16},{8,24},{16,0},{24,8},{1,17},{9,25},{17,1},{25,9},{2,18},{10... | collective-permute-start | bytes 983048 | tf_op jit(solution)/shard_map/ppermute | solution.py:618
  9.1 117.8 %collective-permute-start.5 = (bf16[8,64,320]{2,1,0:T(8,128)(2,1)S(1)}, bf16[8,64,320]{2,1,0:T(8,128)(2,1)}, u32[]{:S(2)}, u32[]{:S(2)}) collective-permute-start(bf16[8,64,320]{2,1,0:T(8,128)(2,1)S(1)} %get-tuple-element.84), channel_id=1, source_target_pairs={{0,24},{8,0},{16,8},{24,16},{1,25},{9,1},{17,9},{25,17},{2,26},{10... | collective-permute-start | bytes 983048 | tf_op jit(solution)/shard_map/ppermute | solution.py:618
  43.9 0.9 copy-start.4
  44.9 0.9 copy-start.5
  45.8 0.9 copy-start.6
  46.6 0.7 copy-start.7
  47.3 0.6 copy-start.8
  123.3 2.4 copy-start.10
  123.3 130.5 %collective-permute-start = (bf16[8,64,320]{2,1,0:T(8,128)(2,1)}, bf16[8,64,320]{2,1,0:T(8,128)(2,1)S(1)}, u32[]{:S(2)}, u32[]{:S(2)}) collective-permute-start(bf16[8,64,320]{2,1,0:T(8,128)(2,1)} %get-tuple-element.49), channel_id=1, source_target_pairs={{0,24},{8,0},{16,8},{24,16},{1,25},{9,1},{17,9},{25,17},{2,26},{10... | collective-permute-start | bytes 983048 | tf_op jit(solution)/shard_map/ppermute | solution.py:676
  125.3 128.6 %collective-permute-start.1 = (bf16[8,64,320]{2,1,0:T(8,128)(2,1)}, bf16[8,64,320]{2,1,0:T(8,128)(2,1)S(1)}, u32[]{:S(2)}, u32[]{:S(2)}) collective-permute-start(bf16[8,64,320]{2,1,0:T(8,128)(2,1)} %get-tuple-element.50), channel_id=1, source_target_pairs={{0,16},{8,24},{16,0},{24,8},{1,17},{9,25},{17,1},{25,9},{2,18},{10... | collective-permute-start | bytes 983048 | tf_op jit(solution)/shard_map/ppermute | solution.py:676
  125.7 128.2 %collective-permute-start.2 = (bf16[8,64,320]{2,1,0:T(8,128)(2,1)}, bf16[8,64,320]{2,1,0:T(8,128)(2,1)S(1)}, u32[]{:S(2)}, u32[]{:S(2)}) collective-permute-start(bf16[8,64,320]{2,1,0:T(8,128)(2,1)} %get-tuple-element.51), channel_id=1, source_target_pairs={{0,8},{8,16},{16,24},{24,0},{1,9},{9,17},{17,25},{25,1},{2,10},{10... | collective-permute-start | bytes 983048 | tf_op jit(solution)/shard_map/ppermute | solution.py:676
  251.4 2.6 %copy-start.12 = (f32[160,320]{1,0:T(8,128)S(1)}, f32[160,320]{1,0:T(8,128)}, u32[]{:S(2)}) copy-start(f32[160,320]{1,0:T(8,128)} %get-tuple-element.105) | copy-start | bytes 614404
  254.0 1.2 copy-start.9

commit v3 on v2

v3 whole, which is shorter than its diff:
```python
import functools

import jax
import jax.numpy as jnp
from jax import lax
from jax.experimental import pallas as pl
from jax.experimental.pallas import tpu as pltpu
from jax.sharding import PartitionSpec as P

MASK_ID = 32
LN_EPS = 1e-5
ROPE_BASE = 10000.0
TRAIN_RATIO = 0.15 * 0.8
NEG_BIG = -1e30
VOCAB_PAD = 128
HEAD_DIM = 16
N_HEADS = 20
D = 320
F = 1280
SEQ = 256
LANES = 128
HEADS_PER_TILE = LANES // HEAD_DIM
N_TILES = -(-D // LANES)
HEAD_UNROLL = 4
QKV_HALF = 512
UO_PAD = 1664
SM_ROWS = 16
BF = jnp.bfloat16
F32 = jnp.float32
SQRT_HALF = 0.7071067811865476
INV_SQRT_2PI = 0.3989422804014327

NN = (((1,), (0,)), ((), ()))
NT = (((1,), (1,)), ((), ()))


def stack_rows(parts):
    return jnp.concatenate(parts, axis=0)


def col_sum(z):
    return jnp.sum(z, axis=0, keepdims=True)


def col_mean(z):
    return jnp.mean(z, axis=0, keepdims=True)


def dot(a, b, dims=NN):
    return lax.dot_general(a, b, dims, preferred_element_type=F32)


def col(vecs_t, j):
    return vecs_t[:, j:j + 1]


def rope(z, cos_t, sin_t):
    z4 = z.reshape(N_HEADS, 2, HEAD_DIM // 2, SEQ)
    lower, upper = z4[:, 0], z4[:, 1]
    new_l = lower * cos_t - upper * sin_t
    new_u = upper * cos_t + lower * sin_t
    return jnp.stack([new_l, new_u], axis=1).reshape(D, SEQ)


def key_bias(shift_base, cp_size, seq_loc, length):
    row = lax.broadcasted_iota(jnp.int32, (SEQ, LANES), 0)
    src = (shift_base - row // seq_loc + cp_size) % cp_size
    pos = src * seq_loc + row % seq_loc
    return jnp.where(pos < length, 0.0, NEG_BIG).astype(F32)


def feature_tiles(z_t):
    pad = stack_rows([z_t, jnp.zeros((N_TILES * LANES - D, SEQ), F32)])
    return [pad[t * LANES:(t + 1) * LANES].T.astype(BF) for t in range(N_TILES)]


def store_token_major(dst_ref, z_t):
    for t, part in enumerate(feature_tiles(z_t)):
        dst_ref[t] = part


def head_rows(tile, slot):
    row = lax.broadcasted_iota(jnp.int32, tile.shape, 0)
    return jnp.where(row // HEAD_DIM == slot, tile, jnp.zeros_like(tile))


def pipeline(n, stages):
    held = {}
    for turn in range(n + len(stages) - 1):
        for j in reversed(range(len(stages))):
            i = turn - j
            if 0 <= i < n:
                held[i] = stages[j](held[i], i) if j else stages[j](i)


def token_scale(tok, length, seq_loc, cp_size, me):
    lane = lax.broadcasted_iota(jnp.int32, (1, SEQ), 1)
    src = (me - lane // seq_loc + cp_size) % cp_size
    pos = src * seq_loc + lane % seq_loc
    is_mask = tok == MASK_ID
    n_mask = jnp.sum(is_mask.astype(F32), axis=1, keepdims=True)
    drop = (1.0 - TRAIN_RATIO) / (1.0 - n_mask / length.astype(F32))
    return jnp.where(is_mask | (pos >= length), 0.0, drop)


def one_hot_rows(tok):
    row = lax.broadcasted_iota(jnp.int32, (VOCAB_PAD, SEQ), 0)
    return jnp.where(row == tok, 1.0, 0.0).astype(BF)


def join_rows(ref):
    return stack_rows([ref[i].astype(F32) for i in range(ref.shape[0])]).astype(BF)


def wide(z):
    return jnp.concatenate([z, z], axis=1)


def spread_vectors(sm_ref, rows_of, dst_ref):
    pieces = sm_ref.shape[0]
    rows = D // pieces
    for i in range(pieces):
        sm_t = sm_ref[i].T
        for n, j in enumerate(rows_of):
            dst_ref[n, i * rows:(i + 1) * rows] = jnp.broadcast_to(sm_t[:rows, j:j + 1], (rows, LANES))


def normalize(z):
    cent = z - col_mean(z)
    rstd = lax.rsqrt(col_mean(cent * cent) + LN_EPS)
    return cent * rstd, rstd


class Gather:
    def __init__(self, cp_size, n_seq, ins, outs, tok_in, tok_out, g_in, g_out, sems):
        self.ins, self.outs, self.tok_in, self.tok_out, self.g_in, self.g_out = ins, outs, tok_in, tok_out, g_in, g_out
        self.send, self.recv, self.tok_send, self.tok_recv, self.g_send, self.g_recv, self.own = sems
        self.cp_size, self.n_seq = cp_size, n_seq
        self.me = lax.axis_index('cp')
        fs = self.fs = lax.axis_index('fsdp')
        y, x, c = place(fs)
        self.near, self.xn, self.yn = neighbours(fs)
        self.dg = neighbours(self.xn)[2]
        self.first = self.xn * (1 - c) + self.yn * c
        self.other = self.yn * (1 - c) + self.xn * c
        self.flip = 1 - 2 * c
        self.cps = [lax.rem(self.me + k, cp_size) for k in range(1, cp_size)]

    def enter(self):
        enter([device(self.me, f) for f in (self.near, self.xn, self.yn)] + [device(z, self.fs) for z in self.cps])

    def routes(self):
        return [(self.fs, self.xn), (self.fs, self.yn), (self.fs, self.near), (self.first, self.other), (self.first, self.near), (self.other, self.near), (self.dg, self.near)]

    def copy(self, a, lane):
        slot, peer = self.routes()[lane]
        src = self.ins[a] if lane < 3 else self.outs[a].at[slot]
        return remote(src, self.outs[a].at[slot], self.send.at[a, lane], self.recv.at[a, slot], device(self.me, peer))

    def push(self, arrays, lanes):
        for a in arrays:
            for lane in lanes:
                self.copy(a, lane).start()

    def arrived(self, arrays, slots):
        for a in arrays:
            for slot in slots:
                remote(self.ins[a], self.outs[a].at[slot], self.send.at[a, 0], self.recv.at[a, slot], device(self.me, self.near)).wait_recv()

    def begin(self, arrays):
        self.push(arrays, (0, 1, 2))
        for a in arrays:
            self.outs[a][self.fs] = self.ins[a][...]

    def relay(self, arrays):
        self.arrived(arrays, [self.first])
        self.push(arrays, (3, 4))
        self.arrived(arrays, [self.other])
        self.push(arrays, (5,))

    def relay_last(self, arrays):
        self.arrived(arrays, [self.dg])
        self.push(arrays, (6,))

    def complete(self, arrays):
        self.arrived(arrays, [self.near] + [slot + self.flip for slot in (self.xn, self.yn, self.dg)])

    def sent(self, arrays):
        for a in arrays:
            for lane in range(7):
                self.copy(a, lane).wait_send()

    def blocks(self, z):
        return self.g_in.at[pl.ds(z * self.n_seq, self.n_seq)]

    def tok_copy(self, k):
        z = self.cps[k - 1]
        return remote(self.tok_in.at[z], self.tok_out.at[k], self.tok_send.at[k], self.tok_recv.at[k], device(z, self.fs))

    def g_copy(self, k):
        z = self.cps[k - 1]
        return remote(self.blocks(z), self.g_out.at[k], self.g_send.at[k], self.g_recv.at[k], device(z, self.fs))

    def own_block(self):
        return pltpu.make_async_copy(self.blocks(self.me), self.g_out.at[0], self.own)


def attn_fwd_kernel(n_steps, cp_size, seq_loc, n_arr, len_ref, emb_ref, cos_ref, sin_ref, tok_in, g_in, *refs):
    ins, refs = refs[:n_arr], refs[n_arr:]
    saved, refs = refs[:n_arr - 1], refs[n_arr - 1:]
    tok_ref, g_out, gain_ref, wqkv_n, h_ref, xhat1_ref, stat_ref, qkv_ref, lse_ref, attn_ref, wqkv_t, k_tm, q_pad, bias, vec_b, tok_s, save_sem, *refs = refs
    outs = refs[:n_arr]
    gather = Gather(cp_size, n_steps, ins, outs, tok_in, tok_s, g_in, g_out, refs[n_arr:])
    kept = outs[:1] + outs[2:]
    saves = [pltpu.make_async_copy(src, dst, save_sem.at[i]) for i, (src, dst) in enumerate(zip(kept, saved))]
    early, late = (0, 1), tuple(range(2, n_arr))
    step = pl.program_id(0)
    me = lax.axis_index('cp')

    @pl.when(step == 0)
    def _():
        gather.enter()
        for k in range(1, cp_size):
            gather.tok_copy(k).start()
        gather.begin(early)
        for k in range(1, cp_size):
            gather.g_copy(k).start()
        gather.own_block().start()
        tok_s[0] = tok_in[me]
        q_pad[...] = jnp.zeros_like(q_pad)
        gather.relay(early)
        gather.begin(late)
        gather.relay_last(early)
        gather.complete(early)
        joined = join_rows(outs[1])
        wqkv_n[...] = joined
        wqkv_t[...] = joined.T
        pieces = outs[0].shape[0]
        rows = D // pieces
        for i in range(pieces):
            gain_ref[i * rows:(i + 1) * rows] = outs[0][i].T[:rows]
        spread_vectors(outs[0], range(5), vec_b)
        for k in range(1, cp_size):
            gather.tok_copy(k).wait()

    @pl.when(step == 2)
    def _():
        gather.relay(late)

    @pl.when(step == 4)
    def _():
        gather.relay_last(late)

    @pl.when(step == 6)
    def _():
        gather.complete(late)
        for copy in saves:
            copy.start()

    length = len_ref[step]
    tok = jnp.concatenate([tok_s[k, pl.ds(step, 1), :] for k in range(cp_size)], axis=1)
    tok_ref[0] = tok
    keep = token_scale(tok, length, seq_loc, cp_size, me)
    e = dot(emb_ref[...], one_hot_rows(tok)) * keep
    xhat1, rstd1 = normalize(e)
    xhat1_ref[0] = xhat1
    h = (xhat1 * wide(vec_b[0]) + wide(vec_b[1])).astype(BF)
    h_ref[0] = h
    stat_ref[0] = stack_rows([rstd1, keep, jnp.zeros((6, SEQ), F32)])
    cos_t, sin_t = cos_ref[...], sin_ref[...]
    q = (dot(wqkv_t[0:D], h) + wide(vec_b[2])) * HEAD_DIM ** -0.5
    q = rope(q, cos_t, sin_t).astype(BF)
    qkv_ref[0, 0:D] = q
    q_pad[0:D] = q
    k = rope(dot(wqkv_t[D:2 * D], h) + wide(vec_b[3]), cos_t, sin_t)
    qkv_ref[0, D:2 * D] = k.astype(BF)
    store_token_major(k_tm, k)
    qkv_ref[0, 2 * D:3 * D] = (dot(wqkv_t[2 * D:3 * D], h) + wide(vec_b[4])).astype(BF)
    bias[...] = key_bias(me, cp_size, seq_loc, length)

    def scores(hd):
        tile, slot = hd // HEADS_PER_TILE, hd % HEADS_PER_TILE
        return dot(k_tm[tile], head_rows(q_pad[tile * LANES:(tile + 1) * LANES, :], slot))

    def weights(s, hd):
        s = s + wide(bias[...])
        m = jnp.max(s, axis=0, keepdims=True)
        p = jnp.exp(s - m)
        l = col_sum(p)
        lse_ref[0, hd] = m + jnp.log(l)
        return p.astype(BF), l

    def attend(pair, hd):
        p, l = pair
        lo = hd * HEAD_DIM
        attn_ref[0, lo:lo + HEAD_DIM] = dot(qkv_ref[0, 2 * D + lo:2 * D + lo + HEAD_DIM, :], p) / l

    pipeline(N_HEADS, (scores, weights, attend))

    @pl.when(step == n_steps - 1)
    def _():
        gather.sent(early + late)
        for copy in saves:
            copy.wait()
        for k in range(1, cp_size):
            gather.g_copy(k).wait()
        gather.own_block().wait()


def to_token_major(z_t):
    return jnp.concatenate(feature_tiles(z_t), axis=1)[:, :D]


def to_feature_major(z):
    z32 = z.astype(F32)
    pad = jnp.concatenate([z32, jnp.zeros((SEQ, N_TILES * LANES - D), F32)], axis=1)
    return stack_rows([pad[:, t * LANES:(t + 1) * LANES].T for t in range(N_TILES)])[:D]


def lane_part(z):
    return z[:, :LANES] + z[:, LANES:]


def ln_grad(dn, xhat, rstd, gain):
    dxh = dn * gain
    m1 = col_mean(dxh)
    m2 = col_mean(dxh * xhat)
    return rstd * (dxh - m1 - xhat * m2)


def row_sum(acc):
    return col_sum(acc.T)


class Homeward:
    def __init__(self, n_seq, seq_loc, buf, out, send, recv):
        self.n_seq, self.seq_loc, self.buf, self.out, self.send, self.recv = n_seq, seq_loc, buf, out, send, recv
        self.cp_size = n_pieces(out, n_seq)
        self.me = lax.axis_index('cp')
        self.fs = lax.axis_index('fsdp')
        self.others = range(1, self.cp_size)

    def enter(self):
        enter([device(lax.rem(self.me + k, self.cp_size), self.fs) for k in self.others])

    def copy(self, step, k):
        src = self.buf.at[lax.rem(step, 2), pl.ds(k * self.seq_loc, self.seq_loc)]
        dst = self.out.at[self.me * self.n_seq + step]
        if k == 0:
            return pltpu.make_async_copy(src, dst, self.send.at[step, k])
        return remote(src, dst, self.send.at[step, k], self.recv.at[step, k], device(lax.rem(self.me + self.cp_size - k, self.cp_size), self.fs))

    def start(self, step):
        for k in range(self.cp_size):
            self.copy(step, k).start()

    def sent(self, step):
        self.copy(step, 0).wait()
        for k in self.others:
            self.copy(step, k).wait_send()

    def arrived(self):
        for step in range(self.n_seq):
            for k in self.others:
                self.copy(step, k).wait_recv()


def n_pieces(out, n_seq):
    return out.shape[0] // n_seq


def ffn_kernel(n_steps, seq_loc, tok_ref, stat_ref, attn_ref, g_ref, emb_ref, sm_ref, wout_ref, wup_ref, wdown_ref,
               out_ref, dres_ref, dattn_ref, dwdown_ref, dwuo_ref, dvec_ref,
               wout_n, wup_n, wout_t, wup_t, wdown_t, vec_b, bup_b, dup_s, gelu_s, acc_bup, acc_vec, out_s, out_send, out_recv):
    step = pl.program_id(0)
    home = Homeward(n_steps, seq_loc, out_s, out_ref, out_send, out_recv)

    @pl.when(step == 0)
    def _():
        home.enter()
        for src, nat, tr in ((wout_ref, wout_n, wout_t), (wup_ref, wup_n, wup_t)):
            joined = join_rows(src)
            nat[...] = joined
            tr[...] = joined.T
        wdown_t[...] = wdown_ref[...].T
        spread_vectors(sm_ref, range(5, 9), vec_b)
        pieces = sm_ref.shape[0]
        rows = D // pieces
        for i in range(pieces):
            sm_t = sm_ref[i].T
            for r in range(F // D):
                lo = i * (F // pieces) + r * rows
                bup_b[lo:lo + rows] = jnp.broadcast_to(sm_t[:rows, 9 + r:10 + r], (rows, LANES))
        for acc in (dwdown_ref, dwuo_ref, acc_bup, acc_vec):
            acc[...] = jnp.zeros_like(acc)

    e = dot(emb_ref[...], one_hot_rows(tok_ref[0])) * stat_ref[0, 1:2]
    o = attn_ref[0].astype(BF)
    x1 = e + dot(wout_t[...], o) + wide(vec_b[0])
    xhat2, rstd2 = normalize(x1)
    a = (xhat2 * wide(vec_b[1]) + wide(vec_b[2])).astype(BF)
    g = stack_rows([g_ref[k, 0] for k in range(g_ref.shape[0])])
    for c in range(F // D):
        rows = slice(c * D, (c + 1) * D)
        u = dot(wup_t[rows], a) + wide(bup_b[rows])
        cdf = 0.5 * (1.0 + lax.erf(u * SQRT_HALF))
        gelu = (u * cdf).astype(BF)
        gelu_s[rows] = gelu
        dup = dot(wdown_ref[rows], g, NT) * (cdf + u * (INV_SQRT_2PI * jnp.exp(-0.5 * u * u)))
        acc_bup[rows] += lane_part(dup)
        dup_s[rows] = dup.astype(BF)
        dwdown_ref[rows] += dot(gelu, g)
    @pl.when(step >= 2)
    def _():
        home.sent(step - 2)

    out_s[lax.rem(step, 2)] = to_token_major(x1 + wide(vec_b[3]) + dot(wdown_t[...], gelu_s[...]))
    home.start(step)
    dup_b = dup_s[...]
    dwuo_ref[:, 0:F] += dot(a, dup_b, NT)
    dn2 = dot(wup_n[...], dup_b)
    g_t = to_feature_major(g)
    dres = g_t + ln_grad(dn2, xhat2, rstd2, wide(vec_b[1]))
    for j, part in enumerate((dres, dn2 * xhat2, dn2, g_t)):
        acc_vec[j] += lane_part(part)
    dres_ref[0] = dres
    dres_b = dres.astype(BF)
    dwuo_ref[:, F:F + D] += dot(o, dres_b, NT)
    dattn_ref[0] = dot(wout_n[...], dres_b)

    @pl.when(step == n_steps - 1)
    def _():
        rows = [row_sum(pad_rows(acc_vec[j])) for j in range(4)] + [row_sum(pad_rows(acc_bup[j * D:(j + 1) * D])) for j in range(F // D)]
        dvec_ref[...] = stack_rows(rows)
        home.sent(step - 1)
        home.sent(step)
        home.arrived()


def pad_rows(z):
    return stack_rows([z, jnp.zeros((N_TILES * LANES - D, LANES), F32)])


def attn_bwd_kernel(n_steps, cp_size, seq_loc, len_ref, me_ref, tok_ref, vec_ref, wqkv_ref, cos_ref, sin_ref, qkv_ref, lse_ref, attn_ref, dattn_ref, dres_ref, xhat1_ref, h_ref, stat_ref, dwdown_ref, dwuo_ref, dvec2_ref,
                    rdown_ref, ruo_ref, rqa_ref, rqb_ref, rsmall_ref,
                    k_tm, v_tm, q_pad, do_pad, bias, dq_s, dk_s, dv_s, acc_b, acc_vec, acc_qa, acc_qb, acc_emb, *red):
    step = pl.program_id(0)
    summer = GradSum(cp_size, (dwdown_ref, dwuo_ref, acc_qa, acc_qb), (rdown_ref, ruo_ref, rqa_ref, rqb_ref), rsmall_ref, red)

    @pl.when(step == 0)
    def _():
        summer.enter()
        for i in (0, 1):
            summer.start(0, i)
        acc_qa[...] = jnp.zeros_like(acc_qa)
        acc_qb[...] = jnp.zeros_like(acc_qb)
        acc_emb[...] = jnp.zeros_like(acc_emb)
        acc_b[...] = jnp.zeros_like(acc_b)
        acc_vec[...] = jnp.zeros_like(acc_vec)
        q_pad[...] = jnp.zeros_like(q_pad)
        do_pad[...] = jnp.zeros_like(do_pad)

    for phase, at in enumerate(PHASE_STEPS):
        @pl.when(step == at)
        def _(phase=phase):
            for i in (0, 1):
                summer.finish(phase, i)
                summer.start(phase + 1, i)

    length = len_ref[step]
    me = me_ref[0]
    vecs = vec_ref[...]
    q_pad[0:D] = qkv_ref[0, 0:D]
    do_pad[0:D] = dattn_ref[0].astype(BF)
    store_token_major(k_tm, qkv_ref[0, D:2 * D].astype(F32))
    store_token_major(v_tm, qkv_ref[0, 2 * D:3 * D].astype(F32))
    bias[...] = key_bias(me, cp_size, seq_loc, length)

    def products(hd):
        tile, slot = hd // HEADS_PER_TILE, hd % HEADS_PER_TILE
        t0 = slice(tile * LANES, (tile + 1) * LANES)
        return dot(k_tm[tile], head_rows(q_pad[t0, :], slot)), dot(v_tm[tile], head_rows(do_pad[t0, :], slot))

    def weights(pair, hd):
        s, dp = pair
        rows = slice(hd * HEAD_DIM, (hd + 1) * HEAD_DIM)
        delta = col_sum(dattn_ref[0, rows, :] * attn_ref[0, rows, :])
        p = jnp.exp((s + wide(bias[...])) - lse_ref[0, hd])
        return p.astype(BF), (p * (dp - delta)).astype(BF)

    def gradients(pair, hd):
        p, ds = pair
        rows = slice(hd * HEAD_DIM, (hd + 1) * HEAD_DIM)
        dq_s[rows, :] = dot(qkv_ref[0, D + hd * HEAD_DIM:D + (hd + 1) * HEAD_DIM, :], ds)
        dk_s[rows, :] = dot(q_pad[rows, :], ds, NT)
        dv_s[rows, :] = dot(do_pad[rows, :], p, NT)

    pipeline(N_HEADS, (products, weights, gradients))

    cos_t, sin_t = cos_ref[...], sin_ref[...]
    h = h_ref[0]
    dq = rope(dq_s[...], cos_t, -sin_t) * HEAD_DIM ** -0.5
    dk = rope(dk_s[...], cos_t, -sin_t)
    dv = dv_s[...]
    dn1 = jnp.zeros((D, SEQ), F32)
    parts = []
    for j, dz in enumerate((dq, dk, dv)):
        acc_b[j] += lane_part(dz)
        parts.append(dz.astype(BF))
    dz_b = stack_rows(parts)
    acc_qa[...] += dot(h, dz_b[:QKV_HALF], NT).reshape(acc_qa.shape)
    acc_qb[:, :, :3 * D - QKV_HALF] += dot(h, dz_b[QKV_HALF:], NT).reshape(acc_qb.shape[0], acc_qb.shape[1], 3 * D - QKV_HALF)
    dn1 = dot(wqkv_ref[...], dz_b)
    xhat1 = xhat1_ref[0]
    acc_vec[0] += lane_part(dn1 * xhat1)
    acc_vec[1] += lane_part(dn1)
    de = dres_ref[0] + ln_grad(dn1, xhat1, stat_ref[0, 0:1], col(vecs, 0))
    de = (de * stat_ref[0, 1:2]).astype(BF)
    acc_emb[...] += dot(one_hot_rows(tok_ref[0]), de, NT)

    @pl.when(step == n_steps - 1)
    def _():
        for i in (2, 3):
            summer.start(0, i)
        rows = [row_sum(pad_rows(acc_vec[j])) for j in range(2)] + [row_sum(pad_rows(acc_b[j])) for j in range(3)]
        small = summer.small
        small[...] = jnp.zeros_like(small)
        small[:EMB_ROWS, :D] = acc_emb[:EMB_ROWS]
        small[EMB_ROWS:EMB_ROWS + len(rows)] = stack_rows(rows)
        small[EMB_ROWS + 8:EMB_ROWS + 16] = dvec2_ref[...]
        summer.start_small(0)
        for phase in range(5):
            for i in (2, 3):
                summer.finish(phase, i)
                if phase < 4:
                    summer.start(phase + 1, i)
            summer.finish_small(phase)
            if phase < 4:
                summer.start_small(phase + 1)
        for i in (0, 1):
            summer.finish(4, i)


MESH = pl.DeviceIdType.MESH
EMB_ROWS = 40
SMALL_ROWS = 64
PHASE_STEPS = (1, 3, 4, 6)
STREAMS = (('xy', (0, 40, 40)), ('yx', (1, 512, 384)), ('xy', (1, 128, 128)), ('yx', (1, 128, 128)))
SMALL_SPEC = (0, SMALL_ROWS // 4, SMALL_ROWS // 4)


def neighbours(fs):
    y, x, c = place(fs)
    return fs + 1 - 2 * c, fs + 2 - 4 * x, fs + 4 - 8 * y


def place(fs):
    return fs // 4, (fs // 2) % 2, fs % 2


def device(cp, fs):
    return {'cp': cp, 'fsdp': fs}


def enter(peers):
    barrier = pltpu.get_barrier_semaphore()
    for peer in peers:
        pl.semaphore_signal(barrier, inc=1, device_id=peer, device_id_type=MESH)
    pl.semaphore_wait(barrier, len(peers))


def remote(src, dst, send_sem, recv_sem, peer):
    return pltpu.make_async_remote_copy(src_ref=src, dst_ref=dst, send_sem=send_sem, recv_sem=recv_sem, device_id=peer, device_id_type=MESH)


def piece_of(ref, spec, p):
    axis, size, stride = spec
    start = pl.multiple_of(p * stride, stride)
    return ref.at[pl.ds(start, size), :] if axis == 0 else ref.at[:, pl.ds(start, size)]


class GradSum:
    def __init__(self, cp_size, big, outs, small_out, refs):
        n = len(STREAMS)
        self.cp_size, self.big, self.outs, self.small_out = cp_size, big, outs, small_out
        self.r0, self.acc, self.r1, self.r2, self.rz, self.rg = (refs[i * n:(i + 1) * n] for i in range(6))
        self.small, self.er, self.ez, self.eg = refs[6 * n:6 * n + 4]
        sems = refs[6 * n + 4:]
        self.sends, self.recvs = sems[0:5], sems[5:10]
        self.small_send, self.small_recv = sems[10], sems[11]
        self.me = lax.axis_index('cp')
        self.fs = lax.axis_index('fsdp')
        self.y, self.x, self.c = place(self.fs)
        fs, y, x, c = self.fs, self.y, self.x, self.c
        self.cps = [lax.rem(self.me + k, cp_size) for k in range(1, cp_size)]
        self.hops = [device(self.me, f) for f in neighbours(fs)]
        self.peers = [device(z, fs) for z in self.cps]

    def enter(self):
        enter(self.hops + self.peers)

    def copies(self, phase, i):
        path, spec = STREAMS[i]
        xy = path == 'xy'
        s, v = self.sends[phase], self.recvs[phase]
        x, y, c, me = self.x, self.y, self.c, self.me
        if phase == 0:
            return [remote(self.big[i].at[2 * j + 1 - c], self.r0[i].at[j], s.at[i, j], v.at[i, j], self.hops[0]) for j in range(4)]
        if phase == 1:
            give = [2 * k + 1 - x if xy else 2 * (1 - y) + k for k in range(2)]
            return [remote(self.acc[i].at[give[k]], self.r1[i].at[k], s.at[i, k], v.at[i, k], self.hops[1 if xy else 2]) for k in range(2)]
        if phase == 2:
            return [remote(self.r1[i].at[1 - y if xy else 1 - x], self.r2[i], s.at[i, 0], v.at[i, 0], self.hops[2 if xy else 1])]
        if phase == 3:
            return [remote(piece_of(self.outs[i], spec, self.cps[k]), self.rz[i].at[k], s.at[i, k], v.at[i, k], self.peers[k]) for k in range(self.cp_size - 1)]
        return [remote(self.rg[i].at[me], self.rg[i].at[me], s.at[i, k], v.at[i, k], self.peers[k]) for k in range(self.cp_size - 1)]

    def start(self, phase, i):
        for copy in self.copies(phase, i):
            copy.start()

    def finish(self, phase, i):
        for copy in self.copies(phase, i):
            copy.wait()
        path, spec = STREAMS[i]
        xy = path == 'xy'
        big, r0, acc, r1, r2, out = self.big[i], self.r0[i], self.acc[i], self.r1[i], self.r2[i], self.outs[i]
        rz, rg = self.rz[i], self.rg[i]
        if phase == 0:
            for j in range(4):
                acc[j] = big[2 * j + self.c] + r0[j]
        elif phase == 1:
            for k in range(2):
                r1[k] = acc[2 * k + self.x if xy else 2 * self.y + k] + r1[k]
        elif phase == 2:
            out[...] = r1[self.y if xy else self.x] + r2[...]
        elif phase == 3:
            rg[self.me] = ((piece_of(out, spec, self.me)[...] + rz[0]) + rz[1]) + rz[2]
        else:
            axis, size, stride = spec
            for p in range(self.cp_size):
                lo = p * stride
                if axis == 0:
                    out[lo:lo + size, :] = rg[p]
                else:
                    out[:, lo:lo + size] = rg[p]

    def small_copies(self, phase):
        s, v = self.small_send, self.small_recv
        if phase < 3:
            return [remote(self.small, self.er.at[phase], s.at[phase], v.at[phase], self.hops[phase])]
        if phase == 3:
            return [remote(piece_of(self.small, SMALL_SPEC, self.cps[k]), self.ez.at[k], s.at[3 + k], v.at[3 + k], self.peers[k]) for k in range(self.cp_size - 1)]
        return [remote(self.eg.at[self.me], self.eg.at[self.me], s.at[6 + k], v.at[6 + k], self.peers[k]) for k in range(self.cp_size - 1)]

    def start_small(self, phase):
        for copy in self.small_copies(phase):
            copy.start()

    def finish_small(self, phase):
        for copy in self.small_copies(phase):
            copy.wait()
        if phase < 3:
            self.small[...] += self.er[phase]
        elif phase == 3:
            self.eg[self.me] = ((piece_of(self.small, SMALL_SPEC, self.me)[...] + self.ez[0]) + self.ez[1]) + self.ez[2]
        else:
            size = SMALL_SPEC[1]
            for p in range(self.cp_size):
                self.small_out[p * size:(p + 1) * size, :] = self.eg[p]


def sum_scratch(cp_size, shapes, small_shape):
    dma = pltpu.SemaphoreType.DMA
    n = len(shapes)
    cut = [((size, sh[1]) if axis == 0 else (sh[0], size)) for sh, (_, (axis, size, _)) in zip(shapes, STREAMS)]
    lanes = small_shape[1]
    scratch = [pltpu.VMEM((4,) + sh, F32) for sh in shapes] * 2 + [pltpu.VMEM((2,) + sh, F32) for sh in shapes] + [pltpu.VMEM(sh, F32) for sh in shapes]
    scratch += [pltpu.VMEM((cp_size - 1,) + sh, F32) for sh in cut] + [pltpu.VMEM((cp_size,) + sh, F32) for sh in cut]
    scratch += [pltpu.VMEM(small_shape, F32), pltpu.VMEM((3,) + small_shape, F32), pltpu.VMEM((cp_size - 1, SMALL_SPEC[1], lanes), F32), pltpu.VMEM((cp_size, SMALL_SPEC[1], lanes), F32)]
    scratch += [dma(shape) for shape in ((n, 4), (n, 2), (n, 1), (n, cp_size - 1), (n, cp_size - 1))] * 2 + [dma((3 + 2 * (cp_size - 1),))] * 2
    return scratch


def per_seq(*shape):
    return pl.BlockSpec((1,) + shape, lambda b: (b,) + (0,) * len(shape))


def whole(*shape):
    return pl.BlockSpec(shape, lambda b: (0,) * len(shape))


SMEM = pl.BlockSpec(memory_space=pltpu.SMEM)


def sds(shape, dtype):
    return jax.ShapeDtypeStruct(shape, dtype)


def call(kernel, grid, in_specs, out_specs, out_shape, scratch, flops, name, **params):
    return pl.pallas_call(
        kernel, grid=(grid,), in_specs=in_specs, out_specs=out_specs, out_shape=out_shape, scratch_shapes=scratch, name=name,
        cost_estimate=pl.CostEstimate(flops=flops, bytes_accessed=50_000_000, transcendentals=10_000_000),
        compiler_params=pltpu.CompilerParams(dimension_semantics=('arbitrary',), vmem_limit_bytes=58 * 1024 * 1024, **params))


def solution(mesh):
    cp_size = mesh.shape['cp']
    fs_size = mesh.shape['fsdp']

    def local_step(tokens, lengths, embed_table, layer_vecs, w_qkv, w_out, w_up, b_up, w_down, grad_out):
        n_loc, seq_loc = tokens.shape
        n_seq = n_loc // cp_size
        me = lax.axis_index('cp')
        fs = lax.axis_index('fsdp')

        len_w = lax.dynamic_slice_in_dim(lengths, me * n_seq, n_seq, 0)
        small = stack_rows([layer_vecs, b_up.reshape(F // D, D // fs_size)])
        small = jnp.pad(small, ((0, SM_ROWS - small.shape[0]), (0, LANES - small.shape[1])))
        shards = [small, w_qkv.reshape(-1, 3 * D), w_out, w_up, w_down]
        full = [(fs_size,) + arr.shape for arr in shards]
        emb_t = jnp.pad(embed_table, ((0, VOCAB_PAD - embed_table.shape[0]), (0, 0))).T

        lane = jnp.arange(SEQ)
        positions = ((me - lane // seq_loc + cp_size) % cp_size) * seq_loc + lane % seq_loc
        inv_freq = 1.0 / (ROPE_BASE ** (jnp.arange(0, HEAD_DIM, 2, dtype=F32) / HEAD_DIM))
        angles = inv_freq[:, None] * positions.astype(F32)[None, :]
        cos_t, sin_t = jnp.cos(angles), jnp.sin(angles)
        me_arr = me.reshape(1).astype(jnp.int32)

        S = SEQ
        dma = pltpu.SemaphoreType.DMA
        vmem = pl.BlockSpec(memory_space=pltpu.VMEM)
        hbm = pl.BlockSpec(memory_space=pl.ANY)
        n_arr = len(shards)
        kept = [0] + list(range(2, n_arr))
        g_shape = (cp_size, n_seq, seq_loc, D)
        per_feature = per_seq(D, S)
        tok = tokens.reshape(cp_size, n_seq, seq_loc)
        outs = call(
            functools.partial(attn_fwd_kernel, n_seq, cp_size, seq_loc, n_arr), n_seq,
            [SMEM, whole(D, VOCAB_PAD), whole(8, S), whole(8, S), vmem, hbm] + [vmem] * n_arr,
            [hbm] * len(kept) + [per_seq(1, S), hbm, whole(D, SM_ROWS), whole(D, 3 * D), per_feature, per_feature, per_seq(8, S), per_seq(3 * D, S), per_seq(N_HEADS, 1, S), per_feature],
            [sds(full[i], shards[i].dtype) for i in kept] + [sds((n_seq, 1, S), jnp.int32), sds(g_shape, BF), sds((D, SM_ROWS), F32), sds((D, 3 * D), BF), sds((n_seq, D, S), BF), sds((n_seq, D, S), F32), sds((n_seq, 8, S), F32), sds((n_seq, 3 * D, S), BF), sds((n_seq, N_HEADS, 1, S), F32), sds((n_seq, D, S), F32)],
            [pltpu.VMEM((3 * D, D), BF), pltpu.VMEM((N_TILES, S, LANES), BF), pltpu.VMEM((N_TILES * LANES, S), BF), pltpu.VMEM((S, LANES), F32), pltpu.VMEM((5, D, LANES), F32), pltpu.VMEM(tok.shape, jnp.int32), dma((len(kept),))] + [pltpu.VMEM(sh, arr.dtype) for sh, arr in zip(full, shards)] + [
             dma((n_arr, 7)), dma((n_arr, fs_size)), dma((cp_size,)), dma((cp_size,)), dma((cp_size,)), dma((cp_size,)), dma],
            4_000_000_000, 'attn_fwd', collective_id=0, has_side_effects=True,
        )(len_w, emb_t, cos_t, sin_t, tok, grad_out, *shards)
        small_p, out_p, up_p, down_p, tok_w, g_w, vecs_t, qkv_w, h, xhat1, stat, qkv, lse, attn = outs

        outs = call(
            functools.partial(ffn_kernel, n_seq, seq_loc), n_seq,
            [per_seq(1, S), per_seq(8, S), per_feature, pl.BlockSpec((cp_size, 1, seq_loc, D), lambda b: (0, b, 0, 0)), whole(D, VOCAB_PAD), whole(*full[0]), whole(*full[2]), whole(*full[3]), whole(F, D)],
            [hbm, per_feature, per_feature, whole(F, D), whole(D, UO_PAD), whole(8, N_TILES * LANES)],
            [sds(grad_out.shape, BF), sds((n_seq, D, S), F32), sds((n_seq, D, S), F32), sds((F, D), F32), sds((D, UO_PAD), F32), sds((8, N_TILES * LANES), F32)],
            [pltpu.VMEM((D, D), BF), pltpu.VMEM((D, F), BF), pltpu.VMEM((D, D), BF), pltpu.VMEM((F, D), BF), pltpu.VMEM((D, F), BF), pltpu.VMEM((4, D, LANES), F32), pltpu.VMEM((F, LANES), F32),
             pltpu.VMEM((F, S), BF), pltpu.VMEM((F, S), BF), pltpu.VMEM((F, LANES), F32), pltpu.VMEM((4, D, LANES), F32), pltpu.VMEM((2, S, D), BF), dma((n_seq, cp_size)), dma((n_seq, cp_size))],
            9_000_000_000, 'ffn', collective_id=2, has_side_effects=True,
        )(tok_w, stat, attn, g_w, emb_t, small_p, out_p, up_p, down_p.reshape(F, D))
        layer_out, dres, dattn, dw_down, dw_uo, dvec2 = outs

        rows = D // fs_size
        shapes = [(F // fs_size, D), (rows, UO_PAD), (rows, QKV_HALF), (rows, QKV_HALF)]
        small_shape = (SMALL_ROWS, N_TILES * LANES)
        acc_q = pltpu.VMEM((fs_size, rows, QKV_HALF), F32)
        r_down, r_uo, r_qa, r_qb, packed = call(
            functools.partial(attn_bwd_kernel, n_seq, cp_size, seq_loc), n_seq,
            [SMEM, SMEM, per_seq(1, S), whole(D, SM_ROWS), whole(D, 3 * D), whole(8, S), whole(8, S), per_seq(3 * D, S), per_seq(N_HEADS, 1, S), per_seq(D, S), per_seq(D, S), per_seq(D, S), per_seq(D, S), per_seq(D, S), per_seq(8, S),
             whole(fs_size, *shapes[0]), whole(fs_size, *shapes[1]), whole(8, N_TILES * LANES)],
            [whole(*sh) for sh in shapes] + [whole(*small_shape)],
            [sds(sh, F32) for sh in shapes] + [sds(small_shape, F32)],
            [pltpu.VMEM((N_TILES, S, LANES), BF), pltpu.VMEM((N_TILES, S, LANES), BF), pltpu.VMEM((N_TILES * LANES, S), BF), pltpu.VMEM((N_TILES * LANES, S), BF), pltpu.VMEM((S, LANES), F32),
             pltpu.VMEM((D, S), F32), pltpu.VMEM((D, S), F32), pltpu.VMEM((D, S), F32), pltpu.VMEM((3, D, LANES), F32), pltpu.VMEM((2, D, LANES), F32), acc_q, acc_q, pltpu.VMEM((VOCAB_PAD, D), F32)] + sum_scratch(cp_size, shapes, small_shape),
            9_000_000_000, 'attn_bwd', collective_id=1, has_side_effects=True,
        )(len_w, me_arr, tok_w, vecs_t, qkv_w, cos_t, sin_t, qkv, lse, attn, dattn, dres, xhat1, h, stat, dw_down.reshape(fs_size, *shapes[0]), dw_uo.reshape(fs_size, *shapes[1]), dvec2)

        vocab = embed_table.shape[0]
        d_vecs = stack_rows([packed[EMB_ROWS:EMB_ROWS + 5], packed[EMB_ROWS + 8:EMB_ROWS + 12]])
        d_vecs = lax.dynamic_slice_in_dim(d_vecs, fs * (D // fs_size), D // fs_size, 1)
        d_bup = packed[EMB_ROWS + 12:EMB_ROWS + 16, :D].reshape(F)
        d_bup = lax.dynamic_slice_in_dim(d_bup, fs * (F // fs_size), F // fs_size, 0)
        d_qkv = jnp.concatenate([r_qa, r_qb], axis=1)[:, :3 * D].reshape(w_qkv.shape)
        return (layer_out, packed[:vocab, :D], d_vecs, d_qkv, r_uo[:, F:F + D], r_uo[:, :F], d_bup, r_down)

    in_specs = (P('fsdp', 'cp'), P('fsdp'), P(), P(None, 'fsdp'), P('fsdp', None, None, None), P('fsdp', None), P('fsdp', None), P('fsdp'), P('fsdp', None), P('fsdp', 'cp', None))
    out_specs = (P('fsdp', 'cp', None), P(), P(None, 'fsdp'), P('fsdp', None, None, None), P('fsdp', None), P('fsdp', None), P('fsdp'), P('fsdp', None))
    return jax.shard_map(local_step, mesh=mesh, in_specs=in_specs, out_specs=out_specs, check_vma=False)
```

time: 256 us -> 222 us (0.87)
  Pallas kernels: 222 us -> 201 us
  starting transfers between devices: 10.3 us -> 0 us
  local copies, waits for them, and re-layouts: 19.1 us -> 15.4 us
    pallas_call x3 -> x2, Pallas kernels: 129 us -> 117 us  [the longest x1 69.1 us: local_step(): call(functools.partial(attn_fwd_kernel, n_seq, cp_size, seq_loc, n_arr),...]
    ppermute x6 -> x0, starting transfers between devices: 10.3 us -> none  [the longest x3 7.02 us: to_whole(): blocks.append(lax.ppermute(blk, 'cp', shift(k)) if k else blk)]
    pallas_call x1, Pallas kernels: 93.2 us -> 84.3 us  [local_step(): call(functools.partial(attn_bwd_kernel, n_seq, cp_size, seq_loc), n_seq,...]
    unnamed x36 -> x7, local copies, waits for them, and re-layouts: 5.4 us -> 2.73 us
    dynamic_slice x1 -> x0, local copies, waits for them, and re-layouts: 2.67 us -> none  [to_whole(): blk = lax.dynamic_slice_in_dim(arr, dest * n_seq, n_seq, 0)]
  transfers between devices with their start and end apart: 6 -> 0, of which waited for: 0 -> 0; matrix products, arithmetic and copies ran while one was open for 5% -> 0% of each run, Pallas kernels for 87% -> 0%
where the time goes in v3:
time: 222 us; the launch traced here: 221 us
  Pallas kernels  201 us (91%)
  local copies, waits for them, and re-layouts  15.4 us (7%)
  other arithmetic  3.79 us (2%)
    pallas_call x1, Pallas kernels, local_step(): call(functools.partial(attn_bwd_kernel, n_seq, cp_size, seq_loc), n_seq,...  84.3 us
    pallas_call x1, Pallas kernels, local_step(): call(functools.partial(attn_fwd_kernel, n_seq, cp_size, seq_loc, n_arr),...  69.1 us
    pallas_call x1, Pallas kernels, local_step(): call(functools.partial(ffn_kernel, n_seq, seq_loc), n_seq, [per_seq(1, S)...  47.8 us

profile of v3, /device:TPU:0, one launch (start us, length us, event | category | flops | bytes accessed | tf_op | source)
XLA Modules:
  0.0 221.2 jit_solution(15891357080236118510)
XLA Ops:
  0.6 1.2 dynamic_slice.9.len_ref
  1.9 0.7 multiply_sine_fusion
  2.6 0.9 copy.21
  3.5 0.7 pad_bitcast_fusion.emb_ref
  4.2 1.7 copy.22.refs_1_
  5.9 0.8 reshape.86
  6.6 1.3 select_maximum_fusion.refs_0_
  7.9 69.1 %attn_fwd.1 = (f32[8,16,128]{2,1,0:T(8,128)}, bf16[8,40,320]{2,1,0:T(8,128)(2,1)}, bf16[8,40,1280]{2,1,0:T(8,128)(2,1)}, bf16[8,160,320]{2,1,0:T(8,128)(2,1)}, s...) custom-call(s32[8]{0:T(128)} %dynamic_slice.9.len_ref, ...), custom_call_target="tpu_custom_call" | custom-call | flops 4000000000 | bytes 50000000 | tf_op jit(solution)/shard_map/attn_fwd/pallas_call | solution.py:740
  77.1 47.8 %ffn.1 = (bf16[32,64,320]{2,1,0:T(8,128)(2,1)}, f32[8,320,256]{2,1,0:T(8,128)}, f32[8,320,256]{2,1,0:T(8,128)}, f32[1280,320]{1,0:T(8,128)}, f32[320,1664]{1,0:T(8,128)}, /*index=5*/f32[8,384]{1,0:T(8,128)}) custom-call(s32[8,1,256]{2,1,0:T(1,128)} %get-tuple-element.33.tok_ref, f32[8,8,256]{2,1,0:T(8,128)} %get-tuple-element.34.stat_ref, ...), custom_call_target="tpu_custom_call" | custom-call | flops 8999999488 | bytes 50000000 | tf_op jit(solution)/shard_map/ffn/pallas_call | solution.py:751
  124.9 84.3 %attn_bwd.1 = (f32[160,320]{1,0:T(8,128)}, f32[40,1664]{1,0:T(8,128)}, f32[40,512]{1,0:T(8,128)}, f32[40,512]{1,0:T(8,128)}, f32[64,384]{1,0:T(8,128)}) custom-call(s32[8]{0:T(128)} %dynamic_slice.9.len_ref, s32[1]{0:T(128)} %bitcast.4.me_ref, s32[8,1,256]{2,1,0:T(1,128)} %get-tuple-element.33.tok_ref, f32[320,16]{1,0:T(8,128)} %get-tuple-element.42.vec_ref, ...), custom_call_target="tpu_custom_call" | custom-call | flops 8999999488 | bytes 50000000 | tf_op jit(solution)/shard_map/attn_bwd/pallas_call | solution.py:766
  209.2 0.0 copy-start
  209.2 1.1 pad_maximum_fusion
  210.3 0.0 copy-start.1
  210.3 1.0 copy.23
  211.3 1.6 slice.26
  212.9 0.7 slice.22
  213.6 0.7 slice.23
  214.3 0.7 fusion
  215.0 1.5 slice.21
  216.4 1.5 slice.25
  217.9 0.7 slice.27
  218.6 0.1 reshape.93
  218.7 0.6 dynamic_slice.11
  219.3 0.0 copy-done
  219.3 1.1 copy.26
  220.5 0.0 copy-done.1
  220.5 0.7 copy.27
  (2 shorter events, 0.0 us)
Async XLA Ops:
  209.2 10.1 %copy-start = (bf16[32,64,320]{2,1,0:T(8,128)(2,1)S(1)}, bf16[32,64,320]{2,1,0:T(8,128)(2,1)}, u32[]{:S(2)}) copy-start(bf16[32,64,320]{2,1,0:T(8,128)(2,1)} %get-tuple-element.76) | copy-start | bytes 3932164
  210.3 10.2 %copy-start.1 = (f32[160,320]{1,0:T(8,128)S(1)}, f32[160,320]{1,0:T(8,128)}, u32[]{:S(2)}) copy-start(f32[160,320]{1,0:T(8,128)} %get-tuple-element.83) | copy-start | bytes 614404

commit v4 on v3

--- a/solution.py
+++ b/solution.py
@@ -24,6 +24,8 @@
 HEAD_UNROLL = 4
 QKV_HALF = 512
 UO_PAD = 1664
+EARLY_SEQS = 5
+FLOPS = 9_000_000_000
 SM_ROWS = 16
 BF = jnp.bfloat16
 F32 = jnp.float32
@@ -214,16 +216,17 @@
     kept = outs[:1] + outs[2:]
     saves = [pltpu.make_async_copy(src, dst, save_sem.at[i]) for i, (src, dst) in enumerate(zip(kept, saved))]
     early, late = (0, 1), tuple(range(2, n_arr))
+    others = range(1, cp_size)
     step = pl.program_id(0)
     me = lax.axis_index('cp')
 
     @pl.when(step == 0)
     def _():
         gather.enter()
-        for k in range(1, cp_size):
+        for k in others:
             gather.tok_copy(k).start()
         gather.begin(early)
-        for k in range(1, cp_size):
+        for k in others:
             gather.g_copy(k).start()
         gather.own_block().start()
         tok_s[0] = tok_in[me]
@@ -240,7 +243,7 @@
         for i in range(pieces):
             gain_ref[i * rows:(i + 1) * rows] = outs[0][i].T[:rows]
         spread_vectors(outs[0], range(5), vec_b)
-        for k in range(1, cp_size):
+        for k in others:
             gather.tok_copy(k).wait()
 
     @pl.when(step == 2)
@@ -257,7 +260,7 @@
         for copy in saves:
             copy.start()
 
-    length = len_ref[step]
+    length = len_ref[lax.axis_index('cp') * n_steps + step]
     tok = jnp.concatenate([tok_s[k, pl.ds(step, 1), :] for k in range(cp_size)], axis=1)
     tok_ref[0] = tok
     keep = token_scale(tok, length, seq_loc, cp_size, me)
@@ -302,7 +305,7 @@
         gather.sent(early + late)
         for copy in saves:
             copy.wait()
-        for k in range(1, cp_size):
+        for k in others:
             gather.g_copy(k).wait()
         gather.own_block().wait()
 
@@ -333,47 +336,32 @@
 
 
 class Homeward:
-    def __init__(self, n_seq, seq_loc, buf, out, send, recv):
-        self.n_seq, self.seq_loc, self.buf, self.out, self.send, self.recv = n_seq, seq_loc, buf, out, send, recv
-        self.cp_size = n_pieces(out, n_seq)
+    def __init__(self, cp_size, seq_loc, send, recv):
+        self.cp_size, self.seq_loc, self.send, self.recv = cp_size, seq_loc, send, recv
         self.me = lax.axis_index('cp')
         self.fs = lax.axis_index('fsdp')
-        self.others = range(1, self.cp_size)
+        self.others = range(1, cp_size)
 
     def enter(self):
         enter([device(lax.rem(self.me + k, self.cp_size), self.fs) for k in self.others])
 
-    def copy(self, step, k):
-        src = self.buf.at[lax.rem(step, 2), pl.ds(k * self.seq_loc, self.seq_loc)]
-        dst = self.out.at[self.me * self.n_seq + step]
-        if k == 0:
-            return pltpu.make_async_copy(src, dst, self.send.at[step, k])
-        return remote(src, dst, self.send.at[step, k], self.recv.at[step, k], device(lax.rem(self.me + self.cp_size - k, self.cp_size), self.fs))
-
-    def start(self, step):
-        for k in range(self.cp_size):
-            self.copy(step, k).start()
-
-    def sent(self, step):
-        self.copy(step, 0).wait()
-        for k in self.others:
-            self.copy(step, k).wait_send()
-
-    def arrived(self):
-        for step in range(self.n_seq):
-            for k in self.others:
-                self.copy(step, k).wait_recv()
-
-
-def n_pieces(out, n_seq):
-    return out.shape[0] // n_seq
-
-
-def ffn_kernel(n_steps, seq_loc, tok_ref, stat_ref, attn_ref, g_ref, emb_ref, sm_ref, wout_ref, wup_ref, wdown_ref,
-               out_ref, dres_ref, dattn_ref, dwdown_ref, dwuo_ref, dvec_ref,
+    def block(self, k):
+        return pl.ds(k * self.seq_loc, self.seq_loc)
+
+    def copies(self, item, srcs, dst):
+        local = pltpu.make_async_copy(srcs[0], dst, self.send.at[item, 0])
+        return [local] + [remote(srcs[k], dst, self.send.at[item, k], self.recv.at[item, k], device(lax.rem(self.me + self.cp_size - k, self.cp_size), self.fs)) for k in self.others]
+
+
+def ffn_kernel(n_steps, cp_size, seq_loc, tok_ref, stat_ref, attn_ref, g_ref, emb_ref, sm_ref, wout_ref, wup_ref, wdown_ref,
+               out_ref, rest_ref, dres_ref, dattn_ref, dwdown_ref, dwuo_ref, dvec_ref,
                wout_n, wup_n, wout_t, wup_t, wdown_t, vec_b, bup_b, dup_s, gelu_s, acc_bup, acc_vec, out_s, out_send, out_recv):
     step = pl.program_id(0)
-    home = Homeward(n_steps, seq_loc, out_s, out_ref, out_send, out_recv)
+    home = Homeward(cp_size, seq_loc, out_send, out_recv)
+
+    def leaving(item):
+        return home.copies(item, [out_s.at[item, home.block(k)] for k in range(cp_size)], out_ref.at[home.me, item])
+
 
     @pl.when(step == 0)
     def _():
@@ -410,12 +398,15 @@
         acc_bup[rows] += lane_part(dup)
         dup_s[rows] = dup.astype(BF)
         dwdown_ref[rows] += dot(gelu, g)
-    @pl.when(step >= 2)
-    def _():
-        home.sent(step - 2)
-
-    out_s[lax.rem(step, 2)] = to_token_major(x1 + wide(vec_b[3]) + dot(wdown_t[...], gelu_s[...]))
-    home.start(step)
+    out_tm = to_token_major(x1 + wide(vec_b[3]) + dot(wdown_t[...], gelu_s[...]))
+    rest_ref[0] = out_tm
+
+    @pl.when(step < EARLY_SEQS)
+    def _():
+        out_s[step] = out_tm
+        for copy in leaving(step):
+            copy.start()
+
     dup_b = dup_s[...]
     dwuo_ref[:, 0:F] += dot(a, dup_b, NT)
     dn2 = dot(wup_n[...], dup_b)
@@ -432,24 +423,29 @@
     def _():
         rows = [row_sum(pad_rows(acc_vec[j])) for j in range(4)] + [row_sum(pad_rows(acc_bup[j * D:(j + 1) * D])) for j in range(F // D)]
         dvec_ref[...] = stack_rows(rows)
-        home.sent(step - 1)
-        home.sent(step)
-        home.arrived()
+        for item in range(EARLY_SEQS):
+            for copy in leaving(item):
+                copy.wait()
 
 
 def pad_rows(z):
     return stack_rows([z, jnp.zeros((N_TILES * LANES - D, LANES), F32)])
 
 
-def attn_bwd_kernel(n_steps, cp_size, seq_loc, len_ref, me_ref, tok_ref, vec_ref, wqkv_ref, cos_ref, sin_ref, qkv_ref, lse_ref, attn_ref, dattn_ref, dres_ref, xhat1_ref, h_ref, stat_ref, dwdown_ref, dwuo_ref, dvec2_ref,
-                    rdown_ref, ruo_ref, rqa_ref, rqb_ref, rsmall_ref,
-                    k_tm, v_tm, q_pad, do_pad, bias, dq_s, dk_s, dv_s, acc_b, acc_vec, acc_qa, acc_qb, acc_emb, *red):
+def attn_bwd_kernel(n_steps, cp_size, seq_loc, len_ref, me_ref, tok_ref, vec_ref, wqkv_ref, cos_ref, sin_ref, qkv_ref, lse_ref, attn_ref, dattn_ref, dres_ref, xhat1_ref, h_ref, stat_ref, dwdown_ref, dwuo_ref, dvec2_ref, rest_ref,
+                    rdown_ref, rup_ref, rout_ref, rqkv_ref, rsmall_ref, outb_ref,
+                    ruo_ref, rqa_ref, rqb_ref, out_send, out_recv, k_tm, v_tm, q_pad, do_pad, bias, dq_s, dk_s, dv_s, acc_b, acc_vec, acc_qa, acc_qb, acc_emb, *red):
     step = pl.program_id(0)
     summer = GradSum(cp_size, (dwdown_ref, dwuo_ref, acc_qa, acc_qb), (rdown_ref, ruo_ref, rqa_ref, rqb_ref), rsmall_ref, red)
 
+    home = Homeward(cp_size, seq_loc, out_send, out_recv)
+    leaving = home.copies(0, [rest_ref.at[:, home.block(k)] for k in range(cp_size)], outb_ref.at[home.me])
+
     @pl.when(step == 0)
     def _():
         summer.enter()
+        for copy in leaving:
+            copy.start()
         for i in (0, 1):
             summer.start(0, i)
         acc_qa[...] = jnp.zeros_like(acc_qa)
@@ -467,7 +463,7 @@
                 summer.finish(phase, i)
                 summer.start(phase + 1, i)
 
-    length = len_ref[step]
+    length = len_ref[lax.axis_index('cp') * n_steps + step]
     me = me_ref[0]
     vecs = vec_ref[...]
     q_pad[0:D] = qkv_ref[0, 0:D]
@@ -539,12 +535,18 @@
                 summer.start_small(phase + 1)
         for i in (0, 1):
             summer.finish(4, i)
+        rup_ref[...] = ruo_ref[:, :F]
+        rout_ref[...] = ruo_ref[:, F:F + D]
+        rqkv_ref[:, :QKV_HALF] = rqa_ref[...]
+        rqkv_ref[:, QKV_HALF:] = rqb_ref[:, :3 * D - QKV_HALF]
+        for copy in leaving:
+            copy.wait()
 
 
 MESH = pl.DeviceIdType.MESH
 EMB_ROWS = 40
 SMALL_ROWS = 64
-PHASE_STEPS = (1, 3, 4, 6)
+PHASE_STEPS = (1, 3, 4, 7)
 STREAMS = (('xy', (0, 40, 40)), ('yx', (1, 512, 384)), ('xy', (1, 128, 128)), ('yx', (1, 128, 128)))
 SMALL_SPEC = (0, SMALL_ROWS // 4, SMALL_ROWS // 4)
 
@@ -714,7 +716,6 @@
         me = lax.axis_index('cp')
         fs = lax.axis_index('fsdp')
 
-        len_w = lax.dynamic_slice_in_dim(lengths, me * n_seq, n_seq, 0)
         small = stack_rows([layer_vecs, b_up.reshape(F // D, D // fs_size)])
         small = jnp.pad(small, ((0, SM_ROWS - small.shape[0]), (0, LANES - small.shape[1])))
         shards = [small, w_qkv.reshape(-1, 3 * D), w_out, w_up, w_down]
@@ -736,51 +737,53 @@
         kept = [0] + list(range(2, n_arr))
         g_shape = (cp_size, n_seq, seq_loc, D)
         per_feature = per_seq(D, S)
+        table = whole(8, S)
         tok = tokens.reshape(cp_size, n_seq, seq_loc)
         outs = call(
             functools.partial(attn_fwd_kernel, n_seq, cp_size, seq_loc, n_arr), n_seq,
-            [SMEM, whole(D, VOCAB_PAD), whole(8, S), whole(8, S), vmem, hbm] + [vmem] * n_arr,
+            [SMEM, whole(D, VOCAB_PAD), table, table, vmem, hbm] + [vmem] * n_arr,
             [hbm] * len(kept) + [per_seq(1, S), hbm, whole(D, SM_ROWS), whole(D, 3 * D), per_feature, per_feature, per_seq(8, S), per_seq(3 * D, S), per_seq(N_HEADS, 1, S), per_feature],
             [sds(full[i], shards[i].dtype) for i in kept] + [sds((n_seq, 1, S), jnp.int32), sds(g_shape, BF), sds((D, SM_ROWS), F32), sds((D, 3 * D), BF), sds((n_seq, D, S), BF), sds((n_seq, D, S), F32), sds((n_seq, 8, S), F32), sds((n_seq, 3 * D, S), BF), sds((n_seq, N_HEADS, 1, S), F32), sds((n_seq, D, S), F32)],
             [pltpu.VMEM((3 * D, D), BF), pltpu.VMEM((N_TILES, S, LANES), BF), pltpu.VMEM((N_TILES * LANES, S), BF), pltpu.VMEM((S, LANES), F32), pltpu.VMEM((5, D, LANES), F32), pltpu.VMEM(tok.shape, jnp.int32), dma((len(kept),))] + [pltpu.VMEM(sh, arr.dtype) for sh, arr in zip(full, shards)] + [
              dma((n_arr, 7)), dma((n_arr, fs_size)), dma((cp_size,)), dma((cp_size,)), dma((cp_size,)), dma((cp_size,)), dma],
-            4_000_000_000, 'attn_fwd', collective_id=0, has_side_effects=True,
-        )(len_w, emb_t, cos_t, sin_t, tok, grad_out, *shards)
+            FLOPS, 'attn_fwd', collective_id=0, has_side_effects=True,
+        )(lengths, emb_t, cos_t, sin_t, tok, grad_out, *shards)
         small_p, out_p, up_p, down_p, tok_w, g_w, vecs_t, qkv_w, h, xhat1, stat, qkv, lse, attn = outs
 
         outs = call(
-            functools.partial(ffn_kernel, n_seq, seq_loc), n_seq,
+            functools.partial(ffn_kernel, n_seq, cp_size, seq_loc), n_seq,
             [per_seq(1, S), per_seq(8, S), per_feature, pl.BlockSpec((cp_size, 1, seq_loc, D), lambda b: (0, b, 0, 0)), whole(D, VOCAB_PAD), whole(*full[0]), whole(*full[2]), whole(*full[3]), whole(F, D)],
-            [hbm, per_feature, per_feature, whole(F, D), whole(D, UO_PAD), whole(8, N_TILES * LANES)],
-            [sds(grad_out.shape, BF), sds((n_seq, D, S), F32), sds((n_seq, D, S), F32), sds((F, D), F32), sds((D, UO_PAD), F32), sds((8, N_TILES * LANES), F32)],
+            [hbm, pl.BlockSpec((1, S, D), lambda b: (jnp.maximum(b - EARLY_SEQS, 0), 0, 0)), per_feature, per_feature, whole(F, D), whole(D, UO_PAD), whole(8, N_TILES * LANES)],
+            [sds((cp_size, EARLY_SEQS, seq_loc, D), BF), sds((n_seq - EARLY_SEQS, S, D), BF), sds((n_seq, D, S), F32), sds((n_seq, D, S), F32), sds((F, D), F32), sds((D, UO_PAD), F32), sds((8, N_TILES * LANES), F32)],
             [pltpu.VMEM((D, D), BF), pltpu.VMEM((D, F), BF), pltpu.VMEM((D, D), BF), pltpu.VMEM((F, D), BF), pltpu.VMEM((D, F), BF), pltpu.VMEM((4, D, LANES), F32), pltpu.VMEM((F, LANES), F32),
-             pltpu.VMEM((F, S), BF), pltpu.VMEM((F, S), BF), pltpu.VMEM((F, LANES), F32), pltpu.VMEM((4, D, LANES), F32), pltpu.VMEM((2, S, D), BF), dma((n_seq, cp_size)), dma((n_seq, cp_size))],
-            9_000_000_000, 'ffn', collective_id=2, has_side_effects=True,
+             pltpu.VMEM((F, S), BF), pltpu.VMEM((F, S), BF), pltpu.VMEM((F, LANES), F32), pltpu.VMEM((4, D, LANES), F32), pltpu.VMEM((EARLY_SEQS, S, D), BF), dma((EARLY_SEQS, cp_size)), dma((EARLY_SEQS, cp_size))],
+            FLOPS, 'ffn', collective_id=2, has_side_effects=True,
         )(tok_w, stat, attn, g_w, emb_t, small_p, out_p, up_p, down_p.reshape(F, D))
-        layer_out, dres, dattn, dw_down, dw_uo, dvec2 = outs
+        out_a, out_rest, dres, dattn, dw_down, dw_uo, dvec2 = outs
 
         rows = D // fs_size
         shapes = [(F // fs_size, D), (rows, UO_PAD), (rows, QKV_HALF), (rows, QKV_HALF)]
         small_shape = (SMALL_ROWS, N_TILES * LANES)
+        results = [shapes[0], (rows, F), (rows, D), (rows, 3 * D), small_shape]
         acc_q = pltpu.VMEM((fs_size, rows, QKV_HALF), F32)
-        r_down, r_uo, r_qa, r_qb, packed = call(
+        r_down, r_up, r_out, r_qkv, packed, out_b = call(
             functools.partial(attn_bwd_kernel, n_seq, cp_size, seq_loc), n_seq,
-            [SMEM, SMEM, per_seq(1, S), whole(D, SM_ROWS), whole(D, 3 * D), whole(8, S), whole(8, S), per_seq(3 * D, S), per_seq(N_HEADS, 1, S), per_seq(D, S), per_seq(D, S), per_seq(D, S), per_seq(D, S), per_seq(D, S), per_seq(8, S),
-             whole(fs_size, *shapes[0]), whole(fs_size, *shapes[1]), whole(8, N_TILES * LANES)],
-            [whole(*sh) for sh in shapes] + [whole(*small_shape)],
-            [sds(sh, F32) for sh in shapes] + [sds(small_shape, F32)],
-            [pltpu.VMEM((N_TILES, S, LANES), BF), pltpu.VMEM((N_TILES, S, LANES), BF), pltpu.VMEM((N_TILES * LANES, S), BF), pltpu.VMEM((N_TILES * LANES, S), BF), pltpu.VMEM((S, LANES), F32),
-             pltpu.VMEM((D, S), F32), pltpu.VMEM((D, S), F32), pltpu.VMEM((D, S), F32), pltpu.VMEM((3, D, LANES), F32), pltpu.VMEM((2, D, LANES), F32), acc_q, acc_q, pltpu.VMEM((VOCAB_PAD, D), F32)] + sum_scratch(cp_size, shapes, small_shape),
-            9_000_000_000, 'attn_bwd', collective_id=1, has_side_effects=True,
-        )(len_w, me_arr, tok_w, vecs_t, qkv_w, cos_t, sin_t, qkv, lse, attn, dattn, dres, xhat1, h, stat, dw_down.reshape(fs_size, *shapes[0]), dw_uo.reshape(fs_size, *shapes[1]), dvec2)
+            [SMEM, SMEM, per_seq(1, S), whole(D, SM_ROWS), whole(D, 3 * D), table, table, per_seq(3 * D, S), per_seq(N_HEADS, 1, S), per_seq(D, S), per_seq(D, S), per_seq(D, S), per_seq(D, S), per_seq(D, S), per_seq(8, S),
+             whole(fs_size, *shapes[0]), whole(fs_size, *shapes[1]), whole(8, N_TILES * LANES), hbm],
+            [whole(*sh) for sh in results] + [hbm],
+            [sds(sh, F32) for sh in results] + [sds((cp_size, n_seq - EARLY_SEQS, seq_loc, D), BF)],
+            [pltpu.VMEM(sh, F32) for sh in shapes[1:]] + [*[dma((1, cp_size))] * 2, pltpu.VMEM((N_TILES, S, LANES), BF), pltpu.VMEM((N_TILES, S, LANES), BF), pltpu.VMEM((N_TILES * LANES, S), BF), pltpu.VMEM((N_TILES * LANES, S), BF), pltpu.VMEM((S, LANES), F32),
+             *[pltpu.VMEM((D, S), F32)] * 3, pltpu.VMEM((3, D, LANES), F32), pltpu.VMEM((2, D, LANES), F32), acc_q, acc_q, pltpu.VMEM((VOCAB_PAD, D), F32)] + sum_scratch(cp_size, shapes, small_shape),
+            FLOPS, 'attn_bwd', collective_id=1, has_side_effects=True,
+        )(lengths, me_arr, tok_w, vecs_t, qkv_w, cos_t, sin_t, qkv, lse, attn, dattn, dres, xhat1, h, stat, dw_down.reshape(fs_size, *shapes[0]), dw_uo.reshape(fs_size, *shapes[1]), dvec2, out_rest)
+        layer_out = jnp.concatenate([out_a, out_b], axis=1).reshape(grad_out.shape)
 
         vocab = embed_table.shape[0]
         d_vecs = stack_rows([packed[EMB_ROWS:EMB_ROWS + 5], packed[EMB_ROWS + 8:EMB_ROWS + 12]])
         d_vecs = lax.dynamic_slice_in_dim(d_vecs, fs * (D // fs_size), D // fs_size, 1)
         d_bup = packed[EMB_ROWS + 12:EMB_ROWS + 16, :D].reshape(F)
         d_bup = lax.dynamic_slice_in_dim(d_bup, fs * (F // fs_size), F // fs_size, 0)
-        d_qkv = jnp.concatenate([r_qa, r_qb], axis=1)[:, :3 * D].reshape(w_qkv.shape)
-        return (layer_out, packed[:vocab, :D], d_vecs, d_qkv, r_uo[:, F:F + D], r_uo[:, :F], d_bup, r_down)
+        return (layer_out, packed[:vocab, :D], d_vecs, r_qkv.reshape(w_qkv.shape), r_out, r_up, d_bup, r_down)
 
     in_specs = (P('fsdp', 'cp'), P('fsdp'), P(), P(None, 'fsdp'), P('fsdp', None, None, None), P('fsdp', None), P('fsdp', None), P('fsdp'), P('fsdp', None), P('fsdp', 'cp', None))
     out_specs = (P('fsdp', 'cp', None), P(), P(None, 'fsdp'), P('fsdp', None, None, None), P('fsdp', None), P('fsdp', None), P('fsdp'), P('fsdp', None))

time: 222 us -> 207 us (0.932)
  Pallas kernels: 201 us -> 191 us
  local copies, waits for them, and re-layouts: 15.4 us -> 9.84 us
    pallas_call x1, Pallas kernels: 47.8 us -> 35.4 us  [local_step(): call(functools.partial(ffn_kernel, n_seq, cp_size, seq_loc), n_seq, [per_...]
    slice x3 -> x0, local copies, waits for them, and re-layouts: 4.06 us -> none  [the longest x1 1.62 us: local_step(): r_uo[:, :F]]
where the time goes in v4:
time: 207 us
  Pallas kernels  191 us (92%)
  local copies, waits for them, and re-layouts  9.84 us (5%)
  other arithmetic  5.27 us (3%)
    pallas_call x1, Pallas kernels, local_step(): call(functools.partial(attn_bwd_kernel, n_seq, cp_size, seq_loc), n_seq,...  86.5 us
    pallas_call x1, Pallas kernels, local_step(): call(functools.partial(attn_fwd_kernel, n_seq, cp_size, seq_loc, n_arr),...  69.1 us
    pallas_call x1, Pallas kernels, local_step(): call(functools.partial(ffn_kernel, n_seq, cp_size, seq_loc), n_seq, [per_...  35.4 us

profile of v4, /device:TPU:0, one launch (start us, length us, event | category | flops | bytes accessed | tf_op | source)
XLA Modules:
  0.0 206.8 jit_solution(13857589750080539432)
XLA Ops:
  0.7 0.7 multiply_sine_fusion
  1.4 0.9 copy.21
  2.3 0.7 pad_bitcast_fusion.emb_ref
  2.9 1.7 copy.22.refs_1_
  4.6 0.8 reshape.89
  5.4 1.3 select_maximum_fusion.refs_0_
  6.7 69.1 %attn_fwd.1 = (f32[8,16,128]{2,1,0:T(8,128)}, bf16[8,40,320]{2,1,0:T(8,128)(2,1)}, bf16[8,40,1280]{2,1,0:T(8,128)(2,1)}, bf16[8,160,320]{2,1,0:T(8,128)(2,1)}, s...) custom-call(s32[32]{0:T(128)} %len_ref.3, ...), custom_call_target="tpu_custom_call" | custom-call | flops 8999999488 | bytes 50000000 | tf_op jit(solution)/shard_map/attn_fwd/pallas_call | solution.py:742
  75.8 35.4 %ffn.1 = (bf16[4,5,64,320]{3,2,1,0:T(8,128)(2,1)}, bf16[3,256,320]{2,1,0:T(8,128)(2,1)}, f32[8,320,256]{2,1,0:T(8,128)}, f32[8,320,256]{2,1,0:T(8,128)}, f32[128...) custom-call(s32[8,1,256]{2,1,0:T(1,128)} %get-tuple-element.35.tok_ref, ...), custom_call_target="tpu_custom_call" | custom-call | flops 8999999488 | bytes 50000000 | tf_op jit(solution)/shard_map/ffn/pallas_call | solution.py:753
  111.2 0.0 copy-start
  111.2 86.5 %attn_bwd.1 = (f32[160,320]{1,0:T(8,128)}, f32[40,1280]{1,0:T(8,128)}, f32[40,320]{1,0:T(8,128)}, f32[40,960]{1,0:T(8,128)}, f32[64,384]{1,0:T(8,128)}, /*index=5*/bf16[4,3,64,320]{3,2,1,0:T(8,128)(2,1)}) custom-call(s32[32]{0:T(128)} %len_ref.3, s32[1]{0:T(128)} %bitcast.4.me_ref, s32[8,1,256]{2,1,0:T(1,128)} %get-tuple-element.35.tok_ref, ...), custom_call_target="tpu_custom_call" | custom-call | flops 8999999488 | bytes 50000000 | tf_op jit(solution)/shard_map/attn_bwd/pallas_call | solution.py:769
  197.7 0.0 copy-start.3
  197.7 0.0 copy-start.4
  197.8 0.8 slice.13
  198.5 0.7 slice.14
  199.2 0.7 fusion
  199.9 0.0 copy-done
  199.9 0.0 copy-start.5
  199.9 0.0 copy-start.2
  199.9 0.0 copy-start.1
  199.9 2.5 %pad_maximum_fusion = bf16[4,8,64,320]{3,2,1,0:T(8,128)(2,1)} fusion(bf16[4,3,64,320]{3,2,1,0:T(8,128)(2,1)} %get-tuple-element.56, bf16[4,5,64,320]{3,2,1,0:T(8,128)(2,1)S(1)} %copy-done), kind=kLoop, calls=%fused_computation | loop fusion | flops 655360 | bytes 2621440 | tf_op jit(solution)/shard_map/concatenate | solution.py:779
  202.5 0.0 copy-done.3
  202.5 1.0 copy.23
  203.5 0.0 copy-done.4
  203.5 0.6 slice.12
  204.1 0.1 reshape.97
  204.2 0.6 dynamic_slice.7
  204.8 0.0 copy-done.5
  204.8 0.6 copy.27
  205.4 0.0 copy-done.2
  205.4 0.7 copy.28
  206.1 0.0 copy-done.1
  206.1 0.7 copy.29
  (3 shorter events, 0.0 us)
Async XLA Ops:
  111.2 88.7 %copy-start = (bf16[4,5,64,320]{3,2,1,0:T(8,128)(2,1)S(1)}, bf16[4,5,64,320]{3,2,1,0:T(8,128)(2,1)}, u32[]{:S(2)}) copy-start(bf16[4,5,64,320]{3,2,1,0:T(8,128)(2,1)} %get-tuple-element.43) | copy-start | bytes 2457604
  197.7 4.7 %copy-start.3 = (f32[40,960]{1,0:T(8,128)S(1)}, f32[40,960]{1,0:T(8,128)}, u32[]{:S(2)}) copy-start(f32[40,960]{1,0:T(8,128)} %get-tuple-element.58) | copy-start | bytes 460804
  197.7 5.7 %copy-start.4 = (f32[64,384]{1,0:T(8,128)S(1)}, f32[64,384]{1,0:T(8,128)}, u32[]{:S(2)}) copy-start(f32[64,384]{1,0:T(8,128)} %get-tuple-element.57) | copy-start | bytes 294916
  199.9 4.9 %copy-start.5 = (f32[40,320]{1,0:T(8,128)S(1)}, f32[40,320]{1,0:T(8,128)}, u32[]{:S(2)}) copy-start(f32[40,320]{1,0:T(8,128)} %get-tuple-element.84) | copy-start | bytes 153604
  199.9 5.5 %copy-start.2 = (f32[40,1280]{1,0:T(8,128)S(1)}, f32[40,1280]{1,0:T(8,128)}, u32[]{:S(2)}) copy-start(f32[40,1280]{1,0:T(8,128)} %get-tuple-element.85) | copy-start | bytes 614404
  199.9 6.2 %copy-start.1 = (f32[160,320]{1,0:T(8,128)S(1)}, f32[160,320]{1,0:T(8,128)}, u32[]{:S(2)}) copy-start(f32[160,320]{1,0:T(8,128)} %get-tuple-element.87) | copy-start | bytes 614404

commit v5 on v4

--- a/solution.py
+++ b/solution.py
@@ -81,15 +81,18 @@
         dst_ref[t] = part
 
 
-def head_rows(tile, slot):
-    row = lax.broadcasted_iota(jnp.int32, tile.shape, 0)
-    return jnp.where(row // HEAD_DIM == slot, tile, jnp.zeros_like(tile))
+def head_rows(ref, hd):
+    slot = hd % HEADS_PER_TILE
+    rows = ref[hd * HEAD_DIM:(hd + 1) * HEAD_DIM, :]
+    before, after = slot * HEAD_DIM, LANES - (slot + 1) * HEAD_DIM
+    parts = [jnp.zeros((before, SEQ), BF)] * (before > 0) + [rows] + [jnp.zeros((after, SEQ), BF)] * (after > 0)
+    return stack_rows(parts)
 
 
 def pipeline(n, stages):
     held = {}
     for turn in range(n + len(stages) - 1):
-        for j in reversed(range(len(stages))):
+        for j in range(len(stages)):
             i = turn - j
             if 0 <= i < n:
                 held[i] = stages[j](held[i], i) if j else stages[j](i)
@@ -282,8 +285,7 @@
     bias[...] = key_bias(me, cp_size, seq_loc, length)
 
     def scores(hd):
-        tile, slot = hd // HEADS_PER_TILE, hd % HEADS_PER_TILE
-        return dot(k_tm[tile], head_rows(q_pad[tile * LANES:(tile + 1) * LANES, :], slot))
+        return dot(k_tm[hd // HEADS_PER_TILE], head_rows(q_pad, hd))
 
     def weights(s, hd):
         s = s + wide(bias[...])
@@ -473,9 +475,8 @@
     bias[...] = key_bias(me, cp_size, seq_loc, length)
 
     def products(hd):
-        tile, slot = hd // HEADS_PER_TILE, hd % HEADS_PER_TILE
-        t0 = slice(tile * LANES, (tile + 1) * LANES)
-        return dot(k_tm[tile], head_rows(q_pad[t0, :], slot)), dot(v_tm[tile], head_rows(do_pad[t0, :], slot))
+        tile = hd // HEADS_PER_TILE
+        return dot(k_tm[tile], head_rows(q_pad, hd)), dot(v_tm[tile], head_rows(do_pad, hd))
 
     def weights(pair, hd):
         s, dp = pair

time: 207 us -> 181 us (0.87)
  Pallas kernels: 191 us -> 165 us
    pallas_call x1, Pallas kernels: 69.1 us -> 48.6 us  [local_step(): call(functools.partial(attn_fwd_kernel, n_seq, cp_size, seq_loc, n_arr),...]
    pallas_call x1, Pallas kernels: 86.5 us -> 80.5 us  [local_step(): call(functools.partial(attn_bwd_kernel, n_seq, cp_size, seq_loc), n_seq,...]
where the time goes in v5:
time: 181 us; the launch traced here: 180 us
  Pallas kernels  165 us (91%)
  local copies, waits for them, and re-layouts  9.84 us (5%)
  other arithmetic  5.27 us (3%)
    pallas_call x1, Pallas kernels, local_step(): call(functools.partial(attn_bwd_kernel, n_seq, cp_size, seq_loc), n_seq,...  80.5 us
    pallas_call x1, Pallas kernels, local_step(): call(functools.partial(attn_fwd_kernel, n_seq, cp_size, seq_loc, n_arr),...  48.6 us
    pallas_call x1, Pallas kernels, local_step(): call(functools.partial(ffn_kernel, n_seq, cp_size, seq_loc), n_seq, [per_...  35.4 us

profile of v5, /device:TPU:0, one launch (start us, length us, event | category | flops | bytes accessed | tf_op | source)
XLA Modules:
  0.0 180.3 jit_solution(16878296915804439794)
XLA Ops:
  0.7 0.7 multiply_sine_fusion
  1.4 0.9 copy.21
  2.3 0.7 pad_bitcast_fusion.emb_ref
  2.9 1.7 copy.22.refs_1_
  4.6 0.8 reshape.89
  5.4 1.3 select_maximum_fusion.refs_0_
  6.7 48.6 %attn_fwd.1 = (f32[8,16,128]{2,1,0:T(8,128)}, bf16[8,40,320]{2,1,0:T(8,128)(2,1)}, bf16[8,40,1280]{2,1,0:T(8,128)(2,1)}, bf16[8,160,320]{2,1,0:T(8,128)(2,1)}, s...) custom-call(s32[32]{0:T(128)} %len_ref.3, ...), custom_call_target="tpu_custom_call" | custom-call | flops 8999999488 | bytes 50000000 | tf_op jit(solution)/shard_map/attn_fwd/pallas_call | solution.py:743
  55.3 35.4 %ffn.1 = (bf16[4,5,64,320]{3,2,1,0:T(8,128)(2,1)}, bf16[3,256,320]{2,1,0:T(8,128)(2,1)}, f32[8,320,256]{2,1,0:T(8,128)}, f32[8,320,256]{2,1,0:T(8,128)}, f32[128...) custom-call(s32[8,1,256]{2,1,0:T(1,128)} %get-tuple-element.35.tok_ref, ...), custom_call_target="tpu_custom_call" | custom-call | flops 8999999488 | bytes 50000000 | tf_op jit(solution)/shard_map/ffn/pallas_call | solution.py:754
  90.7 0.0 copy-start
  90.7 80.5 %attn_bwd.1 = (f32[160,320]{1,0:T(8,128)}, f32[40,1280]{1,0:T(8,128)}, f32[40,320]{1,0:T(8,128)}, f32[40,960]{1,0:T(8,128)}, f32[64,384]{1,0:T(8,128)}, /*index=5*/bf16[4,3,64,320]{3,2,1,0:T(8,128)(2,1)}) custom-call(s32[32]{0:T(128)} %len_ref.3, s32[1]{0:T(128)} %bitcast.4.me_ref, s32[8,1,256]{2,1,0:T(1,128)} %get-tuple-element.35.tok_ref, ...), custom_call_target="tpu_custom_call" | custom-call | flops 8999999488 | bytes 50000000 | tf_op jit(solution)/shard_map/attn_bwd/pallas_call | solution.py:770
  171.2 0.0 copy-start.3
  171.2 0.0 copy-start.4
  171.3 0.8 slice.13
  172.0 0.7 slice.14
  172.7 0.7 fusion
  173.4 0.0 copy-done
  173.4 0.0 copy-start.5
  173.4 0.0 copy-start.2
  173.4 0.0 copy-start.1
  173.4 2.5 %pad_maximum_fusion = bf16[4,8,64,320]{3,2,1,0:T(8,128)(2,1)} fusion(bf16[4,3,64,320]{3,2,1,0:T(8,128)(2,1)} %get-tuple-element.56, bf16[4,5,64,320]{3,2,1,0:T(8,128)(2,1)S(1)} %copy-done), kind=kLoop, calls=%fused_computation | loop fusion | flops 655360 | bytes 2621440 | tf_op jit(solution)/shard_map/concatenate | solution.py:780
  176.0 0.0 copy-done.3
  176.0 1.0 copy.23
  177.0 0.0 copy-done.4
  177.0 0.6 slice.12
  177.6 0.1 reshape.97
  177.7 0.6 dynamic_slice.7
  178.3 0.0 copy-done.5
  178.3 0.6 copy.27
  178.9 0.0 copy-done.2
  178.9 0.7 copy.28
  179.6 0.0 copy-done.1
  179.6 0.7 copy.29
  (3 shorter events, 0.0 us)
Async XLA Ops:
  90.7 82.7 %copy-start = (bf16[4,5,64,320]{3,2,1,0:T(8,128)(2,1)S(1)}, bf16[4,5,64,320]{3,2,1,0:T(8,128)(2,1)}, u32[]{:S(2)}) copy-start(bf16[4,5,64,320]{3,2,1,0:T(8,128)(2,1)} %get-tuple-element.43) | copy-start | bytes 2457604
  171.2 4.7 %copy-start.3 = (f32[40,960]{1,0:T(8,128)S(1)}, f32[40,960]{1,0:T(8,128)}, u32[]{:S(2)}) copy-start(f32[40,960]{1,0:T(8,128)} %get-tuple-element.58) | copy-start | bytes 460804
  171.2 5.7 %copy-start.4 = (f32[64,384]{1,0:T(8,128)S(1)}, f32[64,384]{1,0:T(8,128)}, u32[]{:S(2)}) copy-start(f32[64,384]{1,0:T(8,128)} %get-tuple-element.57) | copy-start | bytes 294916
  173.4 4.9 %copy-start.5 = (f32[40,320]{1,0:T(8,128)S(1)}, f32[40,320]{1,0:T(8,128)}, u32[]{:S(2)}) copy-start(f32[40,320]{1,0:T(8,128)} %get-tuple-element.84) | copy-start | bytes 153604
  173.4 5.5 %copy-start.2 = (f32[40,1280]{1,0:T(8,128)S(1)}, f32[40,1280]{1,0:T(8,128)}, u32[]{:S(2)}) copy-start(f32[40,1280]{1,0:T(8,128)} %get-tuple-element.85) | copy-start | bytes 614404
  173.4 6.2 %copy-start.1 = (f32[160,320]{1,0:T(8,128)S(1)}, f32[160,320]{1,0:T(8,128)}, u32[]{:S(2)}) copy-start(f32[160,320]{1,0:T(8,128)} %get-tuple-element.87) | copy-start | bytes 614404

commit v6 on v5

--- a/solution.py
+++ b/solution.py
@@ -448,7 +448,7 @@
         summer.enter()
         for copy in leaving:
             copy.start()
-        for i in (0, 1):
+        for i in FFN_STREAMS:
             summer.start(0, i)
         acc_qa[...] = jnp.zeros_like(acc_qa)
         acc_qb[...] = jnp.zeros_like(acc_qb)
@@ -461,7 +461,7 @@
     for phase, at in enumerate(PHASE_STEPS):
         @pl.when(step == at)
         def _(phase=phase):
-            for i in (0, 1):
+            for i in FFN_STREAMS:
                 summer.finish(phase, i)
                 summer.start(phase + 1, i)
 
@@ -517,8 +517,11 @@
 
     @pl.when(step == n_steps - 1)
     def _():
-        for i in (2, 3):
+        for i in QKV_STREAMS:
             summer.start(0, i)
+        for i in FFN_STREAMS:
+            summer.finish(3, i)
+            summer.start(4, i)
         rows = [row_sum(pad_rows(acc_vec[j])) for j in range(2)] + [row_sum(pad_rows(acc_b[j])) for j in range(3)]
         small = summer.small
         small[...] = jnp.zeros_like(small)
@@ -527,14 +530,14 @@
         small[EMB_ROWS + 8:EMB_ROWS + 16] = dvec2_ref[...]
         summer.start_small(0)
         for phase in range(5):
-            for i in (2, 3):
+            for i in QKV_STREAMS:
                 summer.finish(phase, i)
                 if phase < 4:
                     summer.start(phase + 1, i)
             summer.finish_small(phase)
             if phase < 4:
                 summer.start_small(phase + 1)
-        for i in (0, 1):
+        for i in FFN_STREAMS:
             summer.finish(4, i)
         rup_ref[...] = ruo_ref[:, :F]
         rout_ref[...] = ruo_ref[:, F:F + D]
@@ -547,7 +550,9 @@
 MESH = pl.DeviceIdType.MESH
 EMB_ROWS = 40
 SMALL_ROWS = 64
-PHASE_STEPS = (1, 3, 4, 7)
+PHASE_STEPS = (1, 4, 5)
+FFN_STREAMS = (0, 1)
+QKV_STREAMS = (2, 3)
 STREAMS = (('xy', (0, 40, 40)), ('yx', (1, 512, 384)), ('xy', (1, 128, 128)), ('yx', (1, 128, 128)))
 SMALL_SPEC = (0, SMALL_ROWS // 4, SMALL_ROWS // 4)
 

time: 181 us -> 181 us (level)
  no operation moved by 1% of the time
where the time goes in v6:
time: 181 us; the launch traced here: 180 us
  Pallas kernels  164 us (91%)
  local copies, waits for them, and re-layouts  9.84 us (5%)
  other arithmetic  5.27 us (3%)
    pallas_call x1, Pallas kernels, local_step(): call(functools.partial(attn_bwd_kernel, n_seq, cp_size, seq_loc), n_seq,...  80.3 us
    pallas_call x1, Pallas kernels, local_step(): call(functools.partial(attn_fwd_kernel, n_seq, cp_size, seq_loc, n_arr),...  48.6 us
    pallas_call x1, Pallas kernels, local_step(): call(functools.partial(ffn_kernel, n_seq, cp_size, seq_loc), n_seq, [per_...  35.4 us

profile of v6, /device:TPU:0, one launch (start us, length us, event | category | flops | bytes accessed | tf_op | source)
XLA Modules:
  0.0 180.1 jit_solution(16364401505184055817)
XLA Ops:
  0.7 0.7 multiply_sine_fusion
  1.4 0.9 copy.21
  2.3 0.7 pad_bitcast_fusion.emb_ref
  2.9 1.7 copy.22.refs_1_
  4.6 0.8 reshape.89
  5.4 1.3 select_maximum_fusion.refs_0_
  6.7 48.6 %attn_fwd.1 = (f32[8,16,128]{2,1,0:T(8,128)}, bf16[8,40,320]{2,1,0:T(8,128)(2,1)}, bf16[8,40,1280]{2,1,0:T(8,128)(2,1)}, bf16[8,160,320]{2,1,0:T(8,128)(2,1)}, s...) custom-call(s32[32]{0:T(128)} %len_ref.3, ...), custom_call_target="tpu_custom_call" | custom-call | flops 8999999488 | bytes 50000000 | tf_op jit(solution)/shard_map/attn_fwd/pallas_call | solution.py:748
  55.3 35.4 %ffn.1 = (bf16[4,5,64,320]{3,2,1,0:T(8,128)(2,1)}, bf16[3,256,320]{2,1,0:T(8,128)(2,1)}, f32[8,320,256]{2,1,0:T(8,128)}, f32[8,320,256]{2,1,0:T(8,128)}, f32[128...) custom-call(s32[8,1,256]{2,1,0:T(1,128)} %get-tuple-element.35.tok_ref, ...), custom_call_target="tpu_custom_call" | custom-call | flops 8999999488 | bytes 50000000 | tf_op jit(solution)/shard_map/ffn/pallas_call | solution.py:759
  90.7 0.0 copy-start
  90.7 80.3 %attn_bwd.1 = (f32[160,320]{1,0:T(8,128)}, f32[40,1280]{1,0:T(8,128)}, f32[40,320]{1,0:T(8,128)}, f32[40,960]{1,0:T(8,128)}, f32[64,384]{1,0:T(8,128)}, /*index=5*/bf16[4,3,64,320]{3,2,1,0:T(8,128)(2,1)}) custom-call(s32[32]{0:T(128)} %len_ref.3, s32[1]{0:T(128)} %bitcast.4.me_ref, s32[8,1,256]{2,1,0:T(1,128)} %get-tuple-element.35.tok_ref, ...), custom_call_target="tpu_custom_call" | custom-call | flops 8999999488 | bytes 50000000 | tf_op jit(solution)/shard_map/attn_bwd/pallas_call | solution.py:775
  171.0 0.0 copy-start.3
  171.1 0.0 copy-start.4
  171.1 0.8 slice.13
  171.8 0.7 slice.14
  172.6 0.7 fusion
  173.2 0.0 copy-done
  173.2 0.0 copy-start.5
  173.2 0.0 copy-start.2
  173.2 0.0 copy-start.1
  173.2 2.5 %pad_maximum_fusion = bf16[4,8,64,320]{3,2,1,0:T(8,128)(2,1)} fusion(bf16[4,3,64,320]{3,2,1,0:T(8,128)(2,1)} %get-tuple-element.56, bf16[4,5,64,320]{3,2,1,0:T(8,128)(2,1)S(1)} %copy-done), kind=kLoop, calls=%fused_computation | loop fusion | flops 655360 | bytes 2621440 | tf_op jit(solution)/shard_map/concatenate | solution.py:785
  175.8 0.0 copy-done.3
  175.8 1.0 copy.23
  176.8 0.0 copy-done.4
  176.8 0.6 slice.12
  177.4 0.1 reshape.97
  177.5 0.6 dynamic_slice.7
  178.1 0.0 copy-done.5
  178.1 0.6 copy.27
  178.7 0.0 copy-done.2
  178.8 0.7 copy.28
  179.4 0.0 copy-done.1
  179.4 0.7 copy.29
  (3 shorter events, 0.0 us)
Async XLA Ops:
  90.7 82.5 %copy-start = (bf16[4,5,64,320]{3,2,1,0:T(8,128)(2,1)S(1)}, bf16[4,5,64,320]{3,2,1,0:T(8,128)(2,1)}, u32[]{:S(2)}) copy-start(bf16[4,5,64,320]{3,2,1,0:T(8,128)(2,1)} %get-tuple-element.43) | copy-start | bytes 2457604
  171.0 4.7 %copy-start.3 = (f32[40,960]{1,0:T(8,128)S(1)}, f32[40,960]{1,0:T(8,128)}, u32[]{:S(2)}) copy-start(f32[40,960]{1,0:T(8,128)} %get-tuple-element.58) | copy-start | bytes 460804
  171.1 5.7 %copy-start.4 = (f32[64,384]{1,0:T(8,128)S(1)}, f32[64,384]{1,0:T(8,128)}, u32[]{:S(2)}) copy-start(f32[64,384]{1,0:T(8,128)} %get-tuple-element.57) | copy-start | bytes 294916
  173.2 4.9 %copy-start.5 = (f32[40,320]{1,0:T(8,128)S(1)}, f32[40,320]{1,0:T(8,128)}, u32[]{:S(2)}) copy-start(f32[40,320]{1,0:T(8,128)} %get-tuple-element.84) | copy-start | bytes 153604
  173.2 5.5 %copy-start.2 = (f32[40,1280]{1,0:T(8,128)S(1)}, f32[40,1280]{1,0:T(8,128)}, u32[]{:S(2)}) copy-start(f32[40,1280]{1,0:T(8,128)} %get-tuple-element.85) | copy-start | bytes 614404
  173.2 6.2 %copy-start.1 = (f32[160,320]{1,0:T(8,128)S(1)}, f32[160,320]{1,0:T(8,128)}, u32[]{:S(2)}) copy-start(f32[160,320]{1,0:T(8,128)} %get-tuple-element.87) | copy-start | bytes 614404
